TPU v7x, 256 devices: a whole 4x4x8 slice. The times are simulated.
256 devices in a mesh: rows: 128 (over y, x, z_lo, core), cols: 2 (over z_hi).
Axes of the slice: x: 4, y: 4, z: 8 (z_hi: 2, z_lo: 4; z = z_hi * 4 + z_lo), core: 2. Of those that a mesh axis runs over, the one named last changes fastest.
Arguments:
- eigvecs: float32 [32768, 2048], P('rows', 'cols'), may hold values from -6 to 6
- reflectors: float32 [32, 32768], P('cols', 'rows'), may hold values from -17 to 17
- starts: int32 [32], replicated, may hold values from 0 to 63
Outputs:
- rotated: float32 [32768, 2048], P('rows', 'cols')
Inputs may be any that keep to these rules, and one draw needn't show every extreme that they name: Sweep j's windows begin at rows starts[j] + k * 64.
All inputs are finite; a program needn't handle non-finite values.
Results may differ from a plain program's by a relative error of at most 0.00011.
Values sent between devices are 32-bit elements; how exact they have to be, the bound alone decides.
No kernel may reach another device: no remote copies, remote signals or barrier semaphores. Data moves between devices by JAX's collectives and lax.ppermute only.
A program may use at most 64 MiB of HBM per device.

v0:
```python
import jax
import jax.numpy as jnp
from jax import lax
from jax.sharding import PartitionSpec as P

BAND = 64
SWEEPS = 32


group_depth = 2


def with_halo(block, sides, width):
    for axis, dim in sides:
        count = lax.axis_size(axis)
        forward = [(i, i + 1) for i in range(count - 1)]
        backward = [(target, source) for source, target in forward]
        low = lax.ppermute(
            lax.slice_in_dim(block, block.shape[dim] - width, None, axis=dim), axis, forward
        )
        high = lax.ppermute(lax.slice_in_dim(block, 0, width, axis=dim), axis, backward)
        block = jnp.concatenate([low, block, high], axis=dim)
    return block


def frame_windows(framed, framed_v, offset, frame_start, count, total_rows):
    frame_rows = framed.shape[0]
    local_row = jnp.arange(frame_rows, dtype=jnp.int32)
    segment = jnp.where(local_row >= offset, jnp.floor_divide(local_row - offset, BAND), -1)
    onehot = (segment[None, :] == jnp.arange(count, dtype=jnp.int32)[:, None]).astype(jnp.float32)
    partial_value = jnp.dot(onehot * framed_v[None, :], framed, precision=lax.Precision.HIGHEST)
    squares = jnp.dot(onehot, framed_v * framed_v, precision=lax.Precision.HIGHEST)
    starts_at = frame_start + offset + jnp.arange(count, dtype=jnp.int32) * BAND
    usable = (starts_at >= 0) & (starts_at + BAND <= total_rows)
    scaled = jnp.where(usable, 2.0 / jnp.where(usable, squares, 1.0), 0.0)
    return (onehot, scaled[:, None] * partial_value)


def chase_windows(framed, framed_v, offset, frame_start, count, total_rows):
    onehot, coeffs = frame_windows(framed, framed_v, offset, frame_start, count, total_rows)
    update = lax.dot_general(
        onehot, coeffs, (((0,), (0,)), ((), ())), precision=lax.Precision.HIGHEST
    )
    return framed - framed_v[:, None] * update


def per_device(eigvecs, reflectors, starts):
    every_sweep = lax.all_gather(reflectors, "cols", axis=0, tiled=True)
    slab_rows = eigvecs.shape[0]
    total_rows = slab_rows * lax.axis_size("rows")
    first_row = lax.axis_index("rows") * slab_rows
    margin = group_depth * BAND
    deep_all = with_halo(every_sweep, (("rows", 1),), margin)
    count = slab_rows // BAND + 2 * group_depth - 1

    def advance_group(group_idx, vectors):
        framed = with_halo(vectors, (("rows", 0),), margin)
        for inner in range(group_depth):
            sweep_idx = group_idx * group_depth + inner
            framed = chase_windows(
                framed,
                deep_all[sweep_idx],
                starts[sweep_idx],
                first_row - margin,
                count,
                total_rows,
            )
        return framed[margin : margin + slab_rows]

    return lax.fori_loop(0, SWEEPS // group_depth, advance_group, eigvecs)


def solution(mesh):
    in_specs = (P("rows", "cols"), P("cols", "rows"), P())
    out_specs = P("rows", "cols")
    return jax.shard_map(
        per_device, mesh=mesh, in_specs=in_specs, out_specs=out_specs, check_vma=False
    )
```

profile of v0, /device:TPU:8, one launch (start us, length us, event | category | flops | bytes accessed | tf_op | source)
XLA Modules:
  0.0 414.7 jit_solution(7386933851411315530)
XLA Ops:
  0.8 9.5 %all_gather.3 = f32[32,256]{1,0:T(8,128)S(1)} all-gather(f32[16,256]{1,0:T(8,128)S(1)} %copy-done.3), channel_id=1, replica_groups=mesh['rows'=128,'cols'=2] {'cols'}, dimensions={0}, use_global_device_ids=true | all-gather | bytes 49152 | tf_op jit(solution)/shard_map/all_gather | solution.py:48
  10.4 5.6 %collective-permute-start.3 = (f32[32,128]{1,0:T(8,128)S(1)}, f32[32,128]{1,0:T(8,128)S(1)}, u32[]{:S(2)}, u32[]{:S(2)}) collective-permute-start(f32[32,128]{1,0:T(8,128)S(1)} %get-tuple-element.184), channel_id=1, source_target_pairs={{2,0},{4,2},{6,4},{8,6},{10,8},{12,10},{14,12},{16,14},{18,16},{20... | collective-permute-start | bytes 49160 | tf_op jit(solution)/shard_map/ppermute | solution.py:21
  16.0 1.9 collective-permute-start.2
  18.0 7.9 %collective-permute-done.2 = f32[32,128]{1,0:T(8,128)S(1)} collective-permute-done((f32[32,128]{1,0:T(8,128)S(1)}, f32[32,128]{1,0:T(8,128)S(1)}, u32[]{:S(2)}, u32[]{:S(2)}) %collective-permute-start.2) | collective-permute-done | bytes 16416 | tf_op jit(solution)/shard_map/ppermute | solution.py:18
  25.9 387.8 %while.16 = (s32[]{:T(128)}, f32[256,1024]{1,0:T(8,128)S(1)}, f32[32,512]{1,0:T(8,128)S(1)}, s32[32]{0:T(128)S(1)}, s32[]{:T(128)}, /*index=5*/s32[]{:T(128)}, s32[]{:T(128)}, s32[]{:T(128)}, s32[]{:T(128)}, s32[]{:T(128)}) while((s32[]{:T(128)}, f32[256,1024]{1,0:T(8,128)S(1)}, f32[32,512]{1,0:T(8,128)S(1)}, s32[32]{0:T(128)S(1)}, s32[]{:T(128)}, ...), condition=%wide.region_1.2_spmd, body=%wide.region_0.1_spmd.sunk | while | flops 177882240 | bytes 24282568 | solution.py:70
  26.0 1.9 collective-permute-start
  27.9 8.4 %collective-permute-start.1 = (f32[128,1024]{1,0:T(8,128)S(1)}, f32[128,1024]{1,0:T(8,128)S(1)}, u32[]{:S(2)}, u32[]{:S(2)}) collective-permute-start(f32[128,1024]{1,0:T(8,128)S(1)} %get-tuple-element.223), channel_id=1, source_target_pairs={{2,0},{4,2},{6,4},{8,6},{10,8},{12,10},{14,12},{16,14},{18,16},{20... | collective-permute-start | bytes 1572872 | tf_op jit(solution)/shard_map/while/body/eval_jaxpr/ppermute | solution.py:21
  39.8 2.7 collective-permute-done
  42.6 2.3 collective-permute-done.1
  49.8 1.9 collective-permute-start
  51.7 8.6 %collective-permute-start.1 = (f32[128,1024]{1,0:T(8,128)S(1)}, f32[128,1024]{1,0:T(8,128)S(1)}, u32[]{:S(2)}, u32[]{:S(2)}) collective-permute-start(f32[128,1024]{1,0:T(8,128)S(1)} %get-tuple-element.223), channel_id=1, source_target_pairs={{2,0},{4,2},{6,4},{8,6},{10,8},{12,10},{14,12},{16,14},{18,16},{20... | collective-permute-start | bytes 1572872 | tf_op jit(solution)/shard_map/while/body/eval_jaxpr/ppermute | solution.py:21
  63.7 4.5 %collective-permute-done = f32[128,1024]{1,0:T(8,128)S(1)} collective-permute-done((f32[128,1024]{1,0:T(8,128)S(1)}, f32[128,1024]{1,0:T(8,128)S(1)}, u32[]{:S(2)}, u32[]{:S(2)}) %collective-permute-start) | collective-permute-done | bytes 524320 | tf_op jit(solution)/shard_map/while/body/eval_jaxpr/ppermute | solution.py:18
  74.1 1.9 collective-permute-start
  76.1 8.6 %collective-permute-start.1 = (f32[128,1024]{1,0:T(8,128)S(1)}, f32[128,1024]{1,0:T(8,128)S(1)}, u32[]{:S(2)}, u32[]{:S(2)}) collective-permute-start(f32[128,1024]{1,0:T(8,128)S(1)} %get-tuple-element.223), channel_id=1, source_target_pairs={{2,0},{4,2},{6,4},{8,6},{10,8},{12,10},{14,12},{16,14},{18,16},{20... | collective-permute-start | bytes 1572872 | tf_op jit(solution)/shard_map/while/body/eval_jaxpr/ppermute | solution.py:21
  88.1 4.6 %collective-permute-done = f32[128,1024]{1,0:T(8,128)S(1)} collective-permute-done((f32[128,1024]{1,0:T(8,128)S(1)}, f32[128,1024]{1,0:T(8,128)S(1)}, u32[]{:S(2)}, u32[]{:S(2)}) %collective-permute-start) | collective-permute-done | bytes 524320 | tf_op jit(solution)/shard_map/while/body/eval_jaxpr/ppermute | solution.py:18
  98.4 1.9 collective-permute-start
  100.3 8.6 %collective-permute-start.1 = (f32[128,1024]{1,0:T(8,128)S(1)}, f32[128,1024]{1,0:T(8,128)S(1)}, u32[]{:S(2)}, u32[]{:S(2)}) collective-permute-start(f32[128,1024]{1,0:T(8,128)S(1)} %get-tuple-element.223), channel_id=1, source_target_pairs={{2,0},{4,2},{6,4},{8,6},{10,8},{12,10},{14,12},{16,14},{18,16},{20... | collective-permute-start | bytes 1572872 | tf_op jit(solution)/shard_map/while/body/eval_jaxpr/ppermute | solution.py:21
  112.3 4.6 %collective-permute-done = f32[128,1024]{1,0:T(8,128)S(1)} collective-permute-done((f32[128,1024]{1,0:T(8,128)S(1)}, f32[128,1024]{1,0:T(8,128)S(1)}, u32[]{:S(2)}, u32[]{:S(2)}) %collective-permute-start) | collective-permute-done | bytes 524320 | tf_op jit(solution)/shard_map/while/body/eval_jaxpr/ppermute | solution.py:18
  122.8 1.9 collective-permute-start
  124.7 8.6 %collective-permute-start.1 = (f32[128,1024]{1,0:T(8,128)S(1)}, f32[128,1024]{1,0:T(8,128)S(1)}, u32[]{:S(2)}, u32[]{:S(2)}) collective-permute-start(f32[128,1024]{1,0:T(8,128)S(1)} %get-tuple-element.223), channel_id=1, source_target_pairs={{2,0},{4,2},{6,4},{8,6},{10,8},{12,10},{14,12},{16,14},{18,16},{20... | collective-permute-start | bytes 1572872 | tf_op jit(solution)/shard_map/while/body/eval_jaxpr/ppermute | solution.py:21
  136.7 4.6 %collective-permute-done = f32[128,1024]{1,0:T(8,128)S(1)} collective-permute-done((f32[128,1024]{1,0:T(8,128)S(1)}, f32[128,1024]{1,0:T(8,128)S(1)}, u32[]{:S(2)}, u32[]{:S(2)}) %collective-permute-start) | collective-permute-done | bytes 524320 | tf_op jit(solution)/shard_map/while/body/eval_jaxpr/ppermute | solution.py:18
  147.1 1.9 collective-permute-start
  149.1 8.6 %collective-permute-start.1 = (f32[128,1024]{1,0:T(8,128)S(1)}, f32[128,1024]{1,0:T(8,128)S(1)}, u32[]{:S(2)}, u32[]{:S(2)}) collective-permute-start(f32[128,1024]{1,0:T(8,128)S(1)} %get-tuple-element.223), channel_id=1, source_target_pairs={{2,0},{4,2},{6,4},{8,6},{10,8},{12,10},{14,12},{16,14},{18,16},{20... | collective-permute-start | bytes 1572872 | tf_op jit(solution)/shard_map/while/body/eval_jaxpr/ppermute | solution.py:21
  161.1 4.6 %collective-permute-done = f32[128,1024]{1,0:T(8,128)S(1)} collective-permute-done((f32[128,1024]{1,0:T(8,128)S(1)}, f32[128,1024]{1,0:T(8,128)S(1)}, u32[]{:S(2)}, u32[]{:S(2)}) %collective-permute-start) | collective-permute-done | bytes 524320 | tf_op jit(solution)/shard_map/while/body/eval_jaxpr/ppermute | solution.py:18
  171.5 1.9 collective-permute-start
  173.4 8.6 %collective-permute-start.1 = (f32[128,1024]{1,0:T(8,128)S(1)}, f32[128,1024]{1,0:T(8,128)S(1)}, u32[]{:S(2)}, u32[]{:S(2)}) collective-permute-start(f32[128,1024]{1,0:T(8,128)S(1)} %get-tuple-element.223), channel_id=1, source_target_pairs={{2,0},{4,2},{6,4},{8,6},{10,8},{12,10},{14,12},{16,14},{18,16},{20... | collective-permute-start | bytes 1572872 | tf_op jit(solution)/shard_map/while/body/eval_jaxpr/ppermute | solution.py:21
  185.5 4.6 %collective-permute-done = f32[128,1024]{1,0:T(8,128)S(1)} collective-permute-done((f32[128,1024]{1,0:T(8,128)S(1)}, f32[128,1024]{1,0:T(8,128)S(1)}, u32[]{:S(2)}, u32[]{:S(2)}) %collective-permute-start) | collective-permute-done | bytes 524320 | tf_op jit(solution)/shard_map/while/body/eval_jaxpr/ppermute | solution.py:18
  195.9 1.9 collective-permute-start
  197.8 8.6 %collective-permute-start.1 = (f32[128,1024]{1,0:T(8,128)S(1)}, f32[128,1024]{1,0:T(8,128)S(1)}, u32[]{:S(2)}, u32[]{:S(2)}) collective-permute-start(f32[128,1024]{1,0:T(8,128)S(1)} %get-tuple-element.223), channel_id=1, source_target_pairs={{2,0},{4,2},{6,4},{8,6},{10,8},{12,10},{14,12},{16,14},{18,16},{20... | collective-permute-start | bytes 1572872 | tf_op jit(solution)/shard_map/while/body/eval_jaxpr/ppermute | solution.py:21
  209.8 4.6 %collective-permute-done = f32[128,1024]{1,0:T(8,128)S(1)} collective-permute-done((f32[128,1024]{1,0:T(8,128)S(1)}, f32[128,1024]{1,0:T(8,128)S(1)}, u32[]{:S(2)}, u32[]{:S(2)}) %collective-permute-start) | collective-permute-done | bytes 524320 | tf_op jit(solution)/shard_map/while/body/eval_jaxpr/ppermute | solution.py:18
  220.3 1.9 collective-permute-start
  222.2 8.6 %collective-permute-start.1 = (f32[128,1024]{1,0:T(8,128)S(1)}, f32[128,1024]{1,0:T(8,128)S(1)}, u32[]{:S(2)}, u32[]{:S(2)}) collective-permute-start(f32[128,1024]{1,0:T(8,128)S(1)} %get-tuple-element.223), channel_id=1, source_target_pairs={{2,0},{4,2},{6,4},{8,6},{10,8},{12,10},{14,12},{16,14},{18,16},{20... | collective-permute-start | bytes 1572872 | tf_op jit(solution)/shard_map/while/body/eval_jaxpr/ppermute | solution.py:21
  234.2 4.6 %collective-permute-done = f32[128,1024]{1,0:T(8,128)S(1)} collective-permute-done((f32[128,1024]{1,0:T(8,128)S(1)}, f32[128,1024]{1,0:T(8,128)S(1)}, u32[]{:S(2)}, u32[]{:S(2)}) %collective-permute-start) | collective-permute-done | bytes 524320 | tf_op jit(solution)/shard_map/while/body/eval_jaxpr/ppermute | solution.py:18
  246.6 8.6 %collective-permute-start.1 = (f32[128,1024]{1,0:T(8,128)S(1)}, f32[128,1024]{1,0:T(8,128)S(1)}, u32[]{:S(2)}, u32[]{:S(2)}) collective-permute-start(f32[128,1024]{1,0:T(8,128)S(1)} %get-tuple-element.223), channel_id=1, source_target_pairs={{2,0},{4,2},{6,4},{8,6},{10,8},{12,10},{14,12},{16,14},{18,16},{20... | collective-permute-start | bytes 1572872 | tf_op jit(solution)/shard_map/while/body/eval_jaxpr/ppermute | solution.py:21
  258.6 4.6 %collective-permute-done = f32[128,1024]{1,0:T(8,128)S(1)} collective-permute-done((f32[128,1024]{1,0:T(8,128)S(1)}, f32[128,1024]{1,0:T(8,128)S(1)}, u32[]{:S(2)}, u32[]{:S(2)}) %collective-permute-start) | collective-permute-done | bytes 524320 | tf_op jit(solution)/shard_map/while/body/eval_jaxpr/ppermute | solution.py:18
  270.8 8.6 %collective-permute-start.1 = (f32[128,1024]{1,0:T(8,128)S(1)}, f32[128,1024]{1,0:T(8,128)S(1)}, u32[]{:S(2)}, u32[]{:S(2)}) collective-permute-start(f32[128,1024]{1,0:T(8,128)S(1)} %get-tuple-element.223), channel_id=1, source_target_pairs={{2,0},{4,2},{6,4},{8,6},{10,8},{12,10},{14,12},{16,14},{18,16},{20... | collective-permute-start | bytes 1572872 | tf_op jit(solution)/shard_map/while/body/eval_jaxpr/ppermute | solution.py:21
  282.9 4.6 %collective-permute-done = f32[128,1024]{1,0:T(8,128)S(1)} collective-permute-done((f32[128,1024]{1,0:T(8,128)S(1)}, f32[128,1024]{1,0:T(8,128)S(1)}, u32[]{:S(2)}, u32[]{:S(2)}) %collective-permute-start) | collective-permute-done | bytes 524320 | tf_op jit(solution)/shard_map/while/body/eval_jaxpr/ppermute | solution.py:18
  293.2 1.9 collective-permute-start
  295.1 8.6 %collective-permute-start.1 = (f32[128,1024]{1,0:T(8,128)S(1)}, f32[128,1024]{1,0:T(8,128)S(1)}, u32[]{:S(2)}, u32[]{:S(2)}) collective-permute-start(f32[128,1024]{1,0:T(8,128)S(1)} %get-tuple-element.223), channel_id=1, source_target_pairs={{2,0},{4,2},{6,4},{8,6},{10,8},{12,10},{14,12},{16,14},{18,16},{20... | collective-permute-start | bytes 1572872 | tf_op jit(solution)/shard_map/while/body/eval_jaxpr/ppermute | solution.py:21
  307.1 4.6 %collective-permute-done = f32[128,1024]{1,0:T(8,128)S(1)} collective-permute-done((f32[128,1024]{1,0:T(8,128)S(1)}, f32[128,1024]{1,0:T(8,128)S(1)}, u32[]{:S(2)}, u32[]{:S(2)}) %collective-permute-start) | collective-permute-done | bytes 524320 | tf_op jit(solution)/shard_map/while/body/eval_jaxpr/ppermute | solution.py:18
  319.4 8.6 %collective-permute-start.1 = (f32[128,1024]{1,0:T(8,128)S(1)}, f32[128,1024]{1,0:T(8,128)S(1)}, u32[]{:S(2)}, u32[]{:S(2)}) collective-permute-start(f32[128,1024]{1,0:T(8,128)S(1)} %get-tuple-element.223), channel_id=1, source_target_pairs={{2,0},{4,2},{6,4},{8,6},{10,8},{12,10},{14,12},{16,14},{18,16},{20... | collective-permute-start | bytes 1572872 | tf_op jit(solution)/shard_map/while/body/eval_jaxpr/ppermute | solution.py:21
  331.4 4.6 %collective-permute-done = f32[128,1024]{1,0:T(8,128)S(1)} collective-permute-done((f32[128,1024]{1,0:T(8,128)S(1)}, f32[128,1024]{1,0:T(8,128)S(1)}, u32[]{:S(2)}, u32[]{:S(2)}) %collective-permute-start) | collective-permute-done | bytes 524320 | tf_op jit(solution)/shard_map/while/body/eval_jaxpr/ppermute | solution.py:18
  343.7 8.6 %collective-permute-start.1 = (f32[128,1024]{1,0:T(8,128)S(1)}, f32[128,1024]{1,0:T(8,128)S(1)}, u32[]{:S(2)}, u32[]{:S(2)}) collective-permute-start(f32[128,1024]{1,0:T(8,128)S(1)} %get-tuple-element.223), channel_id=1, source_target_pairs={{2,0},{4,2},{6,4},{8,6},{10,8},{12,10},{14,12},{16,14},{18,16},{20... | collective-permute-start | bytes 1572872 | tf_op jit(solution)/shard_map/while/body/eval_jaxpr/ppermute | solution.py:21
  355.7 4.6 %collective-permute-done = f32[128,1024]{1,0:T(8,128)S(1)} collective-permute-done((f32[128,1024]{1,0:T(8,128)S(1)}, f32[128,1024]{1,0:T(8,128)S(1)}, u32[]{:S(2)}, u32[]{:S(2)}) %collective-permute-start) | collective-permute-done | bytes 524320 | tf_op jit(solution)/shard_map/while/body/eval_jaxpr/ppermute | solution.py:18
  367.9 8.6 %collective-permute-start.1 = (f32[128,1024]{1,0:T(8,128)S(1)}, f32[128,1024]{1,0:T(8,128)S(1)}, u32[]{:S(2)}, u32[]{:S(2)}) collective-permute-start(f32[128,1024]{1,0:T(8,128)S(1)} %get-tuple-element.223), channel_id=1, source_target_pairs={{2,0},{4,2},{6,4},{8,6},{10,8},{12,10},{14,12},{16,14},{18,16},{20... | collective-permute-start | bytes 1572872 | tf_op jit(solution)/shard_map/while/body/eval_jaxpr/ppermute | solution.py:21
  380.0 4.6 %collective-permute-done = f32[128,1024]{1,0:T(8,128)S(1)} collective-permute-done((f32[128,1024]{1,0:T(8,128)S(1)}, f32[128,1024]{1,0:T(8,128)S(1)}, u32[]{:S(2)}, u32[]{:S(2)}) %collective-permute-start) | collective-permute-done | bytes 524320 | tf_op jit(solution)/shard_map/while/body/eval_jaxpr/ppermute | solution.py:18
  392.2 8.6 %collective-permute-start.1 = (f32[128,1024]{1,0:T(8,128)S(1)}, f32[128,1024]{1,0:T(8,128)S(1)}, u32[]{:S(2)}, u32[]{:S(2)}) collective-permute-start(f32[128,1024]{1,0:T(8,128)S(1)} %get-tuple-element.223), channel_id=1, source_target_pairs={{2,0},{4,2},{6,4},{8,6},{10,8},{12,10},{14,12},{16,14},{18,16},{20... | collective-permute-start | bytes 1572872 | tf_op jit(solution)/shard_map/while/body/eval_jaxpr/ppermute | solution.py:21
  404.2 4.6 %collective-permute-done = f32[128,1024]{1,0:T(8,128)S(1)} collective-permute-done((f32[128,1024]{1,0:T(8,128)S(1)}, f32[128,1024]{1,0:T(8,128)S(1)}, u32[]{:S(2)}, u32[]{:S(2)}) %collective-permute-start) | collective-permute-done | bytes 524320 | tf_op jit(solution)/shard_map/while/body/eval_jaxpr/ppermute | solution.py:18
  (320 shorter events, 136.8 us)
Async XLA Ops:
  0.0 25.9 %copy-start.1 = (f32[256,1024]{1,0:T(8,128)S(1)}, f32[256,1024]{1,0:T(8,128)}, u32[]{:S(2)}) copy-start(f32[256,1024]{1,0:T(8,128)} %param.5) | copy-start | bytes 3145732
  0.0 0.8 copy-start.3
  0.0 25.9 %copy-start.2 = (s32[32]{0:T(128)S(1)}, s32[32]{0:T(128)}, u32[]{:S(2)}) copy-start(s32[32]{0:T(128)} %param.7) | copy-start | bytes 388
  10.4 7.6 %collective-permute-start.3 = (f32[32,128]{1,0:T(8,128)S(1)}, f32[32,128]{1,0:T(8,128)S(1)}, u32[]{:S(2)}, u32[]{:S(2)}) collective-permute-start(f32[32,128]{1,0:T(8,128)S(1)} %get-tuple-element.184), channel_id=1, source_target_pairs={{2,0},{4,2},{6,4},{8,6},{10,8},{12,10},{14,12},{16,14},{18,16},{20... | collective-permute-start | bytes 49160 | tf_op jit(solution)/shard_map/ppermute | solution.py:21
  16.0 9.9 %collective-permute-start.2 = (f32[32,128]{1,0:T(8,128)S(1)}, f32[32,128]{1,0:T(8,128)S(1)}, u32[]{:S(2)}, u32[]{:S(2)}) collective-permute-start(f32[32,128]{1,0:T(8,128)S(1)} %get-tuple-element.183), channel_id=1, source_target_pairs={{0,2},{2,4},{4,6},{6,8},{8,10},{10,12},{12,14},{14,16},{16,18},{18... | collective-permute-start | bytes 49160 | tf_op jit(solution)/shard_map/ppermute | solution.py:18
  26.0 16.4 %collective-permute-start = (f32[128,1024]{1,0:T(8,128)S(1)}, f32[128,1024]{1,0:T(8,128)S(1)}, u32[]{:S(2)}, u32[]{:S(2)}) collective-permute-start(f32[128,1024]{1,0:T(8,128)S(1)} %get-tuple-element.222), channel_id=1, source_target_pairs={{0,2},{2,4},{4,6},{6,8},{8,10},{10,12},{12,14},{14,16},{16,18},{18... | collective-permute-start | bytes 1572872 | tf_op jit(solution)/shard_map/while/body/eval_jaxpr/ppermute | solution.py:18
  27.9 17.0 %collective-permute-start.1 = (f32[128,1024]{1,0:T(8,128)S(1)}, f32[128,1024]{1,0:T(8,128)S(1)}, u32[]{:S(2)}, u32[]{:S(2)}) collective-permute-start(f32[128,1024]{1,0:T(8,128)S(1)} %get-tuple-element.223), channel_id=1, source_target_pairs={{2,0},{4,2},{6,4},{8,6},{10,8},{12,10},{14,12},{16,14},{18,16},{20... | collective-permute-start | bytes 1572872 | tf_op jit(solution)/shard_map/while/body/eval_jaxpr/ppermute | solution.py:21
  49.8 18.5 %collective-permute-start = (f32[128,1024]{1,0:T(8,128)S(1)}, f32[128,1024]{1,0:T(8,128)S(1)}, u32[]{:S(2)}, u32[]{:S(2)}) collective-permute-start(f32[128,1024]{1,0:T(8,128)S(1)} %get-tuple-element.222), channel_id=1, source_target_pairs={{0,2},{2,4},{4,6},{6,8},{8,10},{10,12},{12,14},{14,16},{16,18},{18... | collective-permute-start | bytes 1572872 | tf_op jit(solution)/shard_map/while/body/eval_jaxpr/ppermute | solution.py:18
  51.7 17.6 %collective-permute-start.1 = (f32[128,1024]{1,0:T(8,128)S(1)}, f32[128,1024]{1,0:T(8,128)S(1)}, u32[]{:S(2)}, u32[]{:S(2)}) collective-permute-start(f32[128,1024]{1,0:T(8,128)S(1)} %get-tuple-element.223), channel_id=1, source_target_pairs={{2,0},{4,2},{6,4},{8,6},{10,8},{12,10},{14,12},{16,14},{18,16},{20... | collective-permute-start | bytes 1572872 | tf_op jit(solution)/shard_map/while/body/eval_jaxpr/ppermute | solution.py:21
  74.1 18.6 %collective-permute-start = (f32[128,1024]{1,0:T(8,128)S(1)}, f32[128,1024]{1,0:T(8,128)S(1)}, u32[]{:S(2)}, u32[]{:S(2)}) collective-permute-start(f32[128,1024]{1,0:T(8,128)S(1)} %get-tuple-element.222), channel_id=1, source_target_pairs={{0,2},{2,4},{4,6},{6,8},{8,10},{10,12},{12,14},{14,16},{16,18},{18... | collective-permute-start | bytes 1572872 | tf_op jit(solution)/shard_map/while/body/eval_jaxpr/ppermute | solution.py:18
  76.1 17.5 %collective-permute-start.1 = (f32[128,1024]{1,0:T(8,128)S(1)}, f32[128,1024]{1,0:T(8,128)S(1)}, u32[]{:S(2)}, u32[]{:S(2)}) collective-permute-start(f32[128,1024]{1,0:T(8,128)S(1)} %get-tuple-element.223), channel_id=1, source_target_pairs={{2,0},{4,2},{6,4},{8,6},{10,8},{12,10},{14,12},{16,14},{18,16},{20... | collective-permute-start | bytes 1572872 | tf_op jit(solution)/shard_map/while/body/eval_jaxpr/ppermute | solution.py:21
  98.4 18.6 %collective-permute-start = (f32[128,1024]{1,0:T(8,128)S(1)}, f32[128,1024]{1,0:T(8,128)S(1)}, u32[]{:S(2)}, u32[]{:S(2)}) collective-permute-start(f32[128,1024]{1,0:T(8,128)S(1)} %get-tuple-element.222), channel_id=1, source_target_pairs={{0,2},{2,4},{4,6},{6,8},{8,10},{10,12},{12,14},{14,16},{16,18},{18... | collective-permute-start | bytes 1572872 | tf_op jit(solution)/shard_map/while/body/eval_jaxpr/ppermute | solution.py:18
  100.3 17.6 %collective-permute-start.1 = (f32[128,1024]{1,0:T(8,128)S(1)}, f32[128,1024]{1,0:T(8,128)S(1)}, u32[]{:S(2)}, u32[]{:S(2)}) collective-permute-start(f32[128,1024]{1,0:T(8,128)S(1)} %get-tuple-element.223), channel_id=1, source_target_pairs={{2,0},{4,2},{6,4},{8,6},{10,8},{12,10},{14,12},{16,14},{18,16},{20... | collective-permute-start | bytes 1572872 | tf_op jit(solution)/shard_map/while/body/eval_jaxpr/ppermute | solution.py:21
  122.8 18.6 %collective-permute-start = (f32[128,1024]{1,0:T(8,128)S(1)}, f32[128,1024]{1,0:T(8,128)S(1)}, u32[]{:S(2)}, u32[]{:S(2)}) collective-permute-start(f32[128,1024]{1,0:T(8,128)S(1)} %get-tuple-element.222), channel_id=1, source_target_pairs={{0,2},{2,4},{4,6},{6,8},{8,10},{10,12},{12,14},{14,16},{16,18},{18... | collective-permute-start | bytes 1572872 | tf_op jit(solution)/shard_map/while/body/eval_jaxpr/ppermute | solution.py:18
  124.7 17.6 %collective-permute-start.1 = (f32[128,1024]{1,0:T(8,128)S(1)}, f32[128,1024]{1,0:T(8,128)S(1)}, u32[]{:S(2)}, u32[]{:S(2)}) collective-permute-start(f32[128,1024]{1,0:T(8,128)S(1)} %get-tuple-element.223), channel_id=1, source_target_pairs={{2,0},{4,2},{6,4},{8,6},{10,8},{12,10},{14,12},{16,14},{18,16},{20... | collective-permute-start | bytes 1572872 | tf_op jit(solution)/shard_map/while/body/eval_jaxpr/ppermute | solution.py:21
  147.1 18.6 %collective-permute-start = (f32[128,1024]{1,0:T(8,128)S(1)}, f32[128,1024]{1,0:T(8,128)S(1)}, u32[]{:S(2)}, u32[]{:S(2)}) collective-permute-start(f32[128,1024]{1,0:T(8,128)S(1)} %get-tuple-element.222), channel_id=1, source_target_pairs={{0,2},{2,4},{4,6},{6,8},{8,10},{10,12},{12,14},{14,16},{16,18},{18... | collective-permute-start | bytes 1572872 | tf_op jit(solution)/shard_map/while/body/eval_jaxpr/ppermute | solution.py:18
  149.1 17.6 %collective-permute-start.1 = (f32[128,1024]{1,0:T(8,128)S(1)}, f32[128,1024]{1,0:T(8,128)S(1)}, u32[]{:S(2)}, u32[]{:S(2)}) collective-permute-start(f32[128,1024]{1,0:T(8,128)S(1)} %get-tuple-element.223), channel_id=1, source_target_pairs={{2,0},{4,2},{6,4},{8,6},{10,8},{12,10},{14,12},{16,14},{18,16},{20... | collective-permute-start | bytes 1572872 | tf_op jit(solution)/shard_map/while/body/eval_jaxpr/ppermute | solution.py:21
  171.5 18.6 %collective-permute-start = (f32[128,1024]{1,0:T(8,128)S(1)}, f32[128,1024]{1,0:T(8,128)S(1)}, u32[]{:S(2)}, u32[]{:S(2)}) collective-permute-start(f32[128,1024]{1,0:T(8,128)S(1)} %get-tuple-element.222), channel_id=1, source_target_pairs={{0,2},{2,4},{4,6},{6,8},{8,10},{10,12},{12,14},{14,16},{16,18},{18... | collective-permute-start | bytes 1572872 | tf_op jit(solution)/shard_map/while/body/eval_jaxpr/ppermute | solution.py:18
  173.4 17.6 %collective-permute-start.1 = (f32[128,1024]{1,0:T(8,128)S(1)}, f32[128,1024]{1,0:T(8,128)S(1)}, u32[]{:S(2)}, u32[]{:S(2)}) collective-permute-start(f32[128,1024]{1,0:T(8,128)S(1)} %get-tuple-element.223), channel_id=1, source_target_pairs={{2,0},{4,2},{6,4},{8,6},{10,8},{12,10},{14,12},{16,14},{18,16},{20... | collective-permute-start | bytes 1572872 | tf_op jit(solution)/shard_map/while/body/eval_jaxpr/ppermute | solution.py:21
  195.9 18.6 %collective-permute-start = (f32[128,1024]{1,0:T(8,128)S(1)}, f32[128,1024]{1,0:T(8,128)S(1)}, u32[]{:S(2)}, u32[]{:S(2)}) collective-permute-start(f32[128,1024]{1,0:T(8,128)S(1)} %get-tuple-element.222), channel_id=1, source_target_pairs={{0,2},{2,4},{4,6},{6,8},{8,10},{10,12},{12,14},{14,16},{16,18},{18... | collective-permute-start | bytes 1572872 | tf_op jit(solution)/shard_map/while/body/eval_jaxpr/ppermute | solution.py:18
  197.8 17.6 %collective-permute-start.1 = (f32[128,1024]{1,0:T(8,128)S(1)}, f32[128,1024]{1,0:T(8,128)S(1)}, u32[]{:S(2)}, u32[]{:S(2)}) collective-permute-start(f32[128,1024]{1,0:T(8,128)S(1)} %get-tuple-element.223), channel_id=1, source_target_pairs={{2,0},{4,2},{6,4},{8,6},{10,8},{12,10},{14,12},{16,14},{18,16},{20... | collective-permute-start | bytes 1572872 | tf_op jit(solution)/shard_map/while/body/eval_jaxpr/ppermute | solution.py:21
  220.3 18.6 %collective-permute-start = (f32[128,1024]{1,0:T(8,128)S(1)}, f32[128,1024]{1,0:T(8,128)S(1)}, u32[]{:S(2)}, u32[]{:S(2)}) collective-permute-start(f32[128,1024]{1,0:T(8,128)S(1)} %get-tuple-element.222), channel_id=1, source_target_pairs={{0,2},{2,4},{4,6},{6,8},{8,10},{10,12},{12,14},{14,16},{16,18},{18... | collective-permute-start | bytes 1572872 | tf_op jit(solution)/shard_map/while/body/eval_jaxpr/ppermute | solution.py:18
  222.2 17.6 %collective-permute-start.1 = (f32[128,1024]{1,0:T(8,128)S(1)}, f32[128,1024]{1,0:T(8,128)S(1)}, u32[]{:S(2)}, u32[]{:S(2)}) collective-permute-start(f32[128,1024]{1,0:T(8,128)S(1)} %get-tuple-element.223), channel_id=1, source_target_pairs={{2,0},{4,2},{6,4},{8,6},{10,8},{12,10},{14,12},{16,14},{18,16},{20... | collective-permute-start | bytes 1572872 | tf_op jit(solution)/shard_map/while/body/eval_jaxpr/ppermute | solution.py:21
  244.6 18.6 %collective-permute-start = (f32[128,1024]{1,0:T(8,128)S(1)}, f32[128,1024]{1,0:T(8,128)S(1)}, u32[]{:S(2)}, u32[]{:S(2)}) collective-permute-start(f32[128,1024]{1,0:T(8,128)S(1)} %get-tuple-element.222), channel_id=1, source_target_pairs={{0,2},{2,4},{4,6},{6,8},{8,10},{10,12},{12,14},{14,16},{16,18},{18... | collective-permute-start | bytes 1572872 | tf_op jit(solution)/shard_map/while/body/eval_jaxpr/ppermute | solution.py:18
  246.6 17.5 %collective-permute-start.1 = (f32[128,1024]{1,0:T(8,128)S(1)}, f32[128,1024]{1,0:T(8,128)S(1)}, u32[]{:S(2)}, u32[]{:S(2)}) collective-permute-start(f32[128,1024]{1,0:T(8,128)S(1)} %get-tuple-element.223), channel_id=1, source_target_pairs={{2,0},{4,2},{6,4},{8,6},{10,8},{12,10},{14,12},{16,14},{18,16},{20... | collective-permute-start | bytes 1572872 | tf_op jit(solution)/shard_map/while/body/eval_jaxpr/ppermute | solution.py:21
  268.9 18.6 %collective-permute-start = (f32[128,1024]{1,0:T(8,128)S(1)}, f32[128,1024]{1,0:T(8,128)S(1)}, u32[]{:S(2)}, u32[]{:S(2)}) collective-permute-start(f32[128,1024]{1,0:T(8,128)S(1)} %get-tuple-element.222), channel_id=1, source_target_pairs={{0,2},{2,4},{4,6},{6,8},{8,10},{10,12},{12,14},{14,16},{16,18},{18... | collective-permute-start | bytes 1572872 | tf_op jit(solution)/shard_map/while/body/eval_jaxpr/ppermute | solution.py:18
  270.8 17.5 %collective-permute-start.1 = (f32[128,1024]{1,0:T(8,128)S(1)}, f32[128,1024]{1,0:T(8,128)S(1)}, u32[]{:S(2)}, u32[]{:S(2)}) collective-permute-start(f32[128,1024]{1,0:T(8,128)S(1)} %get-tuple-element.223), channel_id=1, source_target_pairs={{2,0},{4,2},{6,4},{8,6},{10,8},{12,10},{14,12},{16,14},{18,16},{20... | collective-permute-start | bytes 1572872 | tf_op jit(solution)/shard_map/while/body/eval_jaxpr/ppermute | solution.py:21
  293.2 18.6 %collective-permute-start = (f32[128,1024]{1,0:T(8,128)S(1)}, f32[128,1024]{1,0:T(8,128)S(1)}, u32[]{:S(2)}, u32[]{:S(2)}) collective-permute-start(f32[128,1024]{1,0:T(8,128)S(1)} %get-tuple-element.222), channel_id=1, source_target_pairs={{0,2},{2,4},{4,6},{6,8},{8,10},{10,12},{12,14},{14,16},{16,18},{18... | collective-permute-start | bytes 1572872 | tf_op jit(solution)/shard_map/while/body/eval_jaxpr/ppermute | solution.py:18
  295.1 17.5 %collective-permute-start.1 = (f32[128,1024]{1,0:T(8,128)S(1)}, f32[128,1024]{1,0:T(8,128)S(1)}, u32[]{:S(2)}, u32[]{:S(2)}) collective-permute-start(f32[128,1024]{1,0:T(8,128)S(1)} %get-tuple-element.223), channel_id=1, source_target_pairs={{2,0},{4,2},{6,4},{8,6},{10,8},{12,10},{14,12},{16,14},{18,16},{20... | collective-permute-start | bytes 1572872 | tf_op jit(solution)/shard_map/while/body/eval_jaxpr/ppermute | solution.py:21
  317.5 18.6 %collective-permute-start = (f32[128,1024]{1,0:T(8,128)S(1)}, f32[128,1024]{1,0:T(8,128)S(1)}, u32[]{:S(2)}, u32[]{:S(2)}) collective-permute-start(f32[128,1024]{1,0:T(8,128)S(1)} %get-tuple-element.222), channel_id=1, source_target_pairs={{0,2},{2,4},{4,6},{6,8},{8,10},{10,12},{12,14},{14,16},{16,18},{18... | collective-permute-start | bytes 1572872 | tf_op jit(solution)/shard_map/while/body/eval_jaxpr/ppermute | solution.py:18
  319.4 17.5 %collective-permute-start.1 = (f32[128,1024]{1,0:T(8,128)S(1)}, f32[128,1024]{1,0:T(8,128)S(1)}, u32[]{:S(2)}, u32[]{:S(2)}) collective-permute-start(f32[128,1024]{1,0:T(8,128)S(1)} %get-tuple-element.223), channel_id=1, source_target_pairs={{2,0},{4,2},{6,4},{8,6},{10,8},{12,10},{14,12},{16,14},{18,16},{20... | collective-permute-start | bytes 1572872 | tf_op jit(solution)/shard_map/while/body/eval_jaxpr/ppermute | solution.py:21
  341.7 18.6 %collective-permute-start = (f32[128,1024]{1,0:T(8,128)S(1)}, f32[128,1024]{1,0:T(8,128)S(1)}, u32[]{:S(2)}, u32[]{:S(2)}) collective-permute-start(f32[128,1024]{1,0:T(8,128)S(1)} %get-tuple-element.222), channel_id=1, source_target_pairs={{0,2},{2,4},{4,6},{6,8},{8,10},{10,12},{12,14},{14,16},{16,18},{18... | collective-permute-start | bytes 1572872 | tf_op jit(solution)/shard_map/while/body/eval_jaxpr/ppermute | solution.py:18
  343.7 17.5 %collective-permute-start.1 = (f32[128,1024]{1,0:T(8,128)S(1)}, f32[128,1024]{1,0:T(8,128)S(1)}, u32[]{:S(2)}, u32[]{:S(2)}) collective-permute-start(f32[128,1024]{1,0:T(8,128)S(1)} %get-tuple-element.223), channel_id=1, source_target_pairs={{2,0},{4,2},{6,4},{8,6},{10,8},{12,10},{14,12},{16,14},{18,16},{20... | collective-permute-start | bytes 1572872 | tf_op jit(solution)/shard_map/while/body/eval_jaxpr/ppermute | solution.py:21
  366.0 18.6 %collective-permute-start = (f32[128,1024]{1,0:T(8,128)S(1)}, f32[128,1024]{1,0:T(8,128)S(1)}, u32[]{:S(2)}, u32[]{:S(2)}) collective-permute-start(f32[128,1024]{1,0:T(8,128)S(1)} %get-tuple-element.222), channel_id=1, source_target_pairs={{0,2},{2,4},{4,6},{6,8},{8,10},{10,12},{12,14},{14,16},{16,18},{18... | collective-permute-start | bytes 1572872 | tf_op jit(solution)/shard_map/while/body/eval_jaxpr/ppermute | solution.py:18
  367.9 17.5 %collective-permute-start.1 = (f32[128,1024]{1,0:T(8,128)S(1)}, f32[128,1024]{1,0:T(8,128)S(1)}, u32[]{:S(2)}, u32[]{:S(2)}) collective-permute-start(f32[128,1024]{1,0:T(8,128)S(1)} %get-tuple-element.223), channel_id=1, source_target_pairs={{2,0},{4,2},{6,4},{8,6},{10,8},{12,10},{14,12},{16,14},{18,16},{20... | collective-permute-start | bytes 1572872 | tf_op jit(solution)/shard_map/while/body/eval_jaxpr/ppermute | solution.py:21
  390.3 18.6 %collective-permute-start = (f32[128,1024]{1,0:T(8,128)S(1)}, f32[128,1024]{1,0:T(8,128)S(1)}, u32[]{:S(2)}, u32[]{:S(2)}) collective-permute-start(f32[128,1024]{1,0:T(8,128)S(1)} %get-tuple-element.222), channel_id=1, source_target_pairs={{0,2},{2,4},{4,6},{6,8},{8,10},{10,12},{12,14},{14,16},{16,18},{18... | collective-permute-start | bytes 1572872 | tf_op jit(solution)/shard_map/while/body/eval_jaxpr/ppermute | solution.py:18
  392.2 16.8 %collective-permute-start.1 = (f32[128,1024]{1,0:T(8,128)S(1)}, f32[128,1024]{1,0:T(8,128)S(1)}, u32[]{:S(2)}, u32[]{:S(2)}) collective-permute-start(f32[128,1024]{1,0:T(8,128)S(1)} %get-tuple-element.223), channel_id=1, source_target_pairs={{2,0},{4,2},{6,4},{8,6},{10,8},{12,10},{14,12},{16,14},{18,16},{20... | collective-permute-start | bytes 1572872 | tf_op jit(solution)/shard_map/while/body/eval_jaxpr/ppermute | solution.py:21
  413.7 1.0 copy-start
where the time goes:
time: 417 us; the launch traced here: 415 us
  starting transfers between devices  176 us (42%)
  waiting for transfers between devices  93.6 us (22%)
  matrix products  75.7 us (18%)
  other arithmetic  22.4 us (5%)
  loops' own time  21.3 us (5%)
  local copies, waits for them, and re-layouts  16 us (4%)
  blocking collectives  9.54 us (2%)
    ppermute x17, starting transfers between devices, with_halo(): lax.ppermute(lax.slice_in_dim(block, 0, width, axis=dim), axis, backward)  143 us
    ppermute x17, waiting for transfers between devices, with_halo(): lax.ppermute(lax.slice_in_dim(block, block.shape[dim] - width, None, axis...  80.1 us
    dot_general x32, matrix products, chase_windows(): lax.dot_general(onehot, coeffs, (((0,), (0,)), ((), ())), precision=lax.P...  36.7 us
    dot_general x32, matrix products, frame_windows(): jnp.dot(onehot * framed_v[None, :], framed, precision=lax.Precision.HIGHEST)  35 us
    ppermute x17, starting transfers between devices, with_halo(): lax.ppermute(lax.slice_in_dim(block, block.shape[dim] - width, None, axis...  32.6 us
    another operation x1, loops' own time, per_device(): return lax.fori_loop(0, SWEEPS // group_depth, advance_group, eigvecs)  21.3 us
    select_n x32, other arithmetic, frame_windows(): jnp.where(local_row >= offset, jnp.floor_divide(local_row - offset, BAND)...  19.7 us
    ppermute x17, waiting for transfers between devices, with_halo(): lax.ppermute(lax.slice_in_dim(block, 0, width, axis=dim), axis, backward)  13.4 us
  transfers between devices with their start and end apart: 34, of which 32 were waited for; matrix products, arithmetic and copies ran while one was open for 9% of the time, Pallas kernels for 0%

commit v1 on v0

v1 whole, which is shorter than its diff:
```python
import jax
import jax.numpy as jnp
from jax import lax
from jax.experimental import pallas as pl
from jax.experimental.pallas import tpu as pltpu
from jax.sharding import PartitionSpec as P

BAND = 64
SWEEPS = 32
LANES = 128
HALF = SWEEPS // 2
QUARTER = SWEEPS // 4


def dot(a, b, contract=((1,), (0,))):
    return lax.dot_general(
        a, b, (contract, ((), ())), precision=lax.Precision.HIGHEST, preferred_element_type=jnp.float32
    )


def lane_of(shape):
    return lax.broadcasted_iota(jnp.int32, shape, len(shape) - 1)


def row_of(shape):
    return lax.broadcasted_iota(jnp.int32, shape, 0)


def call(kernel, outs, *args, flops=1_000_000):
    nbytes = 4 * sum(a.size for a in args)
    return pl.pallas_call(
        kernel,
        out_shape=[jax.ShapeDtypeStruct(s, jnp.float32) for s in outs],
        in_specs=[pl.BlockSpec(memory_space=pltpu.VMEM)] * len(args),
        out_specs=[pl.BlockSpec(memory_space=pltpu.VMEM)] * len(outs),
        compiler_params=pltpu.CompilerParams(vmem_limit_bytes=16 * 1024 * 1024),
        cost_estimate=pl.CostEstimate(flops=flops, bytes_accessed=nbytes, transcendentals=0),
    )(*args)


def place():
    index = lax.axis_index("rows")
    return index % 2, (index // 2) % 2, index // 2


def factor_kernel(own_ref, other_ref, start_ref, x_ref, a_ref, msg_ref, coef_ref, inner_ref, proj_ref, edge_ref):
    first = lax.axis_index("cols") == 0
    own, other = own_ref[...], other_ref[...]
    r = jnp.concatenate([jnp.where(first, own, other), jnp.where(first, other, own)], axis=0)
    rows = r.shape[1]
    start = start_ref[:, 0:1]
    segment = (lane_of(r.shape) - start + BAND) >> 6
    parts = [jnp.where(segment == k, r, 0.0) for k in range(5)]
    zero = jnp.zeros_like(r)
    inner = jnp.concatenate(parts[1:4], axis=0)
    edge = jnp.concatenate([parts[0], parts[4]], axis=0)
    left = jnp.concatenate([inner, zero, edge], axis=0)
    right = jnp.concatenate([inner, zero, edge, zero, zero], axis=0)
    gram = dot(left, right, ((1,), (1,)))
    earlier = (lane_of(gram.shape) & (SWEEPS - 1)) < (row_of(gram.shape) & (SWEEPS - 1))
    gram = jnp.where(earlier, gram, 0.0)
    count = 3 * SWEEPS
    tau = 2.0 / jnp.sum(inner * inner, axis=1, keepdims=True)
    lower = tau * gram[0:count, 0:LANES]
    rhs = tau * jnp.concatenate([inner, gram[0:count, LANES : 2 * LANES]], axis=1)
    blocks = [[rhs[32 * k + 8 * q : 32 * k + 8 * q + 8] for q in range(4)] for k in range(3)]
    for j in range(SWEEPS - 1):
        source = [blocks[k][j // 8][j % 8 : j % 8 + 1] for k in range(3)]
        for k in range(3):
            for q in range((j + 1) // 8, 4):
                at = 32 * k + 8 * q
                total = blocks[k][q]
                for m in range(3):
                    if abs(m - k) < 2:
                        column = 32 * m + j
                        total = total - lower[at : at + 8, column : column + 1] * source[m]
                blocks[k][q] = total
    solved = jnp.concatenate([blocks[k][q] for k in range(3) for q in range(4)] + [jnp.zeros((32, rhs.shape[1]), jnp.float32)], axis=0)
    back = dot(gram[LANES : LANES + 64, 0:LANES], solved)
    observe = edge - back[:, 0:rows]
    couple = back[:, rows:] - gram[LANES : LANES + 64, LANES : 2 * LANES]
    squares = jnp.sum(edge * edge, axis=1, keepdims=True)
    coef = jnp.where(lane_of(couple.shape) == 64, squares, couple)
    coef_ref[...] = coef
    inner_ref[...] = inner
    proj_ref[...] = solved[0:count, 0:rows]
    edge_ref[...] = edge - dot(solved[0:count, rows : rows + 64], inner, ((0,), (0,)))
    a = dot(observe, x_ref[...])
    half = a.shape[1] // 2
    core, _, _ = place()
    low, high = a[:, 0:half], a[:, half:]
    a_ref[...] = jnp.where(core == 0, low, high)
    msg_ref[...] = jnp.concatenate([jnp.where(core == 0, high, low), coef], axis=1)


def merge_kernel(a_ref, coef_ref, msg_ref, mid_ref, even_ref, odd_ref, out_ref):
    core, parity, _ = place()
    half = a_ref.shape[1]
    mine = jnp.concatenate([a_ref[...], coef_ref[...]], axis=1)
    theirs = msg_ref[...]
    top = jnp.where(core == 0, mine, theirs)
    low = jnp.where(core == 0, theirs, mine)
    tc, lc = top[:, half:], low[:, half:]
    tau = 2.0 / (tc[32:64, 64:65] + lc[0:32, 64:65])
    lane = lane_of(tc.shape)
    tk = jnp.where(lane < 32, tc, 0.0)
    lk = jnp.where((lane >= 32) & (lane < 64), lc, 0.0)
    mid = jnp.concatenate([top[32:64, 0:half] + low[0:32, 0:half], tk[32:64] + lk[0:32]], axis=1) * tau
    left = jnp.concatenate([top[0:32, 0:half], tk[0:32]], axis=1)
    right = jnp.concatenate([low[32:64, 0:half], lk[32:64]], axis=1)
    into_left, into_right = tc[0:32], lc[32:64]
    own_top, own_low = tc[32:64] * tau, lc[0:32] * tau
    blocks = [mid[8 * q : 8 * q + 8] for q in range(4)]
    for j in range(SWEEPS):
        source = blocks[j // 8][j % 8 : j % 8 + 1]
        for q in range((j + 1) // 8, 4):
            at = 8 * q
            weight = own_top[at : at + 8, 32 + j : 33 + j] + own_low[at : at + 8, j : j + 1]
            blocks[q] = blocks[q] + weight * source
        left = left + into_left[:, 32 + j : 33 + j] * source
        right = right + into_right[:, j : j + 1] * source
    mid = jnp.concatenate(blocks, axis=0)

    def ordered(block):
        tile = block[:, half:]
        at = lane_of(tile.shape)
        swapped = jnp.where(at < 32, pltpu.roll(tile, 96, 1), pltpu.roll(tile, 32, 1))
        return jnp.where(at < 64, jnp.where(parity == 0, swapped, tile), 0.0)

    spot = lane_of((32, LANES)) == 64
    left_tile = jnp.where(spot, tc[0:32, 64:65], ordered(left))
    right_tile = jnp.where(spot, lc[32:64, 64:65], ordered(right))
    even_a = jnp.where(parity == 0, right[:, 0:half], left[:, 0:half])
    odd_a = jnp.where(parity == 0, left[:, 0:half], right[:, 0:half])
    even_t = jnp.where(parity == 0, right_tile, left_tile)
    odd_t = jnp.where(parity == 0, left_tile, right_tile)
    mid_ref[...] = jnp.concatenate([mid[:, 0:half], ordered(mid)], axis=1)
    even_ref[...] = jnp.concatenate([even_a, even_t], axis=1)
    odd_ref[...] = jnp.concatenate([odd_a, odd_t], axis=1)
    out_ref[...] = jnp.concatenate([even_a[0:8]] + [even_t[8 * q : 8 * q + 8] for q in range(4)], axis=1)


def substitute(block, lower, first, lane):
    for j in range(block.shape[0] - 1):
        block = block + lower[first : first + block.shape[0], lane + first + j : lane + first + j + 1] * block[j : j + 1]
    return block


def spread(rows, tile, at, solved, lane):
    for j in range(solved.shape[0]):
        rows = rows + tile[at : at + rows.shape[0], lane + j : lane + j + 1] * solved[j : j + 1]
    return rows


def even0_kernel(msg_ref, even_ref, odd_ref, w_ref, pair_ref, even_out, odd_out, out_ref):
    half = even_ref.shape[1] - LANES
    got = msg_ref[...]
    tile = even_ref[:, half:]
    other = jnp.concatenate([got[:, half + LANES * q : half + LANES * (q + 1)] for q in range(4)], axis=0)
    both = tile + other
    tau = 2.0 / both[:, 64:65]
    lower = tau * both
    pair_ref[...] = jnp.where(lane_of(lower.shape) == 64, tau, lower)
    w = substitute((even_ref[0:8, 0:half] + got[:, 0:half]) * tau[0:8], lower, 0, 0)
    w_ref[...] = w
    odd_tile = odd_ref[:, half:]
    odd = spread(odd_ref[:, 0:half], odd_tile, 0, w, 0)
    out_ref[...] = jnp.concatenate([odd[0:16], odd_tile[0:16], odd_tile[16:32]], axis=1)
    odd_out[...] = odd
    even_out[...] = spread(even_ref[8:32, 0:half], tile, 8, w, 0)


def odd0_kernel(msg_ref, start_ref, even_ref, odd_ref, even_t_ref, odd_t_ref, w_ref, pair_ref, even_out, odd_out, out_ref):
    half = even_ref.shape[1]
    _, _, chip = place()
    got = msg_ref[...]
    tile = odd_t_ref[...]
    both = tile + jnp.concatenate([got[:, half : half + LANES], got[:, half + LANES :]], axis=0)
    chips = lax.axis_size("rows") // 2
    valid = (chip > 0) & ((chip < chips - 1) | (start_ref[:, 0:1] == 0))
    tau = jnp.where(valid, 2.0 / jnp.where(valid, both[:, 64:65], 1.0), 0.0)
    lower = tau * both
    pair_ref[...] = jnp.where(lane_of(lower.shape) == 64, tau, lower)
    w = substitute((odd_ref[0:16] + got[:, 0:half]) * tau[0:16], lower, 0, 32)
    w_ref[...] = w
    even = spread(even_ref[...], even_t_ref[...], 8, w, 32)
    out_ref[...] = even[0:16]
    even_out[...] = even
    odd_out[...] = spread(odd_ref[16:32], tile, 16, w, 32)


def even1_kernel(msg_ref, pair_ref, even_ref, odd_ref, even_t_ref, odd_t_ref, w_ref, even_out, out_ref):
    pair = pair_ref[...]
    w = substitute((even_ref[0:16] + msg_ref[...]) * pair[8:24, 64:65], pair, 8, 0)
    w_ref[...] = w
    out_ref[...] = spread(odd_ref[...], odd_t_ref[...], 16, w, 8)
    even_out[...] = spread(even_ref[16:24], even_t_ref[...], 24, w, 8)


def odd1_kernel(msg_ref, pair_ref, odd_ref, even_ref, even_t_ref, w_ref, out_ref):
    pair = pair_ref[...]
    w = substitute((odd_ref[...] + msg_ref[...]) * pair[16:32, 64:65], pair, 16, 32)
    w_ref[...] = w
    out_ref[...] = spread(even_ref[...], even_t_ref[...], 24, w, 48)


def even2_kernel(msg_ref, pair_ref, even_ref, mid_ref, e0_ref, e1_ref, o0_ref, o1_ref, keep_ref, out_ref):
    core, parity, _ = place()
    half = even_ref.shape[1]
    pair = pair_ref[...]
    w = substitute((even_ref[...] + msg_ref[...]) * pair[24:32, 64:65], pair, 24, 0)
    even = jnp.concatenate([e0_ref[...], e1_ref[...], w], axis=0)
    odd = jnp.concatenate([o0_ref[...], o1_ref[...]], axis=0)
    mid = mid_ref[:, 0:half]
    tile = mid_ref[:, half:]
    mid = spread(spread(mid, tile, 0, even, 0), tile, 0, odd, 32)
    left = jnp.where(parity == 0, odd, even)
    right = jnp.where(parity == 0, even, odd)
    upper = jnp.concatenate([left, mid], axis=0)
    lower = jnp.concatenate([mid, right], axis=0)
    keep_ref[...] = jnp.where(core == 0, upper, lower)
    out_ref[...] = jnp.where(core == 0, lower, upper)


def inner_kernel(inner_ref, proj_ref, x_ref, y_ref):
    x = x_ref[...]
    y_ref[...] = x - dot(inner_ref[...], dot(proj_ref[...], x), ((0,), (0,)))


def final_kernel(edge_ref, keep_ref, msg_ref, y_ref, out_ref):
    core, _, _ = place()
    keep, got = keep_ref[...], msg_ref[...]
    w = jnp.concatenate([jnp.where(core == 0, keep, got), jnp.where(core == 0, got, keep)], axis=1)
    out_ref[...] = y_ref[...] - dot(edge_ref[...], w, ((0,), (0,)))


def per_device(eigvecs, reflectors, starts):
    count = lax.axis_size("rows")
    rows, cols = eigvecs.shape
    half = cols // 2
    wide = half + LANES
    on_chip = [(i, i ^ 1) for i in range(count)]
    even_pairs = [(i, i ^ 2) for i in range(count)]
    odd_pairs = [(i, ((i - 2) ^ 2) + 2) for i in range(2, count - 2)]
    start = jnp.broadcast_to(starts[:, None], (SWEEPS, LANES))
    other = lax.ppermute(reflectors, "cols", [(0, 1), (1, 0)])
    a, msg, coef, inner, proj, edge = call(
        factor_kernel,
        [(64, half), (64, wide), (64, LANES), (96, rows), (96, rows), (64, rows)],
        reflectors, other, start, eigvecs,
    )
    got = lax.ppermute(msg, "rows", on_chip)
    mid, even, odd, msg = call(merge_kernel, [(32, wide), (32, wide), (32, wide), (8, half + 4 * LANES)], a, coef, got)
    even_t, odd_t = even[:, half:], odd[:, half:]
    got = lax.ppermute(msg, "rows", even_pairs)
    (partial,) = call(inner_kernel, [(rows, cols)], inner, proj, eigvecs, flops=20_000_000)
    e0, even_pair, even, odd, msg = call(
        even0_kernel, [(8, half), (32, LANES), (24, half), (32, half), (16, half + 2 * LANES)], got, even, odd
    )
    got = lax.ppermute(msg, "rows", odd_pairs)
    o0, odd_pair, even, odd, msg = call(
        odd0_kernel, [(16, half), (32, LANES), (24, half), (16, half), (16, half)], got, start, even, odd, even_t, odd_t
    )
    got = lax.ppermute(msg, "rows", even_pairs)
    e1, even, odd = call(even1_kernel, [(16, half), (8, half), (16, half)], got, even_pair, even, odd, even_t, odd_t)
    got = lax.ppermute(odd, "rows", odd_pairs)
    o1, even = call(odd1_kernel, [(16, half), (8, half)], got, odd_pair, odd, even, even_t)
    got = lax.ppermute(even, "rows", even_pairs)
    keep, msg = call(even2_kernel, [(64, half), (64, half)], got, even_pair, even, mid, e0, e1, o0, o1)
    got = lax.ppermute(msg, "rows", on_chip)
    (out,) = call(final_kernel, [(rows, cols)], edge, keep, got, partial)
    return out


def solution(mesh):
    in_specs = (P("rows", "cols"), P("cols", "rows"), P())
    out_specs = P("rows", "cols")
    return jax.shard_map(
        per_device, mesh=mesh, in_specs=in_specs, out_specs=out_specs, check_vma=False
    )
```

time: 417 us -> 55.1 us (0.13)
  starting transfers between devices: 176 us -> 23.2 us
  matrix products: 75.7 us -> 0 us
  waiting for transfers between devices: 93.6 us -> 20.7 us
  other arithmetic: 22.4 us -> 0 us
  loops' own time: 21.3 us -> 0 us
  local copies, waits for them, and re-layouts: 16 us -> 1.96 us
  blocking collectives: 9.54 us -> 0 us
  Pallas kernels: 0 us -> 8.2 us
    ppermute x34 -> x8, starting transfers between devices: 176 us -> 23.2 us  [the longest x1 7.3 us: per_device(): got = lax.ppermute(odd, 'rows', odd_pairs)]
    dot_general x96 -> x0, matrix products: 75.7 us -> none  [the longest x32 36.7 us: chase_windows(): lax.dot_general(onehot, coeffs, (((0,), (0,)), ((), ())), precision=lax.P...]
    ppermute x34 -> x8, waiting for transfers between devices: 93.6 us -> 20.7 us  [the longest x2 6.8 us: per_device(): got = lax.ppermute(msg, 'rows', even_pairs)]
    another operation x1 -> x0, loops' own time: 21.3 us -> none  [per_device(): return lax.fori_loop(0, SWEEPS // group_depth, advance_group, eigvecs)]
    select_n x32 -> x0, other arithmetic: 19.7 us -> none  [frame_windows(): jnp.where(local_row >= offset, jnp.floor_divide(local_row - offset, BAND)...]
    dynamic_slice x32 -> x0, local copies, waits for them, and re-layouts: 10.3 us -> none  [the longest x16 10 us: advance_group(): starts[sweep_idx]]
    all_gather x1 -> x0, blocking collectives: 9.54 us -> none  [per_device(): every_sweep = lax.all_gather(reflectors, 'cols', axis=0, tiled=True)]
    pallas_call x0 -> x9, Pallas kernels: none -> 8.2 us  [call(): pl.pallas_call(kernel, out_shape=[jax.ShapeDtypeStruct(s, jnp.float32) fo...]
  transfers between devices with their start and end apart: 34 -> 8, of which waited for: 32 -> 7; matrix products, arithmetic and copies ran while one was open for 9% -> 0% of each run, Pallas kernels for 0% -> 3%
where the time goes in v1:
time: 55.1 us; the launch traced here: 54.2 us
  starting transfers between devices  23.2 us (42%)
  waiting for transfers between devices  20.7 us (38%)
  Pallas kernels  8.2 us (15%)
  local copies, waits for them, and re-layouts  1.96 us (4%)
    pallas_call x9, Pallas kernels, call(): pl.pallas_call(kernel, out_shape=[jax.ShapeDtypeStruct(s, jnp.float32) fo...  8.2 us
    ppermute x1, starting transfers between devices, per_device(): got = lax.ppermute(odd, 'rows', odd_pairs)  7.3 us
    ppermute x1, starting transfers between devices, per_device(): got = lax.ppermute(msg, 'rows', odd_pairs)  7.28 us
    ppermute x1, starting transfers between devices, per_device(): other = lax.ppermute(reflectors, 'cols', [(0, 1), (1, 0)])  7.19 us
    ppermute x2, waiting for transfers between devices, per_device(): got = lax.ppermute(msg, 'rows', even_pairs)  6.8 us
    ppermute x1, waiting for transfers between devices, per_device(): got = lax.ppermute(even, 'rows', even_pairs)  3.73 us
    ppermute x1, waiting for transfers between devices, per_device(): got = lax.ppermute(msg, 'rows', odd_pairs)  3.48 us
    ppermute x1, waiting for transfers between devices, per_device(): got = lax.ppermute(odd, 'rows', odd_pairs)  3.31 us
  transfers between devices with their start and end apart: 8, of which 7 were waited for; matrix products, arithmetic and copies ran while one was open for 0% of the time, Pallas kernels for 3%

profile of v1, /device:TPU:8, one launch (start us, length us, event | category | flops | bytes accessed | tf_op | source)
XLA Modules:
  0.0 54.2 jit_solution(15035495484427596493)
XLA Ops:
  0.0 0.0 copy-start.2
  0.0 7.2 %collective-permute-start = (f32[16,256]{1,0:T(8,128)}, f32[16,256]{1,0:T(8,128)S(1)}, u32[]{:S(2)}, u32[]{:S(2)}) collective-permute-start(f32[16,256]{1,0:T(8,128)} %own_ref.1), channel_id=1, source_target_pairs={{0,1},{1,0},{2,3},{3,2},{4,5},{5,4},{6,7},{7,6},{8,9},{9,8},{10,11... | collective-permute-start | bytes 49160 | tf_op jit(solution)/shard_map/ppermute | solution.py:246
  7.2 2.0 %collective-permute-done.other_ref = f32[16,256]{1,0:T(8,128)S(1)} collective-permute-done((f32[16,256]{1,0:T(8,128)}, f32[16,256]{1,0:T(8,128)S(1)}, u32[]{:S(2)}, u32[]{:S(2)}) %collective-permute-start) | collective-permute-done | bytes 16416 | tf_op jit(solution)/shard_map/ppermute | solution.py:246
  9.2 0.7 %broadcast_in_dim.2.start_ref = s32[32,128]{1,0:T(8,128)S(1)} broadcast(s32[32]{0:T(128)} %param.5), dimensions={0} | broadcast | bytes 16512 | tf_op jit(solution)/shard_map/broadcast_in_dim | solution.py:245
  9.9 0.0 copy-done.2
  9.9 0.0 copy-start
  9.9 1.2 %copy-done = f32[256,1024]{1,0:T(8,128)S(1)} copy-done((f32[256,1024]{1,0:T(8,128)S(1)}, f32[256,1024]{1,0:T(8,128)}, u32[]{:S(2)}) %copy-start) | copy-done | bytes 1048600
  11.1 0.0 copy-start.1
  11.1 2.4 %shard_map.37 = (f32[64,512]{1,0:T(8,128)S(1)}, f32[64,640]{1,0:T(8,128)S(1)}, f32[64,128]{1,0:T(8,128)S(1)}, f32[96,256]{1,0:T(8,128)S(1)}, f32[96,256]{1,0:T(8,128)S(1)}, /*index=5*/f32[64,256]{1,0:T(8,128)S(1)}) custom-call(f32[16,256]{1,0:T(8,128)S(1)} %copy-done.2, f32[16,256]{1,0:T(8,128)S(1)} %collective-permute-done.other_ref, ...), custom_call_target="tpu_custom_call" | custom-call | flops 1000000 | bytes 1097728 | tf_op jit(solution)/shard_map/pallas_call | solution.py:31
  13.6 0.1 collective-permute-start.1
  13.7 1.4 %collective-permute-done.1.msg_ref = f32[64,640]{1,0:T(8,128)S(1)} collective-permute-done((f32[64,640]{1,0:T(8,128)S(1)}, f32[64,640]{1,0:T(8,128)S(1)}, u32[]{:S(2)}, u32[]{:S(2)}) %collective-permute-start.1) | collective-permute-done | bytes 163872 | tf_op jit(solution)/shard_map/ppermute | solution.py:252
  15.1 0.8 %shard_map.38 = (f32[32,640]{1,0:T(8,128)S(1)}, f32[32,640]{1,0:T(8,128)S(1)}, f32[32,640]{1,0:T(8,128)S(1)}, f32[8,1024]{1,0:T(8,128)S(1)}) custom-call(f32[64,512]{1,0:T(8,128)S(1)} %get-tuple-element.33.a_ref, f32[64,128]{1,0:T(8,128)S(1)} %get-tuple-element.34.coef_ref, f32[64,640]{1,0:T(8,128)S(1)} %collective-permute-done.1.msg_ref), custom_call_target="tpu_custom_call" | custom-call | flops 1000000 | bytes 327680 | tf_op jit(solution)/shard_map/pallas_call | solution.py:31
  15.9 1.1 %collective-permute-start.2 = (f32[8,1024]{1,0:T(8,128)S(1)}, f32[8,1024]{1,0:T(8,128)S(1)}, u32[]{:S(2)}, u32[]{:S(2)}) collective-permute-start(f32[8,1024]{1,0:T(8,128)S(1)} %get-tuple-element.36), channel_id=1, source_target_pairs={{0,4},{2,6},{4,0},{6,2},{8,12},{10,14},{12,8},{14,10},{16,20},{18,... | collective-permute-start | bytes 98312 | tf_op jit(solution)/shard_map/ppermute | solution.py:255
  17.0 2.9 %collective-permute-done.2.msg_ref = f32[8,1024]{1,0:T(8,128)S(1)} collective-permute-done((f32[8,1024]{1,0:T(8,128)S(1)}, f32[8,1024]{1,0:T(8,128)S(1)}, u32[]{:S(2)}, u32[]{:S(2)}) %collective-permute-start.2) | collective-permute-done | bytes 32800 | tf_op jit(solution)/shard_map/ppermute | solution.py:255
  19.9 0.2 shard_map.39
  20.1 7.3 %collective-permute-start.3 = (f32[16,768]{1,0:T(8,128)S(1)}, f32[16,768]{1,0:T(8,128)S(1)}, u32[]{:S(2)}, u32[]{:S(2)}) collective-permute-start(f32[16,768]{1,0:T(8,128)S(1)} %get-tuple-element.39), channel_id=1, source_target_pairs={{4,8},{6,10},{8,4},{10,6},{12,16},{14,18},{16,12},{18,14},{20,24},... | collective-permute-start | bytes 147464 | tf_op jit(solution)/shard_map/ppermute | solution.py:260
  27.5 3.5 %collective-permute-done.3.msg_ref = f32[16,768]{1,0:T(8,128)S(1)} collective-permute-done((f32[16,768]{1,0:T(8,128)S(1)}, f32[16,768]{1,0:T(8,128)S(1)}, u32[]{:S(2)}, u32[]{:S(2)}) %collective-permute-start.3) | collective-permute-done | bytes 49184 | tf_op jit(solution)/shard_map/ppermute | solution.py:260
  30.9 0.4 shard_map.40
  31.3 0.1 collective-permute-start.4
  31.4 3.9 %collective-permute-done.4.msg_ref = f32[16,512]{1,0:T(8,128)S(1)} collective-permute-done((f32[16,512]{1,0:T(8,128)S(1)}, f32[16,512]{1,0:T(8,128)S(1)}, u32[]{:S(2)}, u32[]{:S(2)}) %collective-permute-start.4) | collective-permute-done | bytes 32800 | tf_op jit(solution)/shard_map/ppermute | solution.py:264
  35.3 0.2 shard_map.41
  35.5 7.3 %collective-permute-start.5 = (f32[16,512]{1,0:T(8,128)S(1)}, f32[16,512]{1,0:T(8,128)S(1)}, u32[]{:S(2)}, u32[]{:S(2)}) collective-permute-start(f32[16,512]{1,0:T(8,128)S(1)} %get-tuple-element.46.odd_ref), channel_id=1, source_target_pairs={{4,8},{6,10},{8,4},{10,6},{12,16},{14,18},{16,12},{18,14},{20,24},... | collective-permute-start | bytes 98312 | tf_op jit(solution)/shard_map/ppermute | solution.py:266
  42.8 3.3 %collective-permute-done.5.msg_ref = f32[16,512]{1,0:T(8,128)S(1)} collective-permute-done((f32[16,512]{1,0:T(8,128)S(1)}, f32[16,512]{1,0:T(8,128)S(1)}, u32[]{:S(2)}, u32[]{:S(2)}) %collective-permute-start.5) | collective-permute-done | bytes 32800 | tf_op jit(solution)/shard_map/ppermute | solution.py:266
  46.1 0.1 shard_map.42
  46.3 0.1 collective-permute-start.6
  46.4 3.7 %collective-permute-done.6.msg_ref = f32[8,512]{1,0:T(8,128)S(1)} collective-permute-done((f32[8,512]{1,0:T(8,128)S(1)}, f32[8,512]{1,0:T(8,128)S(1)}, u32[]{:S(2)}, u32[]{:S(2)}) %collective-permute-start.6) | collective-permute-done | bytes 16416 | tf_op jit(solution)/shard_map/ppermute | solution.py:268
  50.1 0.5 shard_map.43
  50.6 0.1 collective-permute-start.7
  50.7 0.0 copy-done.1
  50.7 1.5 %shard_map.44.y_ref = f32[256,1024]{1,0:T(8,128)S(1)} custom-call(f32[96,256]{1,0:T(8,128)S(1)} %get-tuple-element.57.inner_ref, f32[96,256]{1,0:T(8,128)S(1)} %get-tuple-element.58.proj_ref, f32[256,1024]{1,0:T(8,128)S(1)} %copy-done.1), custom_call_target="tpu_custom_call" | custom-call | flops 20000000 | bytes 1245184 | tf_op jit(solution)/shard_map/pallas_call | solution.py:31
  52.2 0.0 collective-permute-done.7.msg_ref
  52.3 2.0 %shard_map.45 = f32[256,1024]{1,0:T(8,128)} custom-call(f32[64,256]{1,0:T(8,128)S(1)} %get-tuple-element.32.edge_ref, f32[64,512]{1,0:T(8,128)S(1)} %get-tuple-element.55.keep_ref, f32[64,512]{1,0:T(8,128)S(1)} %collective-permute-done.7.msg_ref, f32[256,1024]{1,0:T(8,128)S(1)} %shard_map.44.y_ref), custom_call_target="tpu_custom_call" | custom-call | flops 1000000 | bytes 1376256 | tf_op jit(solution)/shard_map/pallas_call | solution.py:31
  (2 shorter events, 0.0 us)
Async XLA Ops:
  0.0 9.9 %copy-start.2 = (f32[16,256]{1,0:T(8,128)S(1)}, f32[16,256]{1,0:T(8,128)}, u32[]{:S(2)}) copy-start(f32[16,256]{1,0:T(8,128)} %own_ref.1) | copy-start | bytes 49156
  0.0 9.2 %collective-permute-start = (f32[16,256]{1,0:T(8,128)}, f32[16,256]{1,0:T(8,128)S(1)}, u32[]{:S(2)}, u32[]{:S(2)}) collective-permute-start(f32[16,256]{1,0:T(8,128)} %own_ref.1), channel_id=1, source_target_pairs={{0,1},{1,0},{2,3},{3,2},{4,5},{5,4},{6,7},{7,6},{8,9},{9,8},{10,11... | collective-permute-start | bytes 49160 | tf_op jit(solution)/shard_map/ppermute | solution.py:246
  9.9 1.2 %copy-start = (f32[256,1024]{1,0:T(8,128)S(1)}, f32[256,1024]{1,0:T(8,128)}, u32[]{:S(2)}) copy-start(f32[256,1024]{1,0:T(8,128)} %x_ref.3) | copy-start | bytes 3145732
  11.1 39.6 %copy-start.1 = (f32[256,1024]{1,0:T(8,128)S(1)}, f32[256,1024]{1,0:T(8,128)}, u32[]{:S(2)}) copy-start(f32[256,1024]{1,0:T(8,128)} %x_ref.3) | copy-start | bytes 3145732
  13.6 1.5 %collective-permute-start.1 = (f32[64,640]{1,0:T(8,128)S(1)}, f32[64,640]{1,0:T(8,128)S(1)}, u32[]{:S(2)}, u32[]{:S(2)}) collective-permute-start(f32[64,640]{1,0:T(8,128)S(1)} %get-tuple-element.35), channel_id=1, source_target_pairs={{0,2},{2,0},{4,6},{6,4},{8,10},{10,8},{12,14},{14,12},{16,18},{18,... | collective-permute-start | bytes 491528 | tf_op jit(solution)/shard_map/ppermute | solution.py:252
  15.9 4.0 %collective-permute-start.2 = (f32[8,1024]{1,0:T(8,128)S(1)}, f32[8,1024]{1,0:T(8,128)S(1)}, u32[]{:S(2)}, u32[]{:S(2)}) collective-permute-start(f32[8,1024]{1,0:T(8,128)S(1)} %get-tuple-element.36), channel_id=1, source_target_pairs={{0,4},{2,6},{4,0},{6,2},{8,12},{10,14},{12,8},{14,10},{16,20},{18,... | collective-permute-start | bytes 98312 | tf_op jit(solution)/shard_map/ppermute | solution.py:255
  20.1 10.8 %collective-permute-start.3 = (f32[16,768]{1,0:T(8,128)S(1)}, f32[16,768]{1,0:T(8,128)S(1)}, u32[]{:S(2)}, u32[]{:S(2)}) collective-permute-start(f32[16,768]{1,0:T(8,128)S(1)} %get-tuple-element.39), channel_id=1, source_target_pairs={{4,8},{6,10},{8,4},{10,6},{12,16},{14,18},{16,12},{18,14},{20,24},... | collective-permute-start | bytes 147464 | tf_op jit(solution)/shard_map/ppermute | solution.py:260
  31.3 4.0 %collective-permute-start.4 = (f32[16,512]{1,0:T(8,128)S(1)}, f32[16,512]{1,0:T(8,128)S(1)}, u32[]{:S(2)}, u32[]{:S(2)}) collective-permute-start(f32[16,512]{1,0:T(8,128)S(1)} %get-tuple-element.42), channel_id=1, source_target_pairs={{0,4},{2,6},{4,0},{6,2},{8,12},{10,14},{12,8},{14,10},{16,20},{18,... | collective-permute-start | bytes 98312 | tf_op jit(solution)/shard_map/ppermute | solution.py:264
  35.5 10.6 %collective-permute-start.5 = (f32[16,512]{1,0:T(8,128)S(1)}, f32[16,512]{1,0:T(8,128)S(1)}, u32[]{:S(2)}, u32[]{:S(2)}) collective-permute-start(f32[16,512]{1,0:T(8,128)S(1)} %get-tuple-element.46.odd_ref), channel_id=1, source_target_pairs={{4,8},{6,10},{8,4},{10,6},{12,16},{14,18},{16,12},{18,14},{20,24},... | collective-permute-start | bytes 98312 | tf_op jit(solution)/shard_map/ppermute | solution.py:266
  46.3 3.8 %collective-permute-start.6 = (f32[8,512]{1,0:T(8,128)S(1)}, f32[8,512]{1,0:T(8,128)S(1)}, u32[]{:S(2)}, u32[]{:S(2)}) collective-permute-start(f32[8,512]{1,0:T(8,128)S(1)} %get-tuple-element.49.even_ref), channel_id=1, source_target_pairs={{0,4},{2,6},{4,0},{6,2},{8,12},{10,14},{12,8},{14,10},{16,20},{18,... | collective-permute-start | bytes 49160 | tf_op jit(solution)/shard_map/ppermute | solution.py:268
  50.6 1.6 %collective-permute-start.7 = (f32[64,512]{1,0:T(8,128)S(1)}, f32[64,512]{1,0:T(8,128)S(1)}, u32[]{:S(2)}, u32[]{:S(2)}) collective-permute-start(f32[64,512]{1,0:T(8,128)S(1)} %get-tuple-element.56), channel_id=1, source_target_pairs={{0,2},{2,0},{4,6},{6,4},{8,10},{10,8},{12,14},{14,12},{16,18},{18,... | collective-permute-start | bytes 393224 | tf_op jit(solution)/shard_map/ppermute | solution.py:270

commit v2 on v0

v2 whole, which is shorter than its diff:
```python
import jax
import jax.numpy as jnp
from jax import lax
from jax.experimental import pallas as pl
from jax.experimental.pallas import tpu as pltpu
from jax.sharding import PartitionSpec as P

BAND = 64
SWEEPS = 32
LANES = 128


def dot(a, b, contract=((1,), (0,))):
    return lax.dot_general(
        a, b, (contract, ((), ())), precision=lax.Precision.HIGHEST, preferred_element_type=jnp.float32
    )


def lane_of(shape):
    return lax.broadcasted_iota(jnp.int32, shape, len(shape) - 1)


def row_of(shape):
    return lax.broadcasted_iota(jnp.int32, shape, 0)


def call(kernel, outs, *args, flops=1_000_000):
    nbytes = 4 * sum(a.size for a in args)
    return pl.pallas_call(
        kernel,
        out_shape=[jax.ShapeDtypeStruct(s, jnp.float32) if isinstance(s, tuple) else s for s in outs],
        in_specs=[pl.BlockSpec(memory_space=pltpu.VMEM)] * len(args),
        out_specs=[pl.BlockSpec(memory_space=pltpu.VMEM)] * len(outs),
        compiler_params=pltpu.CompilerParams(vmem_limit_bytes=16 * 1024 * 1024),
        cost_estimate=pl.CostEstimate(flops=flops, bytes_accessed=nbytes, transcendentals=0),
    )(*args)


def split(a):
    high = a.astype(jnp.bfloat16)
    return high, (a - high.astype(jnp.float32)).astype(jnp.bfloat16)


def dot3(a, b, contract=((1,), (0,))):
    (ah, al), (bh, bl) = split(a), b if isinstance(b, tuple) else split(b)

    def one(x, y):
        return lax.dot_general(x, y, (contract, ((), ())), preferred_element_type=jnp.float32)

    return one(ah, bh) + (one(ah, bl) + one(al, bh))


def ready_kernel(x_ref, own_ref, start_ref, high_ref, low_ref, copy_ref, column_ref):
    high_ref[...], low_ref[...] = split(x_ref[...])
    copy_ref[...] = own_ref[...]
    square = (SWEEPS, SWEEPS)
    row = start_ref[...].astype(jnp.float32)
    column = jnp.sum(jnp.where(lane_of(square) == row_of(square), row, 0.0), axis=1, keepdims=True)
    column_ref[...] = jnp.broadcast_to(column, (SWEEPS, LANES))


def factor_kernel(own_ref, other_ref, start_ref, high_ref, low_ref, msg_ref, inner_ref, proj_ref, edge_ref):
    first = lax.axis_index("cols") == 0
    own, other = own_ref[...], other_ref[...]
    r = jnp.concatenate([jnp.where(first, own, other), jnp.where(first, other, own)], axis=0)
    rows = r.shape[1]
    start = start_ref[:, 0:1].astype(jnp.int32)
    segment = (lane_of(r.shape) - start + BAND) >> 6
    parts = [jnp.where(segment == k, r, 0.0) for k in range(5)]
    zero = jnp.zeros_like(r)
    inner = jnp.concatenate(parts[1:4], axis=0)
    edge = jnp.concatenate([parts[0], parts[4]], axis=0)
    left = jnp.concatenate([inner, zero, edge], axis=0)
    right = jnp.concatenate([inner, zero, edge, zero, zero], axis=0)
    gram = dot(left, right, ((1,), (1,)))
    earlier = (lane_of(gram.shape) & (SWEEPS - 1)) < (row_of(gram.shape) & (SWEEPS - 1))
    gram = jnp.where(earlier, gram, 0.0)
    count = 3 * SWEEPS
    tau = 2.0 / jnp.sum(inner * inner, axis=1, keepdims=True)
    lower = tau * gram[0:count, 0:LANES]
    rhs = tau * jnp.concatenate([inner, gram[0:count, LANES : 2 * LANES]], axis=1)
    blocks = [[rhs[32 * k + 8 * q : 32 * k + 8 * q + 8] for q in range(4)] for k in range(3)]
    for j in range(SWEEPS - 1):
        source = [blocks[k][j // 8][j % 8 : j % 8 + 1] for k in range(3)]
        for k in range(3):
            for q in range((j + 1) // 8, 4):
                at = 32 * k + 8 * q
                total = blocks[k][q]
                for m in range(3):
                    if abs(m - k) < 2:
                        column = 32 * m + j
                        total = total - lower[at : at + 8, column : column + 1] * source[m]
                blocks[k][q] = total
    solved = jnp.concatenate([blocks[k][q] for k in range(3) for q in range(4)] + [jnp.zeros((32, rhs.shape[1]), jnp.float32)], axis=0)
    back = dot(gram[LANES : LANES + 64, 0:LANES], solved)
    observe = edge - back[:, 0:rows]
    couple = back[:, rows:] - gram[LANES : LANES + 64, LANES : 2 * LANES]
    squares = jnp.sum(edge * edge, axis=1, keepdims=True)
    coef = jnp.where(lane_of(couple.shape) == 64, squares, couple)
    inner_ref[...] = inner
    proj_ref[...] = solved[0:count, 0:rows]
    edge_ref[...] = edge - dot(solved[0:count, rows : rows + 64], inner, ((0,), (0,)))
    msg_ref[...] = jnp.concatenate([dot3(observe, (high_ref[...], low_ref[...])), coef], axis=1)


def to_low(tile):
    return jnp.where(lane_of(tile.shape) < 32, pltpu.roll(tile, LANES - 32, 1), 0.0)


def solve(blocks, lower, lane=0):
    for j in range(SWEEPS):
        source = blocks[j // 8][j % 8 : j % 8 + 1]
        for q in range((j + 1) // 8, len(blocks)):
            blocks[q] = blocks[q] + lower[8 * q : 8 * q + 8, lane + j : lane + j + 1] * source
    return jnp.concatenate(blocks, axis=0)


def spread(rows, tile, at, solved, lane):
    for j in range(solved.shape[0]):
        rows = rows + tile[at : at + rows.shape[0], lane + j : lane + j + 1] * solved[j : j + 1]
    return rows


def substitute(block, lower, first, lane):
    for j in range(block.shape[0] - 1):
        block = block + lower[first : first + block.shape[0], lane + first + j : lane + first + j + 1] * block[j : j + 1]
    return block


def chip_of():
    return lax.axis_index("rows") // 2


def merge_kernel(own_ref, got_ref, mid_ref, e_ref, o_ref):
    even = chip_of() % 2 == 0
    cols = own_ref.shape[1] - LANES
    top, low = got_ref[...], own_ref[...]
    tc, lc = top[:, cols:], low[:, cols:]
    tau = 2.0 / (tc[32:64, 64:65] + lc[0:32, 64:65])
    lane = lane_of(tc.shape)
    tk = jnp.where(lane < 32, tc, 0.0)
    lk = jnp.where((lane >= 32) & (lane < 64), lc, 0.0)
    mid = jnp.concatenate([top[32:64, 0:cols] + low[0:32, 0:cols], tk[32:64] + lk[0:32]], axis=1) * tau
    left = jnp.concatenate([top[0:32, 0:cols], tk[0:32]], axis=1)
    right = jnp.concatenate([low[32:64, 0:cols], lk[32:64]], axis=1)
    weights = (pltpu.roll(tc[32:64], LANES - 32, 1) + lc[0:32]) * tau
    mid = solve([mid[8 * q : 8 * q + 8] for q in range(4)], weights)
    left = spread(left, tc, 0, mid, 32)
    right = spread(right, lc, 32, mid, 0)

    def ordered(block):
        tile = block[:, cols:]
        at = lane_of(tile.shape)
        swapped = jnp.where(at < 32, pltpu.roll(tile, 96, 1), pltpu.roll(tile, 32, 1))
        return jnp.where(at < 64, jnp.where(even, swapped, tile), 0.0)

    spot = lane_of((32, LANES)) == 64
    left = jnp.concatenate([left[:, 0:cols], jnp.where(spot, tc[0:32, 64:65], ordered(left))], axis=1)
    right = jnp.concatenate([right[:, 0:cols], jnp.where(spot, lc[32:64, 64:65], ordered(right))], axis=1)
    mid_ref[...] = jnp.concatenate([mid[:, 0:cols], ordered(mid)], axis=1)
    e_ref[...] = jnp.where(even, right, left)
    o_ref[...] = jnp.where(even, left, right)


def pair_kernel(e_ref, o_ref, got_ref, pair_ref, p_ref, msg_ref):
    cols = e_ref.shape[1] - LANES
    mine, theirs = e_ref[:, cols:], got_ref[:, cols:]
    tau = 2.0 / (mine[:, 64:65] + theirs[:, 64:65])
    lower = tau * (mine + theirs)
    lane = lane_of(mine.shape)
    upper = (lane >= 32) & (lane < 64)
    outer = to_low(theirs) + jnp.where(upper, mine, 0.0)
    pair = jnp.concatenate([e_ref[:, 0:cols] + got_ref[:, 0:cols], outer], axis=1) * tau
    pair = solve([pair[8 * q : 8 * q + 8] for q in range(4)], lower)
    pair_ref[...] = pair
    tile = o_ref[:, cols:]
    p = jnp.concatenate([o_ref[:, 0:cols], jnp.where((lane >= 32) & (lane < 65), tile, 0.0)], axis=1)
    p = spread(p, tile, 0, pair, 0)
    p_ref[...] = p
    msg_ref[...] = jnp.concatenate([p[0:16], p[16:32, cols:]], axis=1)


def outer_kernel(got_ref, pair_ref, w_ref):
    cols = got_ref.shape[1] - LANES
    tile = got_ref[:, cols:]
    kept = to_low(tile) + jnp.where(lane_of(tile.shape) == 64, tile, 0.0)
    w = jnp.concatenate([got_ref[:, 0:cols], kept], axis=1)
    w_ref[...] = spread(w, tile, 0, pair_ref[...], 0)


def p0_kernel(msg_ref, p_ref, w_ref, p0_ref, scaled_ref, out_ref):
    cols = p_ref.shape[1] - LANES
    got = msg_ref[...]
    both = p_ref[:, cols:] + jnp.concatenate([got[:, cols : cols + LANES], got[:, cols + LANES :]], axis=0)
    tau = 2.0 / both[:, 64:65]
    lower = tau * both
    scaled_ref[...] = jnp.where(lane_of(lower.shape) == 64, tau, lower)
    p0 = substitute((p_ref[0:16, 0:cols] + got[:, 0:cols]) * tau[0:16], lower, 0, 32)
    p0_ref[...] = p0
    tile = w_ref[:, cols:]
    out_ref[...] = jnp.concatenate(
        [jnp.concatenate([w_ref[0:16, 0:cols], spread(w_ref[16:32, 0:cols], tile, 16, p0, 32)], axis=0), tile], axis=1
    )


def w_kernel(msg_ref, start_ref, w_ref, p_ref, p0_ref, out_w_ref, out_ref):
    cols = w_ref.shape[1] - LANES
    chip = chip_of()
    chips = lax.axis_size("rows") // 2
    start = start_ref[:, 0:1]
    valid = (chip != 1) & ((chip != chips - 2) | (start == 0.0))
    both = w_ref[:, cols:] + msg_ref[:, cols:]
    tau = jnp.where(valid, 2.0 / jnp.where(valid, both[:, 64:65], 1.0), 0.0)
    w = (w_ref[:, 0:cols] + msg_ref[:, 0:cols]) * tau
    w = solve([w[8 * q : 8 * q + 8] for q in range(4)], tau * both)
    out_w_ref[...] = w
    tile = p_ref[:, cols:]
    rest = spread(p_ref[16:32, 0:cols], tile, 16, p0_ref[...], 32)
    out_ref[...] = spread(rest, tile, 16, w[0:16], 0)


def known_kernel(pair_ref, w_ref, p0_ref, out_ref):
    cols = w_ref.shape[1]
    tile = pair_ref[:, cols:]
    out_ref[...] = spread(spread(pair_ref[:, 0:cols], tile, 0, w_ref[...], 0), tile, 0, p0_ref[...], 32)


def p1_kernel(msg_ref, scaled_ref, rest_ref, pair_ref, known_ref, p0_ref, p_ref, e_ref):
    cols = msg_ref.shape[1]
    scaled = scaled_ref[...]
    p1 = substitute((rest_ref[...] + msg_ref[...]) * scaled[16:32, 64:65], scaled, 16, 32)
    p_ref[...] = jnp.concatenate([p0_ref[...], p1], axis=0)
    e_ref[...] = spread(known_ref[...], pair_ref[:, cols:], 0, p1, 48)


def inside():
    place = chip_of() % 4
    return (place == 1) | (place == 2)


def mid_kernel(mid_ref, p_ref, got_ref, o_ref, out_ref):
    cols = p_ref.shape[1]
    o = jnp.where(inside(), p_ref[...], got_ref[...])
    o_ref[...] = o
    out_ref[...] = spread(mid_ref[:, 0:cols], mid_ref[:, cols:], 0, o, 32)


def back_kernel(mid_ref, part_ref, o_ref, e_ref, got_ref, keep_ref, out_ref):
    cols = e_ref.shape[1]
    even = chip_of() % 2 == 0
    e, o = jnp.where(inside(), e_ref[...], got_ref[...]), o_ref[...]
    mid = spread(part_ref[...], mid_ref[:, cols:], 0, e, 0)
    out_ref[...] = jnp.concatenate([jnp.where(even, o, e), mid], axis=0)
    keep_ref[...] = jnp.concatenate([mid, jnp.where(even, e, o)], axis=0)


def inner_kernel(inner_ref, proj_ref, high_ref, low_ref, x_ref, y_ref):
    part = dot3(proj_ref[...], (high_ref[...], low_ref[...]))
    y_ref[...] = x_ref[...] - dot3(inner_ref[...], part, ((0,), (0,)))


def final_kernel(edge_ref, keep_ref, msg_ref, y_ref, out_ref):
    south = lax.axis_index("rows") % 2 == 0
    w = jnp.where(south, msg_ref[...], keep_ref[...])
    out_ref[...] = y_ref[...] - dot3(edge_ref[...], w, ((0,), (0,)))


def per_device(eigvecs, reflectors, starts):
    count = lax.axis_size("rows")
    chips = count // 2
    rows, cols = eigvecs.shape
    wide = cols + LANES

    def north(pairs):
        return [(2 * a + 1, 2 * b + 1) for a, b in pairs]

    up = [(2 * c, 2 * c + 1) for c in range(chips)]
    down = [(b, a) for a, b in up]
    to_inner = north([(q, q + 1) for q in range(0, chips, 4)] + [(q + 3, q + 2) for q in range(0, chips, 4)])
    to_outer = [(b, a) for a, b in to_inner]
    p_pairs = north([(q + 1, q + 2) for q in range(0, chips, 4)] + [(q + 2, q + 1) for q in range(0, chips, 4)])
    w_pairs = north([(q + 2, q + 5) for q in range(0, chips - 4, 4)] + [(q + 5, q + 2) for q in range(0, chips - 4, 4)])
    other = lax.ppermute(reflectors, "cols", [(0, 1), (1, 0)])
    half = jax.ShapeDtypeStruct(eigvecs.shape, jnp.bfloat16)
    high, low, own, start = call(
        ready_kernel, [half, half, reflectors.shape, (SWEEPS, LANES)], eigvecs, reflectors, starts[None, :], flops=20_000_000
    )
    msg, inner, proj, edge = call(
        factor_kernel,
        [(64, wide), (96, rows), (96, rows), (64, rows)],
        own, other, start, high, low,
    )
    got = lax.ppermute(msg, "rows", up)
    mid, e, o = call(merge_kernel, [(32, wide)] * 3, msg, got)
    got_e = lax.ppermute(e, "rows", to_inner)
    got_o = lax.ppermute(o, "rows", to_inner)
    pair, p, msg = call(pair_kernel, [(32, wide), (32, wide), (16, wide + LANES)], e, o, got_e)
    got = lax.ppermute(msg, "rows", p_pairs)
    (w,) = call(outer_kernel, [(32, wide)], got_o, pair)
    p0, scaled, w = call(p0_kernel, [(16, cols), (32, LANES), (32, wide)], got, p, w)
    got = lax.ppermute(w, "rows", w_pairs)
    (partial,) = call(inner_kernel, [(rows, cols)], inner, proj, high, low, eigvecs, flops=20_000_000)
    w, rest = call(w_kernel, [(32, cols), (16, cols)], got, start, w, p, p0)
    got = lax.ppermute(rest, "rows", p_pairs)
    got_w = lax.ppermute(w, "rows", to_outer)
    (known,) = call(known_kernel, [(32, cols)], pair, w, p0)
    p, e = call(p1_kernel, [(32, cols), (32, cols)], got, scaled, rest, pair, known, p0)
    got_e = lax.ppermute(e, "rows", to_outer)
    o, part = call(mid_kernel, [(32, cols), (32, cols)], mid, p, got_w)
    keep, msg = call(back_kernel, [(64, cols), (64, cols)], mid, part, o, e, got_e)
    got = lax.ppermute(msg, "rows", down)
    (out,) = call(final_kernel, [(rows, cols)], edge, keep, got, partial)
    return out


def solution(mesh):
    in_specs = (P("rows", "cols"), P("cols", "rows"), P())
    out_specs = P("rows", "cols")
    return jax.shard_map(
        per_device, mesh=mesh, in_specs=in_specs, out_specs=out_specs, check_vma=False
    )
```

time: 417 us -> 52.4 us (0.13)
  starting transfers between devices: 176 us -> 14.8 us
  matrix products: 75.7 us -> 0 us
  waiting for transfers between devices: 93.6 us -> 24.9 us
  other arithmetic: 22.4 us -> 0 us
  loops' own time: 21.3 us -> 0 us
  local copies, waits for them, and re-layouts: 16 us -> 1.95 us
  Pallas kernels: 0 us -> 9.83 us
  blocking collectives: 9.54 us -> 0 us
    ppermute x34 -> x10, starting transfers between devices: 176 us -> 14.8 us  [the longest x1 7.19 us: per_device(): other = lax.ppermute(reflectors, 'cols', [(0, 1), (1, 0)])]
    dot_general x96 -> x0, matrix products: 75.7 us -> none  [the longest x32 36.7 us: chase_windows(): lax.dot_general(onehot, coeffs, (((0,), (0,)), ((), ())), precision=lax.P...]
    ppermute x34 -> x10, waiting for transfers between devices: 93.6 us -> 24.9 us  [the longest x1 23.7 us: per_device(): got = lax.ppermute(msg, 'rows', down)]
    another operation x1 -> x0, loops' own time: 21.3 us -> none  [per_device(): return lax.fori_loop(0, SWEEPS // group_depth, advance_group, eigvecs)]
    select_n x32 -> x0, other arithmetic: 19.7 us -> none  [frame_windows(): jnp.where(local_row >= offset, jnp.floor_divide(local_row - offset, BAND)...]
    dynamic_slice x32 -> x0, local copies, waits for them, and re-layouts: 10.3 us -> none  [the longest x16 10 us: advance_group(): starts[sweep_idx]]
    pallas_call x0 -> x13, Pallas kernels: none -> 9.83 us  [call(): pl.pallas_call(kernel, out_shape=[jax.ShapeDtypeStruct(s, jnp.float32) if...]
    all_gather x1 -> x0, blocking collectives: 9.54 us -> none  [per_device(): every_sweep = lax.all_gather(reflectors, 'cols', axis=0, tiled=True)]
  transfers between devices with their start and end apart: 34 -> 10, of which waited for: 32 -> 2; matrix products, arithmetic and copies ran while one was open for 9% -> 0% of each run, Pallas kernels for 0% -> 7%
where the time goes in v2:
time: 52.4 us; the launch traced here: 51.7 us
  waiting for transfers between devices  24.9 us (48%)
  starting transfers between devices  14.8 us (28%)
  Pallas kernels  9.83 us (19%)
  local copies, waits for them, and re-layouts  1.95 us (4%)
    ppermute x1, waiting for transfers between devices, per_device(): got = lax.ppermute(msg, 'rows', down)  23.7 us
    pallas_call x13, Pallas kernels, call(): pl.pallas_call(kernel, out_shape=[jax.ShapeDtypeStruct(s, jnp.float32) if...  9.83 us
    ppermute x1, starting transfers between devices, per_device(): other = lax.ppermute(reflectors, 'cols', [(0, 1), (1, 0)])  7.19 us
    unnamed x8, local copies, waits for them, and re-layouts  1.95 us
    ppermute x1, starting transfers between devices, per_device(): got = lax.ppermute(msg, 'rows', up)  1.47 us
    ppermute x1, starting transfers between devices, per_device(): got = lax.ppermute(msg, 'rows', down)  1.29 us
    ppermute x1, waiting for transfers between devices, per_device(): got = lax.ppermute(msg, 'rows', up)  1.17 us
  transfers between devices with their start and end apart: 10, of which 2 were waited for; matrix products, arithmetic and copies ran while one was open for 0% of the time, Pallas kernels for 7%

profile of v2, /device:TPU:8, one launch (start us, length us, event | category | flops | bytes accessed | tf_op | source)
XLA Modules:
  0.0 51.7 jit_solution(16580476882081792495)
XLA Ops:
  0.0 0.0 copy-start.3
  0.0 7.2 %collective-permute-start = (f32[16,256]{1,0:T(8,128)}, f32[16,256]{1,0:T(8,128)S(1)}, u32[]{:S(2)}, u32[]{:S(2)}) collective-permute-start(f32[16,256]{1,0:T(8,128)} %own_ref.1), channel_id=1, source_target_pairs={{0,1},{1,0},{2,3},{3,2},{4,5},{5,4},{6,7},{7,6},{8,9},{9,8},{10,11... | collective-permute-start | bytes 49160 | tf_op jit(solution)/shard_map/ppermute | solution.py:283
  7.2 0.0 copy-done.3
  7.2 0.0 copy-start
  7.2 1.2 %copy-done = f32[256,1024]{1,0:T(8,128)S(1)} copy-done((f32[256,1024]{1,0:T(8,128)S(1)}, f32[256,1024]{1,0:T(8,128)}, u32[]{:S(2)}) %copy-start) | copy-done | bytes 1048600
  8.4 0.0 copy-start.2
  8.4 0.7 %copy-done.2 = f32[16,256]{1,0:T(8,128)S(1)} copy-done((f32[16,256]{1,0:T(8,128)S(1)}, f32[16,256]{1,0:T(8,128)}, u32[]{:S(2)}) %copy-start.2) | copy-done | bytes 16408
  9.1 0.3 shard_map.37
  9.4 0.0 collective-permute-done.other_ref
  9.4 2.2 %shard_map.38 = (f32[64,1152]{1,0:T(8,128)S(1)}, f32[96,256]{1,0:T(8,128)S(1)}, f32[96,256]{1,0:T(8,128)S(1)}, f32[64,256]{1,0:T(8,128)S(1)}) custom-call(f32[16,256]{1,0:T(8,128)S(1)} %get-tuple-element.30.own_ref, f32[16,256]{1,0:T(8,128)S(1)} %collective-permute-done.other_ref, f32[32,128]{1,0:T(8,128)S(1)} %get-tuple-element.31.start_ref, ...), custom_call_target="tpu_custom_call" | custom-call | flops 1000000 | bytes 2146304 | tf_op jit(solution)/shard_map/pallas_call | solution.py:29
  11.7 1.5 %collective-permute-start.1 = (f32[64,1152]{1,0:T(8,128)S(1)}, f32[64,1152]{1,0:T(8,128)S(1)}, u32[]{:S(2)}, u32[]{:S(2)}) collective-permute-start(f32[64,1152]{1,0:T(8,128)S(1)} %get-tuple-element.35.own_ref), channel_id=1, source_target_pairs={{0,2},{4,6},{8,10},{12,14},{16,18},{20,22},{24,26},{28,30},{32,34}... | collective-permute-start | bytes 884744 | tf_op jit(solution)/shard_map/ppermute | solution.py:293
  13.1 1.2 %collective-permute-done.1.got_ref = f32[64,1152]{1,0:T(8,128)S(1)} collective-permute-done((f32[64,1152]{1,0:T(8,128)S(1)}, f32[64,1152]{1,0:T(8,128)S(1)}, u32[]{:S(2)}, u32[]{:S(2)}) %collective-permute-start.1) | collective-permute-done | bytes 294944 | tf_op jit(solution)/shard_map/ppermute | solution.py:293
  14.3 1.3 %shard_map.39 = (f32[32,1152]{1,0:T(8,128)S(1)}, f32[32,1152]{1,0:T(8,128)S(1)}, f32[32,1152]{1,0:T(8,128)S(1)}) custom-call(f32[64,1152]{1,0:T(8,128)S(1)} %get-tuple-element.35.own_ref, f32[64,1152]{1,0:T(8,128)S(1)} %collective-permute-done.1.got_ref), custom_call_target="tpu_custom_call" | custom-call | flops 1000000 | bytes 589824 | tf_op jit(solution)/shard_map/pallas_call | solution.py:29
  15.6 0.7 %collective-permute-start.2 = (f32[32,1152]{1,0:T(8,128)S(1)}, f32[32,1152]{1,0:T(8,128)S(1)}, u32[]{:S(2)}, u32[]{:S(2)}) collective-permute-start(f32[32,1152]{1,0:T(8,128)S(1)} %get-tuple-element.37.e_ref), channel_id=1, source_target_pairs={{2,6},{18,22},{34,38},{50,54},{66,70},{82,86},{98,102},{114,118},{... | collective-permute-start | bytes 442376 | tf_op jit(solution)/shard_map/ppermute | solution.py:295
  16.3 0.7 %collective-permute-start.4 = (f32[32,1152]{1,0:T(8,128)S(1)}, f32[32,1152]{1,0:T(8,128)S(1)}, u32[]{:S(2)}, u32[]{:S(2)}) collective-permute-start(f32[32,1152]{1,0:T(8,128)S(1)} %get-tuple-element.38.o_ref), channel_id=1, source_target_pairs={{2,6},{18,22},{34,38},{50,54},{66,70},{82,86},{98,102},{114,118},{... | collective-permute-start | bytes 442376 | tf_op jit(solution)/shard_map/ppermute | solution.py:296
  16.9 0.0 collective-permute-done.2.got_ref
  16.9 0.8 %shard_map.40 = (f32[32,1152]{1,0:T(8,128)S(1)}, f32[32,1152]{1,0:T(8,128)S(1)}, f32[16,1280]{1,0:T(8,128)S(1)}) custom-call(f32[32,1152]{1,0:T(8,128)S(1)} %get-tuple-element.37.e_ref, f32[32,1152]{1,0:T(8,128)S(1)} %get-tuple-element.38.o_ref, f32[32,1152]{1,0:T(8,128)S(1)} %collective-permute-done.2.got_ref), custom_call_target="tpu_custom_call" | custom-call | flops 1000000 | bytes 442368 | tf_op jit(solution)/shard_map/pallas_call | solution.py:29
  17.7 0.7 %collective-permute-start.3 = (f32[16,1280]{1,0:T(8,128)S(1)}, f32[16,1280]{1,0:T(8,128)S(1)}, u32[]{:S(2)}, u32[]{:S(2)}) collective-permute-start(f32[16,1280]{1,0:T(8,128)S(1)} %get-tuple-element.39), channel_id=1, source_target_pairs={{6,10},{22,26},{38,42},{54,58},{70,74},{86,90},{102,106},{118,122}... | collective-permute-start | bytes 245768 | tf_op jit(solution)/shard_map/ppermute | solution.py:298
  18.4 0.0 collective-permute-done.4.got_ref
  18.4 0.4 shard_map.41.w_ref
  18.8 0.0 collective-permute-done.3.msg_ref
  18.8 0.3 shard_map.42
  19.1 0.7 %collective-permute-start.5 = (f32[32,1152]{1,0:T(8,128)S(1)}, f32[32,1152]{1,0:T(8,128)S(1)}, u32[]{:S(2)}, u32[]{:S(2)}) collective-permute-start(f32[32,1152]{1,0:T(8,128)S(1)} %get-tuple-element.42.w_ref), channel_id=1, source_target_pairs={{10,22},{26,38},{42,54},{58,70},{74,86},{90,102},{106,118},{122,13... | collective-permute-start | bytes 442376 | tf_op jit(solution)/shard_map/ppermute | solution.py:301
  19.8 0.0 collective-permute-done.5.msg_ref
  19.8 0.5 %shard_map.43 = (f32[32,1024]{1,0:T(8,128)S(1)}, f32[16,1024]{1,0:T(8,128)S(1)}) custom-call(f32[32,1152]{1,0:T(8,128)S(1)} %collective-permute-done.5.msg_ref, f32[32,128]{1,0:T(8,128)S(1)} %get-tuple-element.31.start_ref, f32[32,1152]{1,0:T(8,128)S(1)} %get-tuple-element.42.w_ref, f32[32,1152]{1,0:T(8,128)S(1)} %get-tuple-element.40.p_ref, ...), custom_call_target="tpu_custom_call" | custom-call | flops 1000000 | bytes 524288 | tf_op jit(solution)/shard_map/pallas_call | solution.py:29
  20.4 0.0 copy-start.1
  20.4 0.8 %collective-permute-start.6 = (f32[16,1024]{1,0:T(8,128)S(1)}, f32[16,1024]{1,0:T(8,128)S(1)}, u32[]{:S(2)}, u32[]{:S(2)}) collective-permute-start(f32[16,1024]{1,0:T(8,128)S(1)} %get-tuple-element.44.rest_ref), channel_id=1, source_target_pairs={{6,10},{22,26},{38,42},{54,58},{70,74},{86,90},{102,106},{118,122}... | collective-permute-start | bytes 196616 | tf_op jit(solution)/shard_map/ppermute | solution.py:304
  21.2 0.7 %collective-permute-start.7 = (f32[32,1024]{1,0:T(8,128)S(1)}, f32[32,1024]{1,0:T(8,128)S(1)}, u32[]{:S(2)}, u32[]{:S(2)}) collective-permute-start(f32[32,1024]{1,0:T(8,128)S(1)} %get-tuple-element.46.w_ref), channel_id=1, source_target_pairs={{6,2},{22,18},{38,34},{54,50},{70,66},{86,82},{102,98},{118,114},{... | collective-permute-start | bytes 393224 | tf_op jit(solution)/shard_map/ppermute | solution.py:305
  21.9 0.5 shard_map.44.known_ref
  22.4 0.0 collective-permute-done.6.msg_ref
  22.4 0.3 shard_map.45
  22.7 0.7 %collective-permute-start.8 = (f32[32,1024]{1,0:T(8,128)S(1)}, f32[32,1024]{1,0:T(8,128)S(1)}, u32[]{:S(2)}, u32[]{:S(2)}) collective-permute-start(f32[32,1024]{1,0:T(8,128)S(1)} %get-tuple-element.50.e_ref), channel_id=1, source_target_pairs={{6,2},{22,18},{38,34},{54,50},{70,66},{86,82},{102,98},{118,114},{... | collective-permute-start | bytes 393224 | tf_op jit(solution)/shard_map/ppermute | solution.py:308
  23.4 0.0 collective-permute-done.7.got_ref
  23.4 0.4 shard_map.46
  23.8 0.0 collective-permute-done.8.got_ref
  23.8 0.4 shard_map.47
  24.2 1.3 %collective-permute-start.9 = (f32[64,1024]{1,0:T(8,128)S(1)}, f32[64,1024]{1,0:T(8,128)S(1)}, u32[]{:S(2)}, u32[]{:S(2)}) collective-permute-start(f32[64,1024]{1,0:T(8,128)S(1)} %get-tuple-element.52), channel_id=1, source_target_pairs={{2,0},{6,4},{10,8},{14,12},{18,16},{22,20},{26,24},{30,28},{34,32}... | collective-permute-start | bytes 786440 | tf_op jit(solution)/shard_map/ppermute | solution.py:311
  25.5 0.0 copy-done.1
  25.5 0.9 %shard_map.48.y_ref = f32[256,1024]{1,0:T(8,128)S(1)} custom-call(f32[96,256]{1,0:T(8,128)S(1)} %get-tuple-element.53.inner_ref, f32[96,256]{1,0:T(8,128)S(1)} %get-tuple-element.54.proj_ref, bf16[256,1024]{1,0:T(8,128)(2,1)S(1)} %get-tuple-element.32.high_ref, bf16[256,1024]{1,0:T(8,128)(2,1)S(1)} %get-tuple-element.33.low_ref, f32[256,1024]{1,0:T(8,128)S(1)} %copy-done.1), custom_call_target="tpu_custom_call" | custom-call | flops 20000000 | bytes 3342336 | tf_op jit(solution)/shard_map/pallas_call | solution.py:29
  26.4 23.7 %collective-permute-done.9.msg_ref = f32[64,1024]{1,0:T(8,128)S(1)} collective-permute-done((f32[64,1024]{1,0:T(8,128)S(1)}, f32[64,1024]{1,0:T(8,128)S(1)}, u32[]{:S(2)}, u32[]{:S(2)}) %collective-permute-start.9) | collective-permute-done | bytes 262176 | tf_op jit(solution)/shard_map/ppermute | solution.py:311
  50.1 1.6 %shard_map.49 = f32[256,1024]{1,0:T(8,128)} custom-call(f32[64,256]{1,0:T(8,128)S(1)} %get-tuple-element.34.edge_ref, f32[64,1024]{1,0:T(8,128)S(1)} %get-tuple-element.51.keep_ref, f32[64,1024]{1,0:T(8,128)S(1)} %collective-permute-done.9.msg_ref, f32[256,1024]{1,0:T(8,128)S(1)} %shard_map.48.y_ref), custom_call_target="tpu_custom_call" | custom-call | flops 1000000 | bytes 1638400 | tf_op jit(solution)/shard_map/pallas_call | solution.py:29
Async XLA Ops:
  0.0 7.2 %copy-start.3 = (s32[32]{0:T(128)S(1)}, s32[32]{0:T(128)}, u32[]{:S(2)}) copy-start(s32[32]{0:T(128)} %param.5) | copy-start | bytes 388
  0.0 9.4 %collective-permute-start = (f32[16,256]{1,0:T(8,128)}, f32[16,256]{1,0:T(8,128)S(1)}, u32[]{:S(2)}, u32[]{:S(2)}) collective-permute-start(f32[16,256]{1,0:T(8,128)} %own_ref.1), channel_id=1, source_target_pairs={{0,1},{1,0},{2,3},{3,2},{4,5},{5,4},{6,7},{7,6},{8,9},{9,8},{10,11... | collective-permute-start | bytes 49160 | tf_op jit(solution)/shard_map/ppermute | solution.py:283
  7.2 1.2 %copy-start = (f32[256,1024]{1,0:T(8,128)S(1)}, f32[256,1024]{1,0:T(8,128)}, u32[]{:S(2)}) copy-start(f32[256,1024]{1,0:T(8,128)} %x_ref.3) | copy-start | bytes 3145732
  8.4 0.7 %copy-start.2 = (f32[16,256]{1,0:T(8,128)S(1)}, f32[16,256]{1,0:T(8,128)}, u32[]{:S(2)}) copy-start(f32[16,256]{1,0:T(8,128)} %own_ref.1) | copy-start | bytes 49156
  11.7 2.7 %collective-permute-start.1 = (f32[64,1152]{1,0:T(8,128)S(1)}, f32[64,1152]{1,0:T(8,128)S(1)}, u32[]{:S(2)}, u32[]{:S(2)}) collective-permute-start(f32[64,1152]{1,0:T(8,128)S(1)} %get-tuple-element.35.own_ref), channel_id=1, source_target_pairs={{0,2},{4,6},{8,10},{12,14},{16,18},{20,22},{24,26},{28,30},{32,34}... | collective-permute-start | bytes 884744 | tf_op jit(solution)/shard_map/ppermute | solution.py:293
  15.6 1.4 %collective-permute-start.2 = (f32[32,1152]{1,0:T(8,128)S(1)}, f32[32,1152]{1,0:T(8,128)S(1)}, u32[]{:S(2)}, u32[]{:S(2)}) collective-permute-start(f32[32,1152]{1,0:T(8,128)S(1)} %get-tuple-element.37.e_ref), channel_id=1, source_target_pairs={{2,6},{18,22},{34,38},{50,54},{66,70},{82,86},{98,102},{114,118},{... | collective-permute-start | bytes 442376 | tf_op jit(solution)/shard_map/ppermute | solution.py:295
  16.3 2.1 %collective-permute-start.4 = (f32[32,1152]{1,0:T(8,128)S(1)}, f32[32,1152]{1,0:T(8,128)S(1)}, u32[]{:S(2)}, u32[]{:S(2)}) collective-permute-start(f32[32,1152]{1,0:T(8,128)S(1)} %get-tuple-element.38.o_ref), channel_id=1, source_target_pairs={{2,6},{18,22},{34,38},{50,54},{66,70},{82,86},{98,102},{114,118},{... | collective-permute-start | bytes 442376 | tf_op jit(solution)/shard_map/ppermute | solution.py:296
  17.7 1.1 %collective-permute-start.3 = (f32[16,1280]{1,0:T(8,128)S(1)}, f32[16,1280]{1,0:T(8,128)S(1)}, u32[]{:S(2)}, u32[]{:S(2)}) collective-permute-start(f32[16,1280]{1,0:T(8,128)S(1)} %get-tuple-element.39), channel_id=1, source_target_pairs={{6,10},{22,26},{38,42},{54,58},{70,74},{86,90},{102,106},{118,122}... | collective-permute-start | bytes 245768 | tf_op jit(solution)/shard_map/ppermute | solution.py:298
  19.1 0.7 %collective-permute-start.5 = (f32[32,1152]{1,0:T(8,128)S(1)}, f32[32,1152]{1,0:T(8,128)S(1)}, u32[]{:S(2)}, u32[]{:S(2)}) collective-permute-start(f32[32,1152]{1,0:T(8,128)S(1)} %get-tuple-element.42.w_ref), channel_id=1, source_target_pairs={{10,22},{26,38},{42,54},{58,70},{74,86},{90,102},{106,118},{122,13... | collective-permute-start | bytes 442376 | tf_op jit(solution)/shard_map/ppermute | solution.py:301
  20.4 5.1 %copy-start.1 = (f32[256,1024]{1,0:T(8,128)S(1)}, f32[256,1024]{1,0:T(8,128)}, u32[]{:S(2)}) copy-start(f32[256,1024]{1,0:T(8,128)} %x_ref.3) | copy-start | bytes 3145732
  20.4 2.0 %collective-permute-start.6 = (f32[16,1024]{1,0:T(8,128)S(1)}, f32[16,1024]{1,0:T(8,128)S(1)}, u32[]{:S(2)}, u32[]{:S(2)}) collective-permute-start(f32[16,1024]{1,0:T(8,128)S(1)} %get-tuple-element.44.rest_ref), channel_id=1, source_target_pairs={{6,10},{22,26},{38,42},{54,58},{70,74},{86,90},{102,106},{118,122}... | collective-permute-start | bytes 196616 | tf_op jit(solution)/shard_map/ppermute | solution.py:304
  21.2 2.2 %collective-permute-start.7 = (f32[32,1024]{1,0:T(8,128)S(1)}, f32[32,1024]{1,0:T(8,128)S(1)}, u32[]{:S(2)}, u32[]{:S(2)}) collective-permute-start(f32[32,1024]{1,0:T(8,128)S(1)} %get-tuple-element.46.w_ref), channel_id=1, source_target_pairs={{6,2},{22,18},{38,34},{54,50},{70,66},{86,82},{102,98},{118,114},{... | collective-permute-start | bytes 393224 | tf_op jit(solution)/shard_map/ppermute | solution.py:305
  22.7 1.1 %collective-permute-start.8 = (f32[32,1024]{1,0:T(8,128)S(1)}, f32[32,1024]{1,0:T(8,128)S(1)}, u32[]{:S(2)}, u32[]{:S(2)}) collective-permute-start(f32[32,1024]{1,0:T(8,128)S(1)} %get-tuple-element.50.e_ref), channel_id=1, source_target_pairs={{6,2},{22,18},{38,34},{54,50},{70,66},{86,82},{102,98},{118,114},{... | collective-permute-start | bytes 393224 | tf_op jit(solution)/shard_map/ppermute | solution.py:308
  24.2 25.9 %collective-permute-start.9 = (f32[64,1024]{1,0:T(8,128)S(1)}, f32[64,1024]{1,0:T(8,128)S(1)}, u32[]{:S(2)}, u32[]{:S(2)}) collective-permute-start(f32[64,1024]{1,0:T(8,128)S(1)} %get-tuple-element.52), channel_id=1, source_target_pairs={{2,0},{6,4},{10,8},{14,12},{18,16},{22,20},{26,24},{30,28},{34,32}... | collective-permute-start | bytes 786440 | tf_op jit(solution)/shard_map/ppermute | solution.py:311

commit v3 on v2

--- a/solution.py
+++ b/solution.py
@@ -209,9 +209,10 @@
     chips = lax.axis_size("rows") // 2
     start = start_ref[:, 0:1]
     valid = (chip != 1) & ((chip != chips - 2) | (start == 0.0))
-    both = w_ref[:, cols:] + msg_ref[:, cols:]
+    got = jnp.where((chip != 1) & (chip != chips - 2), msg_ref[...], 0.0)
+    both = w_ref[:, cols:] + got[:, cols:]
     tau = jnp.where(valid, 2.0 / jnp.where(valid, both[:, 64:65], 1.0), 0.0)
-    w = (w_ref[:, 0:cols] + msg_ref[:, 0:cols]) * tau
+    w = (w_ref[:, 0:cols] + got[:, 0:cols]) * tau
     w = solve([w[8 * q : 8 * q + 8] for q in range(4)], tau * both)
     out_w_ref[...] = w
     tile = p_ref[:, cols:]
@@ -259,10 +260,21 @@
     y_ref[...] = x_ref[...] - dot3(inner_ref[...], part, ((0,), (0,)))
 
 
-def final_kernel(edge_ref, keep_ref, msg_ref, y_ref, out_ref):
+def final_kernel(edge_ref, keep_ref, msg_ref, y_ref, out_ref, piece_ref, sems):
     south = lax.axis_index("rows") % 2 == 0
-    w = jnp.where(south, msg_ref[...], keep_ref[...])
-    out_ref[...] = y_ref[...] - dot3(edge_ref[...], w, ((0,), (0,)))
+    edge = edge_ref[...]
+    pieces = piece_ref.shape[0]
+    width = piece_ref.shape[2]
+    copies = []
+    for i in range(pieces):
+        at = slice(i * width, (i + 1) * width)
+        w = jnp.where(south, msg_ref[:, at], keep_ref[:, at])
+        piece_ref[i] = y_ref[:, at] - dot3(edge, w, ((0,), (0,)))
+        copy = pltpu.make_async_copy(piece_ref.at[i], out_ref.at[:, at], sems.at[i])
+        copy.start()
+        copies.append(copy)
+    for copy in copies:
+        copy.wait()
 
 
 def per_device(eigvecs, reflectors, starts):
@@ -271,15 +283,16 @@
     rows, cols = eigvecs.shape
     wide = cols + LANES
 
-    def north(pairs):
-        return [(2 * a + 1, 2 * b + 1) for a, b in pairs]
-
-    up = [(2 * c, 2 * c + 1) for c in range(chips)]
-    down = [(b, a) for a, b in up]
-    to_inner = north([(q, q + 1) for q in range(0, chips, 4)] + [(q + 3, q + 2) for q in range(0, chips, 4)])
-    to_outer = [(b, a) for a, b in to_inner]
-    p_pairs = north([(q + 1, q + 2) for q in range(0, chips, 4)] + [(q + 2, q + 1) for q in range(0, chips, 4)])
-    w_pairs = north([(q + 2, q + 5) for q in range(0, chips - 4, 4)] + [(q + 5, q + 2) for q in range(0, chips - 4, 4)])
+    def place_of(i):
+        return i % 2 == 1, (i // 2) % 4 in (1, 2), (i // 2) % 4 == 2
+
+    def swap(pick):
+        return [(i, pick(i, *place_of(i)) % count) for i in range(count)]
+
+    on_chip = swap(lambda i, north, inside, last: i ^ 1)
+    in_pair = swap(lambda i, north, inside, last: i ^ 2 if north else i ^ 8)
+    p_pairs = swap(lambda i, north, inside, last: i ^ 6 if north and inside else i ^ 8)
+    w_pairs = swap(lambda i, north, inside, last: (i + 6 if last else i - 6) if north and inside else i ^ 8 if north else i ^ 2)
     other = lax.ppermute(reflectors, "cols", [(0, 1), (1, 0)])
     half = jax.ShapeDtypeStruct(eigvecs.shape, jnp.bfloat16)
     high, low, own, start = call(
@@ -290,10 +303,10 @@
         [(64, wide), (96, rows), (96, rows), (64, rows)],
         own, other, start, high, low,
     )
-    got = lax.ppermute(msg, "rows", up)
+    got = lax.ppermute(msg, "rows", on_chip)
     mid, e, o = call(merge_kernel, [(32, wide)] * 3, msg, got)
-    got_e = lax.ppermute(e, "rows", to_inner)
-    got_o = lax.ppermute(o, "rows", to_inner)
+    got_e = lax.ppermute(e, "rows", in_pair)
+    got_o = lax.ppermute(o, "rows", in_pair)
     pair, p, msg = call(pair_kernel, [(32, wide), (32, wide), (16, wide + LANES)], e, o, got_e)
     got = lax.ppermute(msg, "rows", p_pairs)
     (w,) = call(outer_kernel, [(32, wide)], got_o, pair)
@@ -302,15 +315,21 @@
     (partial,) = call(inner_kernel, [(rows, cols)], inner, proj, high, low, eigvecs, flops=20_000_000)
     w, rest = call(w_kernel, [(32, cols), (16, cols)], got, start, w, p, p0)
     got = lax.ppermute(rest, "rows", p_pairs)
-    got_w = lax.ppermute(w, "rows", to_outer)
+    got_w = lax.ppermute(w, "rows", in_pair)
     (known,) = call(known_kernel, [(32, cols)], pair, w, p0)
     p, e = call(p1_kernel, [(32, cols), (32, cols)], got, scaled, rest, pair, known, p0)
-    got_e = lax.ppermute(e, "rows", to_outer)
+    got_e = lax.ppermute(e, "rows", in_pair)
     o, part = call(mid_kernel, [(32, cols), (32, cols)], mid, p, got_w)
     keep, msg = call(back_kernel, [(64, cols), (64, cols)], mid, part, o, e, got_e)
-    got = lax.ppermute(msg, "rows", down)
-    (out,) = call(final_kernel, [(rows, cols)], edge, keep, got, partial)
-    return out
+    got = lax.ppermute(msg, "rows", on_chip)
+    return pl.pallas_call(
+        final_kernel,
+        out_shape=jax.ShapeDtypeStruct((rows, cols), jnp.float32),
+        in_specs=[pl.BlockSpec(memory_space=pltpu.VMEM)] * 4,
+        out_specs=pl.BlockSpec(memory_space=pl.ANY),
+        scratch_shapes=[pltpu.VMEM((4, rows, cols // 4), jnp.float32), pltpu.SemaphoreType.DMA((4,))],
+        compiler_params=pltpu.CompilerParams(vmem_limit_bytes=16 * 1024 * 1024),
+    )(edge, keep, got, partial)
 
 
 def solution(mesh):

time: 52.4 us -> 45.9 us (0.88)
  the two profiles are of different devices: /device:TPU:8 before, /device:TPU:1 now
where the time goes in v3:
time: 45.9 us; the launch traced here: 45.7 us
  starting transfers between devices  22.9 us (50%)
  waiting for transfers between devices  11 us (24%)
  Pallas kernels  9.69 us (21%)
  local copies, waits for them, and re-layouts  1.95 us (4%)
    pallas_call x12, Pallas kernels, call(): pl.pallas_call(kernel, out_shape=[jax.ShapeDtypeStruct(s, jnp.float32) if...  8.25 us
    ppermute x1, starting transfers between devices, per_device(): other = lax.ppermute(reflectors, 'cols', [(0, 1), (1, 0)])  7.73 us
    ppermute x2, waiting for transfers between devices, per_device(): got_e = lax.ppermute(e, 'rows', in_pair)  4.79 us
    ppermute x1, starting transfers between devices, per_device(): got_w = lax.ppermute(w, 'rows', in_pair)  3.95 us
    ppermute x2, starting transfers between devices, per_device(): got = lax.ppermute(msg, 'rows', on_chip)  3.62 us
    ppermute x2, starting transfers between devices, per_device(): got_e = lax.ppermute(e, 'rows', in_pair)  3.28 us
    ppermute x1, waiting for transfers between devices, per_device(): got = lax.ppermute(w, 'rows', w_pairs)  2.92 us
    unnamed x8, local copies, waits for them, and re-layouts  1.95 us
  transfers between devices with their start and end apart: 10, of which 6 were waited for; matrix products, arithmetic and copies ran while one was open for 0% of the time, Pallas kernels for 8%

profile of v3, /device:TPU:1, one launch (start us, length us, event | category | flops | bytes accessed | tf_op | source)
XLA Modules:
  0.0 45.7 jit_solution(1183924449620874642)
XLA Ops:
  0.0 0.0 copy-start.3
  0.0 7.7 %collective-permute-start = (f32[16,256]{1,0:T(8,128)}, f32[16,256]{1,0:T(8,128)S(1)}, u32[]{:S(2)}, u32[]{:S(2)}) collective-permute-start(f32[16,256]{1,0:T(8,128)} %own_ref.1), channel_id=1, source_target_pairs={{0,1},{1,0},{2,3},{3,2},{4,5},{5,4},{6,7},{7,6},{8,9},{9,8},{10,11... | collective-permute-start | bytes 49160 | tf_op jit(solution)/shard_map/ppermute | solution.py:296
  7.7 0.0 copy-done.3
  7.7 0.0 copy-start
  7.7 1.2 %copy-done = f32[256,1024]{1,0:T(8,128)S(1)} copy-done((f32[256,1024]{1,0:T(8,128)S(1)}, f32[256,1024]{1,0:T(8,128)}, u32[]{:S(2)}) %copy-start) | copy-done | bytes 1048600
  9.0 0.0 copy-start.2
  9.0 0.7 %copy-done.2 = f32[16,256]{1,0:T(8,128)S(1)} copy-done((f32[16,256]{1,0:T(8,128)S(1)}, f32[16,256]{1,0:T(8,128)}, u32[]{:S(2)}) %copy-start.2) | copy-done | bytes 16408
  9.7 0.3 shard_map.37
  10.0 0.0 collective-permute-done.other_ref
  10.0 2.2 %shard_map.38 = (f32[64,1152]{1,0:T(8,128)S(1)}, f32[96,256]{1,0:T(8,128)S(1)}, f32[96,256]{1,0:T(8,128)S(1)}, f32[64,256]{1,0:T(8,128)S(1)}) custom-call(f32[16,256]{1,0:T(8,128)S(1)} %get-tuple-element.30.own_ref, f32[16,256]{1,0:T(8,128)S(1)} %collective-permute-done.other_ref, f32[32,128]{1,0:T(8,128)S(1)} %get-tuple-element.31.start_ref, ...), custom_call_target="tpu_custom_call" | custom-call | flops 1000000 | bytes 2146304 | tf_op jit(solution)/shard_map/pallas_call | solution.py:29
  12.2 1.2 %collective-permute-start.1 = (f32[64,1152]{1,0:T(8,128)S(1)}, f32[64,1152]{1,0:T(8,128)S(1)}, u32[]{:S(2)}, u32[]{:S(2)}) collective-permute-start(f32[64,1152]{1,0:T(8,128)S(1)} %get-tuple-element.35.own_ref), channel_id=1, source_target_pairs={{0,2},{2,0},{4,6},{6,4},{8,10},{10,8},{12,14},{14,12},{16,18},{18,... | collective-permute-start | bytes 884744 | tf_op jit(solution)/shard_map/ppermute | solution.py:306
  13.4 1.2 %collective-permute-done.1.got_ref = f32[64,1152]{1,0:T(8,128)S(1)} collective-permute-done((f32[64,1152]{1,0:T(8,128)S(1)}, f32[64,1152]{1,0:T(8,128)S(1)}, u32[]{:S(2)}, u32[]{:S(2)}) %collective-permute-start.1) | collective-permute-done | bytes 294944 | tf_op jit(solution)/shard_map/ppermute | solution.py:306
  14.6 1.3 %shard_map.39 = (f32[32,1152]{1,0:T(8,128)S(1)}, f32[32,1152]{1,0:T(8,128)S(1)}, f32[32,1152]{1,0:T(8,128)S(1)}) custom-call(f32[64,1152]{1,0:T(8,128)S(1)} %get-tuple-element.35.own_ref, f32[64,1152]{1,0:T(8,128)S(1)} %collective-permute-done.1.got_ref), custom_call_target="tpu_custom_call" | custom-call | flops 1000000 | bytes 589824 | tf_op jit(solution)/shard_map/pallas_call | solution.py:29
  15.8 0.7 %collective-permute-start.2 = (f32[32,1152]{1,0:T(8,128)S(1)}, f32[32,1152]{1,0:T(8,128)S(1)}, u32[]{:S(2)}, u32[]{:S(2)}) collective-permute-start(f32[32,1152]{1,0:T(8,128)S(1)} %get-tuple-element.37.e_ref), channel_id=1, source_target_pairs={{0,16},{2,6},{4,20},{6,2},{8,24},{10,14},{12,28},{14,10},{16,0},{1... | collective-permute-start | bytes 442376 | tf_op jit(solution)/shard_map/ppermute | solution.py:308
  16.5 0.9 %collective-permute-start.4 = (f32[32,1152]{1,0:T(8,128)S(1)}, f32[32,1152]{1,0:T(8,128)S(1)}, u32[]{:S(2)}, u32[]{:S(2)}) collective-permute-start(f32[32,1152]{1,0:T(8,128)S(1)} %get-tuple-element.38.o_ref), channel_id=1, source_target_pairs={{0,16},{2,6},{4,20},{6,2},{8,24},{10,14},{12,28},{14,10},{16,0},{1... | collective-permute-start | bytes 442376 | tf_op jit(solution)/shard_map/ppermute | solution.py:309
  17.4 2.8 %collective-permute-done.2.got_ref = f32[32,1152]{1,0:T(8,128)S(1)} collective-permute-done((f32[32,1152]{1,0:T(8,128)S(1)}, f32[32,1152]{1,0:T(8,128)S(1)}, u32[]{:S(2)}, u32[]{:S(2)}) %collective-permute-start.2) | collective-permute-done | bytes 147488 | tf_op jit(solution)/shard_map/ppermute | solution.py:308
  20.2 0.8 %shard_map.40 = (f32[32,1152]{1,0:T(8,128)S(1)}, f32[32,1152]{1,0:T(8,128)S(1)}, f32[16,1280]{1,0:T(8,128)S(1)}) custom-call(f32[32,1152]{1,0:T(8,128)S(1)} %get-tuple-element.37.e_ref, f32[32,1152]{1,0:T(8,128)S(1)} %get-tuple-element.38.o_ref, f32[32,1152]{1,0:T(8,128)S(1)} %collective-permute-done.2.got_ref), custom_call_target="tpu_custom_call" | custom-call | flops 1000000 | bytes 442368 | tf_op jit(solution)/shard_map/pallas_call | solution.py:29
  21.0 1.2 %collective-permute-start.3 = (f32[16,1280]{1,0:T(8,128)S(1)}, f32[16,1280]{1,0:T(8,128)S(1)}, u32[]{:S(2)}, u32[]{:S(2)}) collective-permute-start(f32[16,1280]{1,0:T(8,128)S(1)} %get-tuple-element.39), channel_id=1, source_target_pairs={{0,16},{2,18},{4,20},{6,10},{8,24},{10,6},{12,28},{14,30},{16,0},{... | collective-permute-start | bytes 245768 | tf_op jit(solution)/shard_map/ppermute | solution.py:311
  22.2 0.0 collective-permute-done.4.got_ref
  22.2 0.4 shard_map.41.w_ref
  22.6 1.8 %collective-permute-done.3.msg_ref = f32[16,1280]{1,0:T(8,128)S(1)} collective-permute-done((f32[16,1280]{1,0:T(8,128)S(1)}, f32[16,1280]{1,0:T(8,128)S(1)}, u32[]{:S(2)}, u32[]{:S(2)}) %collective-permute-start.3) | collective-permute-done | bytes 81952 | tf_op jit(solution)/shard_map/ppermute | solution.py:311
  24.4 0.3 shard_map.42
  24.7 1.2 %collective-permute-start.5 = (f32[32,1152]{1,0:T(8,128)S(1)}, f32[32,1152]{1,0:T(8,128)S(1)}, u32[]{:S(2)}, u32[]{:S(2)}) collective-permute-start(f32[32,1152]{1,0:T(8,128)S(1)} %get-tuple-element.42.w_ref), channel_id=1, source_target_pairs={{0,4},{2,18},{4,0},{6,250},{8,12},{10,22},{12,8},{14,30},{16,20},{... | collective-permute-start | bytes 442376 | tf_op jit(solution)/shard_map/ppermute | solution.py:314
  25.9 2.9 %collective-permute-done.5.msg_ref = f32[32,1152]{1,0:T(8,128)S(1)} collective-permute-done((f32[32,1152]{1,0:T(8,128)S(1)}, f32[32,1152]{1,0:T(8,128)S(1)}, u32[]{:S(2)}, u32[]{:S(2)}) %collective-permute-start.5) | collective-permute-done | bytes 147488 | tf_op jit(solution)/shard_map/ppermute | solution.py:314
  28.8 0.5 %shard_map.43 = (f32[32,1024]{1,0:T(8,128)S(1)}, f32[16,1024]{1,0:T(8,128)S(1)}) custom-call(f32[32,1152]{1,0:T(8,128)S(1)} %collective-permute-done.5.msg_ref, f32[32,128]{1,0:T(8,128)S(1)} %get-tuple-element.31.start_ref, f32[32,1152]{1,0:T(8,128)S(1)} %get-tuple-element.42.w_ref, f32[32,1152]{1,0:T(8,128)S(1)} %get-tuple-element.40.p_ref, ...), custom_call_target="tpu_custom_call" | custom-call | flops 1000000 | bytes 524288 | tf_op jit(solution)/shard_map/pallas_call | solution.py:29
  29.3 0.0 copy-start.1
  29.3 1.2 %collective-permute-start.6 = (f32[16,1024]{1,0:T(8,128)S(1)}, f32[16,1024]{1,0:T(8,128)S(1)}, u32[]{:S(2)}, u32[]{:S(2)}) collective-permute-start(f32[16,1024]{1,0:T(8,128)S(1)} %get-tuple-element.44.rest_ref), channel_id=1, source_target_pairs={{0,16},{2,18},{4,20},{6,10},{8,24},{10,6},{12,28},{14,30},{16,0},{... | collective-permute-start | bytes 196616 | tf_op jit(solution)/shard_map/ppermute | solution.py:317
  30.5 4.0 %collective-permute-start.7 = (f32[32,1024]{1,0:T(8,128)S(1)}, f32[32,1024]{1,0:T(8,128)S(1)}, u32[]{:S(2)}, u32[]{:S(2)}) collective-permute-start(f32[32,1024]{1,0:T(8,128)S(1)} %get-tuple-element.46.w_ref), channel_id=1, source_target_pairs={{0,16},{2,6},{4,20},{6,2},{8,24},{10,14},{12,28},{14,10},{16,0},{1... | collective-permute-start | bytes 393224 | tf_op jit(solution)/shard_map/ppermute | solution.py:318
  34.5 0.5 %shard_map.44.known_ref = f32[32,1024]{1,0:T(8,128)S(1)} custom-call(f32[32,1152]{1,0:T(8,128)S(1)} %get-tuple-element.41.pair_ref, f32[32,1024]{1,0:T(8,128)S(1)} %get-tuple-element.46.w_ref, f32[16,1024]{1,0:T(8,128)S(1)} %get-tuple-element.43.p0_ref), custom_call_target="tpu_custom_call" | custom-call | flops 1000000 | bytes 344064 | tf_op jit(solution)/shard_map/pallas_call | solution.py:29
  35.0 0.0 collective-permute-done.6.msg_ref
  35.0 0.3 shard_map.45
  35.3 2.6 %collective-permute-start.8 = (f32[32,1024]{1,0:T(8,128)S(1)}, f32[32,1024]{1,0:T(8,128)S(1)}, u32[]{:S(2)}, u32[]{:S(2)}) collective-permute-start(f32[32,1024]{1,0:T(8,128)S(1)} %get-tuple-element.50.e_ref), channel_id=1, source_target_pairs={{0,16},{2,6},{4,20},{6,2},{8,24},{10,14},{12,28},{14,10},{16,0},{1... | collective-permute-start | bytes 393224 | tf_op jit(solution)/shard_map/ppermute | solution.py:321
  37.9 0.0 collective-permute-done.7.got_ref
  37.9 0.4 shard_map.46
  38.3 2.0 %collective-permute-done.8.got_ref = f32[32,1024]{1,0:T(8,128)S(1)} collective-permute-done((f32[32,1024]{1,0:T(8,128)S(1)}, f32[32,1024]{1,0:T(8,128)S(1)}, u32[]{:S(2)}, u32[]{:S(2)}) %collective-permute-start.8) | collective-permute-done | bytes 131104 | tf_op jit(solution)/shard_map/ppermute | solution.py:321
  40.3 0.4 shard_map.47
  40.7 2.4 %collective-permute-start.9 = (f32[64,1024]{1,0:T(8,128)S(1)}, f32[64,1024]{1,0:T(8,128)S(1)}, u32[]{:S(2)}, u32[]{:S(2)}) collective-permute-start(f32[64,1024]{1,0:T(8,128)S(1)} %get-tuple-element.52), channel_id=1, source_target_pairs={{0,2},{2,0},{4,6},{6,4},{8,10},{10,8},{12,14},{14,12},{16,18},{18,... | collective-permute-start | bytes 786440 | tf_op jit(solution)/shard_map/ppermute | solution.py:324
  43.1 0.0 copy-done.1
  43.1 0.9 %shard_map.48.y_ref = f32[256,1024]{1,0:T(8,128)S(1)} custom-call(f32[96,256]{1,0:T(8,128)S(1)} %get-tuple-element.53.inner_ref, f32[96,256]{1,0:T(8,128)S(1)} %get-tuple-element.54.proj_ref, bf16[256,1024]{1,0:T(8,128)(2,1)S(1)} %get-tuple-element.32.high_ref, bf16[256,1024]{1,0:T(8,128)(2,1)S(1)} %get-tuple-element.33.low_ref, f32[256,1024]{1,0:T(8,128)S(1)} %copy-done.1), custom_call_target="tpu_custom_call" | custom-call | flops 20000000 | bytes 3342336 | tf_op jit(solution)/shard_map/pallas_call | solution.py:29
  44.0 0.3 collective-permute-done.9.msg_ref
  44.3 1.4 %shard_map.49 = f32[256,1024]{1,0:T(8,128)} custom-call(f32[64,256]{1,0:T(8,128)S(1)} %get-tuple-element.34.edge_ref, f32[64,1024]{1,0:T(8,128)S(1)} %get-tuple-element.51.keep_ref, f32[64,1024]{1,0:T(8,128)S(1)} %collective-permute-done.9.msg_ref, f32[256,1024]{1,0:T(8,128)S(1)} %shard_map.48.y_ref), custom_call_target="tpu_custom_call" | custom-call | tf_op jit(solution)/shard_map/pallas_call | solution.py:325
Async XLA Ops:
  0.0 7.7 %copy-start.3 = (s32[32]{0:T(128)S(1)}, s32[32]{0:T(128)}, u32[]{:S(2)}) copy-start(s32[32]{0:T(128)} %param.5) | copy-start | bytes 388
  0.0 10.0 %collective-permute-start = (f32[16,256]{1,0:T(8,128)}, f32[16,256]{1,0:T(8,128)S(1)}, u32[]{:S(2)}, u32[]{:S(2)}) collective-permute-start(f32[16,256]{1,0:T(8,128)} %own_ref.1), channel_id=1, source_target_pairs={{0,1},{1,0},{2,3},{3,2},{4,5},{5,4},{6,7},{7,6},{8,9},{9,8},{10,11... | collective-permute-start | bytes 49160 | tf_op jit(solution)/shard_map/ppermute | solution.py:296
  7.7 1.2 %copy-start = (f32[256,1024]{1,0:T(8,128)S(1)}, f32[256,1024]{1,0:T(8,128)}, u32[]{:S(2)}) copy-start(f32[256,1024]{1,0:T(8,128)} %x_ref.3) | copy-start | bytes 3145732
  9.0 0.7 %copy-start.2 = (f32[16,256]{1,0:T(8,128)S(1)}, f32[16,256]{1,0:T(8,128)}, u32[]{:S(2)}) copy-start(f32[16,256]{1,0:T(8,128)} %own_ref.1) | copy-start | bytes 49156
  12.2 2.4 %collective-permute-start.1 = (f32[64,1152]{1,0:T(8,128)S(1)}, f32[64,1152]{1,0:T(8,128)S(1)}, u32[]{:S(2)}, u32[]{:S(2)}) collective-permute-start(f32[64,1152]{1,0:T(8,128)S(1)} %get-tuple-element.35.own_ref), channel_id=1, source_target_pairs={{0,2},{2,0},{4,6},{6,4},{8,10},{10,8},{12,14},{14,12},{16,18},{18,... | collective-permute-start | bytes 884744 | tf_op jit(solution)/shard_map/ppermute | solution.py:306
  15.8 4.4 %collective-permute-start.2 = (f32[32,1152]{1,0:T(8,128)S(1)}, f32[32,1152]{1,0:T(8,128)S(1)}, u32[]{:S(2)}, u32[]{:S(2)}) collective-permute-start(f32[32,1152]{1,0:T(8,128)S(1)} %get-tuple-element.37.e_ref), channel_id=1, source_target_pairs={{0,16},{2,6},{4,20},{6,2},{8,24},{10,14},{12,28},{14,10},{16,0},{1... | collective-permute-start | bytes 442376 | tf_op jit(solution)/shard_map/ppermute | solution.py:308
  16.5 5.6 %collective-permute-start.4 = (f32[32,1152]{1,0:T(8,128)S(1)}, f32[32,1152]{1,0:T(8,128)S(1)}, u32[]{:S(2)}, u32[]{:S(2)}) collective-permute-start(f32[32,1152]{1,0:T(8,128)S(1)} %get-tuple-element.38.o_ref), channel_id=1, source_target_pairs={{0,16},{2,6},{4,20},{6,2},{8,24},{10,14},{12,28},{14,10},{16,0},{1... | collective-permute-start | bytes 442376 | tf_op jit(solution)/shard_map/ppermute | solution.py:309
  21.0 3.4 %collective-permute-start.3 = (f32[16,1280]{1,0:T(8,128)S(1)}, f32[16,1280]{1,0:T(8,128)S(1)}, u32[]{:S(2)}, u32[]{:S(2)}) collective-permute-start(f32[16,1280]{1,0:T(8,128)S(1)} %get-tuple-element.39), channel_id=1, source_target_pairs={{0,16},{2,18},{4,20},{6,10},{8,24},{10,6},{12,28},{14,30},{16,0},{... | collective-permute-start | bytes 245768 | tf_op jit(solution)/shard_map/ppermute | solution.py:311
  24.7 4.1 %collective-permute-start.5 = (f32[32,1152]{1,0:T(8,128)S(1)}, f32[32,1152]{1,0:T(8,128)S(1)}, u32[]{:S(2)}, u32[]{:S(2)}) collective-permute-start(f32[32,1152]{1,0:T(8,128)S(1)} %get-tuple-element.42.w_ref), channel_id=1, source_target_pairs={{0,4},{2,18},{4,0},{6,250},{8,12},{10,22},{12,8},{14,30},{16,20},{... | collective-permute-start | bytes 442376 | tf_op jit(solution)/shard_map/ppermute | solution.py:314
  29.3 13.8 %copy-start.1 = (f32[256,1024]{1,0:T(8,128)S(1)}, f32[256,1024]{1,0:T(8,128)}, u32[]{:S(2)}) copy-start(f32[256,1024]{1,0:T(8,128)} %x_ref.3) | copy-start | bytes 3145732
  29.3 5.6 %collective-permute-start.6 = (f32[16,1024]{1,0:T(8,128)S(1)}, f32[16,1024]{1,0:T(8,128)S(1)}, u32[]{:S(2)}, u32[]{:S(2)}) collective-permute-start(f32[16,1024]{1,0:T(8,128)S(1)} %get-tuple-element.44.rest_ref), channel_id=1, source_target_pairs={{0,16},{2,18},{4,20},{6,10},{8,24},{10,6},{12,28},{14,30},{16,0},{... | collective-permute-start | bytes 196616 | tf_op jit(solution)/shard_map/ppermute | solution.py:317
  30.5 7.4 %collective-permute-start.7 = (f32[32,1024]{1,0:T(8,128)S(1)}, f32[32,1024]{1,0:T(8,128)S(1)}, u32[]{:S(2)}, u32[]{:S(2)}) collective-permute-start(f32[32,1024]{1,0:T(8,128)S(1)} %get-tuple-element.46.w_ref), channel_id=1, source_target_pairs={{0,16},{2,6},{4,20},{6,2},{8,24},{10,14},{12,28},{14,10},{16,0},{1... | collective-permute-start | bytes 393224 | tf_op jit(solution)/shard_map/ppermute | solution.py:318
  35.3 5.0 %collective-permute-start.8 = (f32[32,1024]{1,0:T(8,128)S(1)}, f32[32,1024]{1,0:T(8,128)S(1)}, u32[]{:S(2)}, u32[]{:S(2)}) collective-permute-start(f32[32,1024]{1,0:T(8,128)S(1)} %get-tuple-element.50.e_ref), channel_id=1, source_target_pairs={{0,16},{2,6},{4,20},{6,2},{8,24},{10,14},{12,28},{14,10},{16,0},{1... | collective-permute-start | bytes 393224 | tf_op jit(solution)/shard_map/ppermute | solution.py:321
  40.7 3.6 %collective-permute-start.9 = (f32[64,1024]{1,0:T(8,128)S(1)}, f32[64,1024]{1,0:T(8,128)S(1)}, u32[]{:S(2)}, u32[]{:S(2)}) collective-permute-start(f32[64,1024]{1,0:T(8,128)S(1)} %get-tuple-element.52), channel_id=1, source_target_pairs={{0,2},{2,0},{4,6},{6,4},{8,10},{10,8},{12,14},{14,12},{16,18},{18,... | collective-permute-start | bytes 786440 | tf_op jit(solution)/shard_map/ppermute | solution.py:324

commit v4 on v3

v4 whole, which is shorter than its diff:
```python
import jax
import jax.numpy as jnp
from jax import lax
from jax.experimental import pallas as pl
from jax.experimental.pallas import tpu as pltpu
from jax.sharding import PartitionSpec as P


BAND = 64
SWEEPS = 32
LANES = 128


def dot(a, b, contract=((1,), (0,))):
    return lax.dot_general(
        a, b, (contract, ((), ())), precision=lax.Precision.HIGHEST, preferred_element_type=jnp.float32
    )


def lane_of(shape):
    return lax.broadcasted_iota(jnp.int32, shape, len(shape) - 1)


def row_of(shape):
    return lax.broadcasted_iota(jnp.int32, shape, 0)


def call(kernel, outs, *args, where=None, flops=1_000_000):
    def body(*refs):
        if where is None:
            kernel(*refs)
        else:
            pl.when(where())(lambda: kernel(*refs))

    nbytes = 4 * sum(a.size for a in args)
    return pl.pallas_call(
        body,
        out_shape=[jax.ShapeDtypeStruct(s, jnp.float32) if isinstance(s, tuple) else s for s in outs],
        in_specs=[pl.BlockSpec(memory_space=pltpu.VMEM)] * len(args),
        out_specs=[pl.BlockSpec(memory_space=pltpu.VMEM)] * len(outs),
        compiler_params=pltpu.CompilerParams(vmem_limit_bytes=16 * 1024 * 1024),
        cost_estimate=pl.CostEstimate(flops=flops, bytes_accessed=nbytes, transcendentals=0),
    )(*args)


def chip_of():
    return lax.axis_index("rows") // 2


def is_north():
    return lax.axis_index("rows") % 2 == 1


def is_inside():
    index = lax.axis_index("rows")
    place = (index // 2) % 4
    return (index % 2 == 1) & ((place == 1) | (place == 2))


def split(a):
    high = a.astype(jnp.bfloat16)
    return high, (a - high.astype(jnp.float32)).astype(jnp.bfloat16)


def dot3(a, b, contract=((1,), (0,))):
    (ah, al), (bh, bl) = split(a), b if isinstance(b, tuple) else split(b)

    def one(x, y):
        return lax.dot_general(x, y, (contract, ((), ())), preferred_element_type=jnp.float32)

    return one(ah, bh) + (one(ah, bl) + one(al, bh))


def ready_kernel(x_ref, start_ref, high_ref, low_ref, column_ref):
    high_ref[...], low_ref[...] = split(x_ref[...])
    square = (SWEEPS, SWEEPS)
    row = start_ref[...].astype(jnp.float32)
    column = jnp.sum(jnp.where(lane_of(square) == row_of(square), row, 0.0), axis=1, keepdims=True)
    column_ref[...] = jnp.broadcast_to(column, (SWEEPS, LANES))


def factor_kernel(own_ref, other_ref, start_ref, high_ref, low_ref, msg_ref, inner_ref, edge_ref, solved_ref):
    first = lax.axis_index("cols") == 0
    own, other = own_ref[...], other_ref[...]
    r = jnp.concatenate([jnp.where(first, own, other), jnp.where(first, other, own)], axis=0)
    rows = r.shape[1]
    start = start_ref[:, 0:1].astype(jnp.int32)
    segment = (lane_of(r.shape) - start + BAND) >> 6
    parts = [jnp.where(segment == k, r, 0.0) for k in range(5)]
    zero = jnp.zeros_like(r)
    inner = jnp.concatenate(parts[1:4], axis=0)
    edge = jnp.concatenate([parts[0], parts[4]], axis=0)
    left = jnp.concatenate([inner, zero, edge], axis=0)
    right = jnp.concatenate([inner, zero, edge, zero, zero], axis=0)
    gram = dot3(left, right, ((1,), (1,)))
    earlier = (lane_of(gram.shape) & (SWEEPS - 1)) < (row_of(gram.shape) & (SWEEPS - 1))
    gram = jnp.where(earlier, gram, 0.0)
    count = 3 * SWEEPS
    tau = 2.0 / jnp.sum(inner * inner, axis=1, keepdims=True)
    lower = tau * gram[0:count, 0:LANES]
    rhs = tau * jnp.concatenate([inner, gram[0:count, LANES : 2 * LANES]], axis=1)
    blocks = [[rhs[32 * k + 8 * q : 32 * k + 8 * q + 8] for q in range(4)] for k in range(3)]
    for j in range(SWEEPS - 1):
        source = [blocks[k][j // 8][j % 8 : j % 8 + 1] for k in range(3)]
        for k in range(3):
            for q in range((j + 1) // 8, 4):
                at = 32 * k + 8 * q
                total = blocks[k][q]
                for m in range(3):
                    if abs(m - k) < 2:
                        column = 32 * m + j
                        total = total - lower[at : at + 8, column : column + 1] * source[m]
                blocks[k][q] = total
    solved = jnp.concatenate([blocks[k][q] for k in range(3) for q in range(4)] + [jnp.zeros((32, rhs.shape[1]), jnp.float32)], axis=0)
    back = dot3(gram[LANES : LANES + 64, 0:LANES], solved)
    observe = edge - back[:, 0:rows]
    couple = back[:, rows:] - gram[LANES : LANES + 64, LANES : 2 * LANES]
    squares = jnp.sum(edge * edge, axis=1, keepdims=True)
    coef = jnp.where(lane_of(couple.shape) == 64, squares, couple)
    inner_ref[...] = inner
    edge_ref[...] = edge
    solved_ref[...] = solved[0:count]
    msg_ref[...] = jnp.concatenate([dot3(observe, (high_ref[...], low_ref[...])), coef], axis=1)


def to_low(tile):
    return jnp.where(lane_of(tile.shape) < 32, pltpu.roll(tile, LANES - 32, 1), 0.0)


def solve(blocks, lower, lane=0):
    for j in range(SWEEPS):
        source = blocks[j // 8][j % 8 : j % 8 + 1]
        for q in range((j + 1) // 8, len(blocks)):
            blocks[q] = blocks[q] + lower[8 * q : 8 * q + 8, lane + j : lane + j + 1] * source
    return jnp.concatenate(blocks, axis=0)


def spread(rows, tile, at, solved, lane, first=0, reach=1):
    blocks = [rows[8 * q : 8 * q + 8] for q in range(rows.shape[0] // 8)]
    for j in range(solved.shape[0]):
        for q in range(len(blocks)):
            top = at + 8 * q
            if top + 7 >= first + j + reach:
                column = lane + first + j
                blocks[q] = blocks[q] + tile[top : top + 8, column : column + 1] * solved[j : j + 1]
    return blocks[0] if len(blocks) == 1 else jnp.concatenate(blocks, axis=0)


def substitute(block, lower, first, lane):
    for j in range(block.shape[0] - 1):
        block = block + lower[first : first + block.shape[0], lane + first + j : lane + first + j + 1] * block[j : j + 1]
    return block


def merge_kernel(own_ref, got_ref, mid_ref, first_ref, rest_ref):
    even = chip_of() % 2 == 0
    cols = own_ref.shape[1] - LANES
    top, low = got_ref[...], own_ref[...]
    tc, lc = top[:, cols:], low[:, cols:]
    tau = 2.0 / (tc[32:64, 64:65] + lc[0:32, 64:65])
    lane = lane_of(tc.shape)
    tk = jnp.where(lane < 32, tc, 0.0)
    lk = jnp.where((lane >= 32) & (lane < 64), lc, 0.0)
    mid = jnp.concatenate([top[32:64, 0:cols] + low[0:32, 0:cols], tk[32:64] + lk[0:32]], axis=1) * tau
    left = jnp.concatenate([top[0:32, 0:cols], tk[0:32]], axis=1)
    right = jnp.concatenate([low[32:64, 0:cols], lk[32:64]], axis=1)
    weights = (pltpu.roll(tc[32:64], LANES - 32, 1) + lc[0:32]) * tau
    mid = solve([mid[8 * q : 8 * q + 8] for q in range(4)], weights)
    left = spread(left, tc[0:32], 0, mid, 32, reach=4)
    right = spread(right, lc[32:64], 0, mid, 0, reach=4)

    def ordered(block):
        tile = block[:, cols:]
        at = lane_of(tile.shape)
        swapped = jnp.where(at < 32, pltpu.roll(tile, 96, 1), pltpu.roll(tile, 32, 1))
        return jnp.where(at < 64, jnp.where(even, swapped, tile), 0.0)

    spot = lane_of((32, LANES)) == 64
    left = jnp.concatenate([left[:, 0:cols], jnp.where(spot, tc[0:32, 64:65], ordered(left))], axis=1)
    right = jnp.concatenate([right[:, 0:cols], jnp.where(spot, lc[32:64, 64:65], ordered(right))], axis=1)
    mid_ref[...] = jnp.concatenate([mid[:, 0:cols], ordered(mid)], axis=1)
    e = jnp.where(even, right, left)
    first_ref[...] = e[0:8]
    rest_ref[...] = jnp.concatenate([e[8:32], jnp.where(even, left, right)], axis=0)


def pair_kernel(first_ref, rest_ref, got_ref, msg_ref):
    cols = first_ref.shape[1] - LANES
    both = first_ref[...] + got_ref[...]
    tau = 2.0 / both[:, cols + 64 : cols + 65]
    e = substitute(both[:, 0:cols] * tau, tau * both[:, cols:], 0, 0)
    tile = rest_ref[24:56, cols:]
    p = spread(rest_ref[24:40, 0:cols], tile, 0, e, 0, reach=8)
    msg_ref[...] = jnp.concatenate([p, tile[0:16], tile[16:32]], axis=1)


def edges_kernel(first_ref, rest_ref, got_first_ref, got_rest_ref, pair_ref, p_ref, w_ref):
    cols = first_ref.shape[1] - LANES
    own = jnp.concatenate([first_ref[...], rest_ref[0:24]], axis=0)
    got = jnp.concatenate([got_first_ref[...], got_rest_ref[0:24]], axis=0)
    mine, theirs = own[:, cols:], got[:, cols:]
    tau = 2.0 / (mine[:, 64:65] + theirs[:, 64:65])
    lane = lane_of(mine.shape)
    upper = (lane >= 32) & (lane < 64)
    outer = to_low(theirs) + jnp.where(upper, mine, 0.0)
    pair = jnp.concatenate([own[:, 0:cols] + got[:, 0:cols], outer], axis=1) * tau
    pair = solve([pair[8 * q : 8 * q + 8] for q in range(4)], tau * (mine + theirs))
    pair_ref[...] = pair
    tile = rest_ref[40:56, cols:]
    p = jnp.concatenate([rest_ref[40:56, 0:cols], jnp.where((lane_of(tile.shape) >= 32) & (lane_of(tile.shape) < 64), tile, 0.0)], axis=1)
    p_ref[...] = spread(p, rest_ref[24:56, cols:], 16, pair[0:24], 0, reach=8)
    tile = got_rest_ref[24:56, cols:]
    w = jnp.concatenate([got_rest_ref[24:56, 0:cols], to_low(tile) + jnp.where(lane == 64, tile, 0.0)], axis=1)
    w_ref[...] = spread(w, tile, 0, pair[0:24], 0, reach=8)


def p0_kernel(msg_ref, own_ref, w_ref, p0_ref, scaled_ref, out_ref):
    cols = w_ref.shape[1] - LANES
    both = own_ref[...] + msg_ref[...]
    tile = jnp.concatenate([both[:, cols : cols + LANES], both[:, cols + LANES :]], axis=0)
    tau = 2.0 / tile[:, 64:65]
    lower = tau * tile
    scaled_ref[...] = jnp.where(lane_of(lower.shape) == 64, tau, lower)
    p0 = substitute(both[:, 0:cols] * tau[0:16], lower, 0, 32)
    p0_ref[...] = p0
    tile = w_ref[:, cols:]
    w = jnp.concatenate([w_ref[0:16, 0:cols], spread(w_ref[16:32, 0:cols], tile, 16, p0, 32, reach=16)], axis=0)
    out_ref[...] = jnp.concatenate([w, tile], axis=1)


def w_kernel(msg_ref, start_ref, w_ref, p_ref, p0_ref, out_w_ref, out_ref):
    cols = w_ref.shape[1] - LANES
    chip = chip_of()
    chips = lax.axis_size("rows") // 2
    start = start_ref[:, 0:1]
    valid = (chip != 1) & ((chip != chips - 2) | (start == 0.0))
    got = jnp.where((chip != 1) & (chip != chips - 2), msg_ref[...], 0.0)
    both = w_ref[...] + got
    squares = both[:, cols + 64 : cols + 65]
    tau = jnp.where(valid, 2.0 / jnp.where(valid, squares, 1.0), 0.0)
    w = both[:, 0:cols] * tau
    w = solve([w[8 * q : 8 * q + 8] for q in range(4)], tau * both[:, cols:])
    out_w_ref[...] = w
    tile = jnp.concatenate([p_ref[:, cols:], p_ref[:, cols:]], axis=0)
    rest = spread(p_ref[:, 0:cols], tile, 16, p0_ref[...], 32)
    out_ref[...] = spread(rest, tile, 16, w[0:16], 0, reach=16)


def e0_kernel(pair_ref, w_ref, p0_ref, out_ref, tail_ref):
    cols = w_ref.shape[1]
    tile = pair_ref[:, cols:]
    w = w_ref[...]
    e = spread(pair_ref[:, 0:cols], tile, 0, w[0:24], 0, reach=8)
    e = spread(e, tile, 0, p0_ref[...], 32, reach=8)
    out_ref[...] = jnp.concatenate([w, e[0:24]], axis=0)
    tail_ref[...] = e[24:32]


def p1_kernel(msg_ref, scaled_ref, rest_ref, pair_ref, tail_ref, p0_ref, p_ref, out_ref):
    cols = msg_ref.shape[1]
    scaled = scaled_ref[...]
    p1 = substitute((rest_ref[...] + msg_ref[...]) * scaled[16:32, 64:65], scaled, 16, 32)
    p_ref[...] = jnp.concatenate([p0_ref[...], p1], axis=0)
    out_ref[...] = spread(tail_ref[...], pair_ref[:, cols:], 24, p1[0:8], 32, first=16, reach=8)


def mid_kernel(mid_ref, p_ref, own_ref, got_ref, part_ref, o_ref, e_ref):
    cols = p_ref.shape[1]
    inside = is_inside()
    o = jnp.where(inside, p_ref[...], got_ref[0:32])
    e = jnp.where(inside, own_ref[32:56], got_ref[32:56])
    tile = mid_ref[:, cols:]
    o_ref[...] = o
    e_ref[...] = e
    part_ref[...] = spread(spread(mid_ref[:, 0:cols], tile, 0, e, 0, reach=4), tile, 0, o, 32, reach=4)


def back_kernel(mid_ref, part_ref, o_ref, e_ref, own_ref, got_ref, keep_ref, out_ref):
    cols = o_ref.shape[1]
    even = chip_of() % 2 == 0
    tail = jnp.where(is_inside(), own_ref[...], got_ref[...])
    last = spread(part_ref[24:32], mid_ref[:, cols:], 24, tail, 0, first=24, reach=4)
    for q in range(4):
        at = slice(8 * q, 8 * q + 8)
        below = slice(32 + 8 * q, 40 + 8 * q)
        e = tail if q == 3 else e_ref[at]
        mid = last if q == 3 else part_ref[at]
        o = o_ref[at]
        out_ref[at] = jnp.where(even, o, e)
        out_ref[below] = mid
        keep_ref[at] = mid
        keep_ref[below] = jnp.where(even, e, o)


def inner_kernel(inner_ref, edge_ref, solved_ref, high_ref, low_ref, x_ref, y_ref, lhs_ref):
    rows = x_ref.shape[0]
    inner = inner_ref[...]
    part = dot3(solved_ref[:, 0:rows], (high_ref[...], low_ref[...]))
    y_ref[...] = x_ref[...] - dot3(inner, part, ((0,), (0,)))
    edge = edge_ref[...] - dot(solved_ref[:, rows : rows + 64], inner, ((0,), (0,)))
    high = edge.astype(jnp.bfloat16).astype(jnp.float32)
    stack = jnp.concatenate([high, high, edge - high, jnp.zeros_like(edge)], axis=0)
    lhs_ref[...] = stack.T.astype(jnp.bfloat16)


def final_kernel(lhs_ref, keep_ref, msg_ref, y_ref, out_ref, piece_ref, sems):
    north = is_north()
    lhs = lhs_ref[...]
    width = piece_ref.shape[2]
    copies = []
    for i in range(piece_ref.shape[0]):
        at = slice(i * width, (i + 1) * width)
        high, low = split(jnp.where(north, keep_ref[:, at], msg_ref[:, at]))
        rhs = jnp.concatenate([high, low, high, jnp.zeros_like(high)], axis=0)
        piece_ref[i] = y_ref[:, at] - jnp.dot(lhs, rhs, preferred_element_type=jnp.float32)
        copy = pltpu.make_async_copy(piece_ref.at[i], out_ref.at[:, at], sems.at[i])
        copy.start()
        copies.append(copy)
    for copy in copies:
        copy.wait()


def trade(array, pairs):
    return lax.ppermute(array, "rows", pairs)


def per_device(eigvecs, reflectors, starts):
    count = lax.axis_size("rows")
    chips = count // 2
    rows, cols = eigvecs.shape
    wide = cols + LANES

    far = 32 if count >= 64 else 8

    def swap(pick):
        return [(i, pick(i, i // 2, i % 2 == 1, (i // 2) % 4 in (1, 2))) for i in range(count)]

    def next_quad(i, chip, north, inside):
        end = chip < 2 or chip >= chips - 2
        if end and not inside:
            return None if north else i + 3 if chip == 0 else i - 1
        if north and inside:
            return i - 3 if chip == 1 else i + 1 if end else i + 6 if chip % 4 == 2 else i - 6
        return i ^ far if inside else i ^ 1

    on_chip = swap(lambda i, chip, north, inside: i ^ 1)
    in_pair = swap(lambda i, chip, north, inside: i ^ 2 if north else i ^ 8)
    p_pairs = swap(lambda i, chip, north, inside: (i ^ 6 if north else i ^ 8) if inside else i ^ 1)
    w_pairs = [
        (2 * i + c, 2 * i + 1 - c if j is None else 2 * j + c) for i, j in swap(next_quad) for c in range(2)
    ]
    other = lax.ppermute(reflectors, "cols", [(0, 1), (1, 0)])
    half = jax.ShapeDtypeStruct(eigvecs.shape, jnp.bfloat16)
    high, low, start = call(ready_kernel, [half, half, (SWEEPS, LANES)], eigvecs, starts[None, :], flops=20_000_000)
    msg, inner, edge, solved = call(
        factor_kernel, [(64, wide), (96, rows), (64, rows), (96, rows + LANES)], reflectors, other, start, high, low
    )
    got = lax.ppermute(msg, "rows", on_chip)
    mid, first, rest = call(merge_kernel, [(32, wide), (8, wide), (56, wide)], msg, got, where=is_north)
    got_first = trade(first, in_pair)
    got_rest = trade(rest, in_pair)
    (msg,) = call(pair_kernel, [(16, wide + LANES)], first, rest, got_first, where=is_inside)
    got = lax.ppermute(msg, "rows", p_pairs)
    pair, p, w = call(
        edges_kernel, [(32, wide), (16, wide), (32, wide)], first, rest, got_first, got_rest, where=is_inside
    )
    p0, scaled, w = call(p0_kernel, [(16, cols), (32, LANES), (32, wide)], got, msg, w, where=is_inside)
    got = lax.ppermute(w, ("rows", "cols"), w_pairs)
    partial, lhs = call(
        inner_kernel, [(rows, cols), jax.ShapeDtypeStruct((rows, 256), jnp.bfloat16)],
        inner, edge, solved, high, low, eigvecs, flops=20_000_000,
    )
    w, rest = call(w_kernel, [(32, cols), (16, cols)], got, start, w, p, p0, where=is_inside)
    got = trade(rest, p_pairs)
    most, tail = call(e0_kernel, [(56, cols), (8, cols)], pair, w, p0, where=is_inside)
    got_most = trade(most, in_pair)
    p, tail = call(p1_kernel, [(32, cols), (8, cols)], got, scaled, rest, pair, tail, p0, where=is_inside)
    got = lax.ppermute(tail, "rows", in_pair)
    part, o, e = call(mid_kernel, [(32, cols), (32, cols), (24, cols)], mid, p, most, got_most, where=is_north)
    keep, msg = call(back_kernel, [(64, cols), (64, cols)], mid, part, o, e, tail, got, where=is_north)
    got = lax.ppermute(msg, "rows", on_chip)
    return pl.pallas_call(
        final_kernel,
        out_shape=jax.ShapeDtypeStruct((rows, cols), jnp.float32),
        in_specs=[pl.BlockSpec(memory_space=pltpu.VMEM)] * 4,
        out_specs=pl.BlockSpec(memory_space=pl.ANY),
        scratch_shapes=[pltpu.VMEM((4, rows, cols // 4), jnp.float32), pltpu.SemaphoreType.DMA((4,))],
        compiler_params=pltpu.CompilerParams(vmem_limit_bytes=16 * 1024 * 1024),
    )(lhs, keep, got, partial)


def solution(mesh):
    in_specs = (P("rows", "cols"), P("cols", "rows"), P())
    out_specs = P("rows", "cols")

    return jax.shard_map(per_device, mesh=mesh, in_specs=in_specs, out_specs=out_specs, check_vma=False)
```

time: 45.9 us -> 42.1 us (0.917)
  the two profiles are of different devices: /device:TPU:1 before, /device:TPU:37 now
where the time goes in v4:
time: 42.1 us; the launch traced here: 41.9 us
  starting transfers between devices  16.8 us (40%)
  waiting for transfers between devices  15.2 us (36%)
  Pallas kernels  8.11 us (19%)
  local copies, waits for them, and re-layouts  1.66 us (4%)
    ppermute x4, waiting for transfers between devices, trade(): return lax.ppermute(array, 'rows', pairs)  7.69 us
    pallas_call x12, Pallas kernels, call(): pl.pallas_call(body, out_shape=[jax.ShapeDtypeStruct(s, jnp.float32) if i...  6.87 us
    ppermute x1, starting transfers between devices, per_device(): other = lax.ppermute(reflectors, 'cols', [(0, 1), (1, 0)])  6.01 us
    ppermute x2, starting transfers between devices, per_device(): got = lax.ppermute(msg, 'rows', on_chip)  4.92 us
    ppermute x1, waiting for transfers between devices, per_device(): got = lax.ppermute(w, ('rows', 'cols'), w_pairs)  3.61 us
    ppermute x4, starting transfers between devices, trade(): return lax.ppermute(array, 'rows', pairs)  3.05 us
    unnamed x8, local copies, waits for them, and re-layouts  1.66 us
    ppermute x1, waiting for transfers between devices, per_device(): got = lax.ppermute(msg, 'rows', p_pairs)  1.58 us
  transfers between devices with their start and end apart: 10, of which 8 were waited for; matrix products, arithmetic and copies ran while one was open for 0% of the time, Pallas kernels for 7%

profile of v4, /device:TPU:37, one launch (start us, length us, event | category | flops | bytes accessed | tf_op | source)
XLA Modules:
  0.0 41.9 jit_solution(6296977402760942048)
XLA Ops:
  0.0 0.0 copy-start.3
  0.0 6.0 %collective-permute-start = (f32[16,256]{1,0:T(8,128)}, f32[16,256]{1,0:T(8,128)S(1)}, u32[]{:S(2)}, u32[]{:S(2)}) collective-permute-start(f32[16,256]{1,0:T(8,128)} %refs_0_.3), channel_id=1, source_target_pairs={{0,1},{1,0},{2,3},{3,2},{4,5},{5,4},{6,7},{7,6},{8,9},{9,8},{10,11... | collective-permute-start | bytes 49160 | tf_op jit(solution)/shard_map/ppermute | solution.py:352
  6.0 0.0 copy-done.3
  6.0 0.0 copy-start
  6.0 1.2 %copy-done = f32[256,1024]{1,0:T(8,128)S(1)} copy-done((f32[256,1024]{1,0:T(8,128)S(1)}, f32[256,1024]{1,0:T(8,128)}, u32[]{:S(2)}) %copy-start) | copy-done | bytes 1048600
  7.2 0.0 copy-start.2
  7.2 0.3 shard_map.37
  7.5 0.0 collective-permute-done.refs_1_
  7.5 0.4 %copy-done.2 = f32[16,256]{1,0:T(8,128)S(1)} copy-done((f32[16,256]{1,0:T(8,128)S(1)}, f32[16,256]{1,0:T(8,128)}, u32[]{:S(2)}) %copy-start.2) | copy-done | bytes 16408
  8.0 2.0 %shard_map.38 = (f32[64,1152]{1,0:T(8,128)S(1)}, f32[96,256]{1,0:T(8,128)S(1)}, f32[64,256]{1,0:T(8,128)S(1)}, f32[96,384]{1,0:T(8,128)S(1)}) custom-call(f32[16,256]{1,0:T(8,128)S(1)} %copy-done.2, f32[16,256]{1,0:T(8,128)S(1)} %collective-permute-done.refs_1_, f32[32,128]{1,0:T(8,128)S(1)} %get-tuple-element.34.refs_2_.refs_1_, ...), custom_call_target="tpu_custom_call" | custom-call | flops 1000000 | bytes 2146304 | tf_op jit(solution)/shard_map/pallas_call | solution.py:36
  9.9 1.0 %collective-permute-start.1 = (f32[64,1152]{1,0:T(8,128)S(1)}, f32[64,1152]{1,0:T(8,128)S(1)}, u32[]{:S(2)}, u32[]{:S(2)}) collective-permute-start(f32[64,1152]{1,0:T(8,128)S(1)} %get-tuple-element.41.refs_0_), channel_id=1, source_target_pairs={{0,2},{2,0},{4,6},{6,4},{8,10},{10,8},{12,14},{14,12},{16,18},{18,... | collective-permute-start | bytes 884744 | tf_op jit(solution)/shard_map/ppermute | solution.py:358
  11.0 1.2 %collective-permute-done.1.refs_1_ = f32[64,1152]{1,0:T(8,128)S(1)} collective-permute-done((f32[64,1152]{1,0:T(8,128)S(1)}, f32[64,1152]{1,0:T(8,128)S(1)}, u32[]{:S(2)}, u32[]{:S(2)}) %collective-permute-start.1) | collective-permute-done | bytes 294944 | tf_op jit(solution)/shard_map/ppermute | solution.py:358
  12.2 0.9 %shard_map.40 = (f32[32,1152]{1,0:T(8,128)S(1)}, f32[8,1152]{1,0:T(8,128)S(1)}, f32[56,1152]{1,0:T(8,128)S(1)}) custom-call(f32[64,1152]{1,0:T(8,128)S(1)} %get-tuple-element.41.refs_0_, f32[64,1152]{1,0:T(8,128)S(1)} %collective-permute-done.1.refs_1_), custom_call_target="tpu_custom_call" | custom-call | flops 1000000 | bytes 589824 | tf_op jit(solution)/shard_map/pallas_call | solution.py:36
  13.1 0.8 %collective-permute-start.4 = (f32[56,1152]{1,0:T(8,128)S(1)}, f32[56,1152]{1,0:T(8,128)S(1)}, u32[]{:S(2)}, u32[]{:S(2)}) collective-permute-start(f32[56,1152]{1,0:T(8,128)S(1)} %get-tuple-element.44.refs_1_), channel_id=1, source_target_pairs={{0,16},{2,6},{4,20},{6,2},{8,24},{10,14},{12,28},{14,10},{16,0},{1... | collective-permute-start | bytes 774152 | tf_op jit(solution)/shard_map/ppermute | solution.py:324
  13.9 0.7 %collective-permute-start.2 = (f32[8,1152]{1,0:T(8,128)S(1)}, f32[8,1152]{1,0:T(8,128)S(1)}, u32[]{:S(2)}, u32[]{:S(2)}) collective-permute-start(f32[8,1152]{1,0:T(8,128)S(1)} %get-tuple-element.43.refs_0_), channel_id=1, source_target_pairs={{0,16},{2,6},{4,20},{6,2},{8,24},{10,14},{12,28},{14,10},{16,0},{1... | collective-permute-start | bytes 110600 | tf_op jit(solution)/shard_map/ppermute | solution.py:324
  14.7 4.2 %collective-permute-done.2.refs_2_ = f32[8,1152]{1,0:T(8,128)S(1)} collective-permute-done((f32[8,1152]{1,0:T(8,128)S(1)}, f32[8,1152]{1,0:T(8,128)S(1)}, u32[]{:S(2)}, u32[]{:S(2)}) %collective-permute-start.2) | collective-permute-done | bytes 36896 | tf_op jit(solution)/shard_map/ppermute | solution.py:324
  18.9 0.2 shard_map.41.refs_1_
  19.1 1.4 %collective-permute-start.3 = (f32[16,1280]{1,0:T(8,128)S(1)}, f32[16,1280]{1,0:T(8,128)S(1)}, u32[]{:S(2)}, u32[]{:S(2)}) collective-permute-start(f32[16,1280]{1,0:T(8,128)S(1)} %shard_map.41.refs_1_), channel_id=1, source_target_pairs={{0,2},{2,0},{4,20},{6,10},{8,24},{10,6},{12,14},{14,12},{16,18},{1... | collective-permute-start | bytes 245768 | tf_op jit(solution)/shard_map/ppermute | solution.py:363
  20.5 0.0 collective-permute-done.4.refs_3_
  20.5 0.7 %shard_map.42 = (f32[32,1152]{1,0:T(8,128)S(1)}, f32[16,1152]{1,0:T(8,128)S(1)}, f32[32,1152]{1,0:T(8,128)S(1)}) custom-call(f32[8,1152]{1,0:T(8,128)S(1)} %get-tuple-element.43.refs_0_, f32[56,1152]{1,0:T(8,128)S(1)} %get-tuple-element.44.refs_1_, f32[8,1152]{1,0:T(8,128)S(1)} %collective-permute-done.2.refs_2_, f32[56,1152]{1,0:T(8,128)S(1)} %collective-permute-done.4.refs_3_), custom_call_target="tpu_custom_call" | custom-call | flops 1000000 | bytes 589824 | tf_op jit(solution)/shard_map/pallas_call | solution.py:36
  21.2 1.6 %collective-permute-done.3.refs_0_ = f32[16,1280]{1,0:T(8,128)S(1)} collective-permute-done((f32[16,1280]{1,0:T(8,128)S(1)}, f32[16,1280]{1,0:T(8,128)S(1)}, u32[]{:S(2)}, u32[]{:S(2)}) %collective-permute-start.3) | collective-permute-done | bytes 81952 | tf_op jit(solution)/shard_map/ppermute | solution.py:363
  22.8 0.3 shard_map.43
  23.1 1.4 %collective-permute-start.5 = (f32[32,1152]{1,0:T(8,128)S(1)}, f32[32,1152]{1,0:T(8,128)S(1)}, u32[]{:S(2)}, u32[]{:S(2)}) collective-permute-start(f32[32,1152]{1,0:T(8,128)S(1)} %get-tuple-element.46.refs_2_), channel_id=1, source_target_pairs={{0,6},{1,7},{2,3},{3,2},{4,68},{5,69},{6,0},{7,1},{8,72},{9,73},{1... | collective-permute-start | bytes 442376 | tf_op jit(solution)/shard_map/ppermute | solution.py:368
  24.4 3.6 %collective-permute-done.5.refs_0_ = f32[32,1152]{1,0:T(8,128)S(1)} collective-permute-done((f32[32,1152]{1,0:T(8,128)S(1)}, f32[32,1152]{1,0:T(8,128)S(1)}, u32[]{:S(2)}, u32[]{:S(2)}) %collective-permute-start.5) | collective-permute-done | bytes 147488 | tf_op jit(solution)/shard_map/ppermute | solution.py:368
  28.0 0.5 %shard_map.44 = (f32[32,1024]{1,0:T(8,128)S(1)}, f32[16,1024]{1,0:T(8,128)S(1)}) custom-call(f32[32,1152]{1,0:T(8,128)S(1)} %collective-permute-done.5.refs_0_, f32[32,128]{1,0:T(8,128)S(1)} %get-tuple-element.34.refs_2_.refs_1_, f32[32,1152]{1,0:T(8,128)S(1)} %get-tuple-element.46.refs_2_, f32[16,1152]{1,0:T(8,128)S(1)} %get-tuple-element.47.refs_3_, ...), custom_call_target="tpu_custom_call" | custom-call | flops 1000000 | bytes 450560 | tf_op jit(solution)/shard_map/pallas_call | solution.py:36
  28.6 0.0 copy-start.1
  28.6 0.3 shard_map.45
  28.9 0.1 collective-permute-start.7
  29.0 1.4 %collective-permute-start.6 = (f32[16,1024]{1,0:T(8,128)S(1)}, f32[16,1024]{1,0:T(8,128)S(1)}, u32[]{:S(2)}, u32[]{:S(2)}) collective-permute-start(f32[16,1024]{1,0:T(8,128)S(1)} %get-tuple-element.49.refs_2_), channel_id=1, source_target_pairs={{0,2},{2,0},{4,20},{6,10},{8,24},{10,6},{12,14},{14,12},{16,18},{1... | collective-permute-start | bytes 196616 | tf_op jit(solution)/shard_map/ppermute | solution.py:324
  30.4 2.1 %collective-permute-done.6.refs_0_ = f32[16,1024]{1,0:T(8,128)S(1)} collective-permute-done((f32[16,1024]{1,0:T(8,128)S(1)}, f32[16,1024]{1,0:T(8,128)S(1)}, u32[]{:S(2)}, u32[]{:S(2)}) %collective-permute-start.6) | collective-permute-done | bytes 65568 | tf_op jit(solution)/shard_map/ppermute | solution.py:324
  32.5 0.2 shard_map.46
  32.7 0.1 collective-permute-start.8
  32.8 1.4 %collective-permute-done.7.refs_3_ = f32[56,1024]{1,0:T(8,128)S(1)} collective-permute-done((f32[56,1024]{1,0:T(8,128)S(1)}, f32[56,1024]{1,0:T(8,128)S(1)}, u32[]{:S(2)}, u32[]{:S(2)}) %collective-permute-start.7) | collective-permute-done | bytes 229408 | tf_op jit(solution)/shard_map/ppermute | solution.py:324
  34.2 0.4 shard_map.47
  34.6 1.0 %collective-permute-done.8.refs_5_ = f32[8,1024]{1,0:T(8,128)S(1)} collective-permute-done((f32[8,1024]{1,0:T(8,128)S(1)}, f32[8,1024]{1,0:T(8,128)S(1)}, u32[]{:S(2)}, u32[]{:S(2)}) %collective-permute-start.8) | collective-permute-done | bytes 32800 | tf_op jit(solution)/shard_map/ppermute | solution.py:378
  35.5 0.1 shard_map.48
  35.6 3.9 %collective-permute-start.9 = (f32[64,1024]{1,0:T(8,128)S(1)}, f32[64,1024]{1,0:T(8,128)S(1)}, u32[]{:S(2)}, u32[]{:S(2)}) collective-permute-start(f32[64,1024]{1,0:T(8,128)S(1)} %get-tuple-element.61), channel_id=1, source_target_pairs={{0,2},{2,0},{4,6},{6,4},{8,10},{10,8},{12,14},{14,12},{16,18},{18,... | collective-permute-start | bytes 786440 | tf_op jit(solution)/shard_map/ppermute | solution.py:381
  39.5 0.0 copy-done.1
  39.5 1.0 %shard_map.39 = (f32[256,1024]{1,0:T(8,128)S(1)}, bf16[256,256]{1,0:T(8,128)(2,1)S(1)}) custom-call(f32[96,256]{1,0:T(8,128)S(1)} %get-tuple-element.37.refs_0_, f32[64,256]{1,0:T(8,128)S(1)} %get-tuple-element.38.refs_1_, f32[96,384]{1,0:T(8,128)S(1)} %get-tuple-element.39.refs_2_, bf16[256,1024]{1,0:T(8,128)(2,1)S(1)} %get-tuple-element.35.refs_3_, ...), custom_call_target="tpu_custom_call" | custom-call | flops 20000000 | bytes 3457024 | tf_op jit(solution)/shard_map/pallas_call | solution.py:36
  40.6 0.1 collective-permute-done.9.msg_ref
  40.7 1.2 %shard_map.49 = f32[256,1024]{1,0:T(8,128)} custom-call(bf16[256,256]{1,0:T(8,128)(2,1)S(1)} %get-tuple-element.40.lhs_ref, f32[64,1024]{1,0:T(8,128)S(1)} %get-tuple-element.60.keep_ref, f32[64,1024]{1,0:T(8,128)S(1)} %collective-permute-done.9.msg_ref, f32[256,1024]{1,0:T(8,128)S(1)} %get-tuple-element.62.y_ref), custom_call_target="tpu_custom_call" | custom-call | tf_op jit(solution)/shard_map/pallas_call | solution.py:382
Async XLA Ops:
  0.0 6.0 %copy-start.3 = (s32[32]{0:T(128)S(1)}, s32[32]{0:T(128)}, u32[]{:S(2)}) copy-start(s32[32]{0:T(128)} %param.5) | copy-start | bytes 388
  0.0 7.5 %collective-permute-start = (f32[16,256]{1,0:T(8,128)}, f32[16,256]{1,0:T(8,128)S(1)}, u32[]{:S(2)}, u32[]{:S(2)}) collective-permute-start(f32[16,256]{1,0:T(8,128)} %refs_0_.3), channel_id=1, source_target_pairs={{0,1},{1,0},{2,3},{3,2},{4,5},{5,4},{6,7},{7,6},{8,9},{9,8},{10,11... | collective-permute-start | bytes 49160 | tf_op jit(solution)/shard_map/ppermute | solution.py:352
  6.0 1.2 %copy-start = (f32[256,1024]{1,0:T(8,128)S(1)}, f32[256,1024]{1,0:T(8,128)}, u32[]{:S(2)}) copy-start(f32[256,1024]{1,0:T(8,128)} %refs_5_.1) | copy-start | bytes 3145732
  7.2 0.7 %copy-start.2 = (f32[16,256]{1,0:T(8,128)S(1)}, f32[16,256]{1,0:T(8,128)}, u32[]{:S(2)}) copy-start(f32[16,256]{1,0:T(8,128)} %refs_0_.3) | copy-start | bytes 49156
  9.9 2.3 %collective-permute-start.1 = (f32[64,1152]{1,0:T(8,128)S(1)}, f32[64,1152]{1,0:T(8,128)S(1)}, u32[]{:S(2)}, u32[]{:S(2)}) collective-permute-start(f32[64,1152]{1,0:T(8,128)S(1)} %get-tuple-element.41.refs_0_), channel_id=1, source_target_pairs={{0,2},{2,0},{4,6},{6,4},{8,10},{10,8},{12,14},{14,12},{16,18},{18,... | collective-permute-start | bytes 884744 | tf_op jit(solution)/shard_map/ppermute | solution.py:358
  13.1 7.4 %collective-permute-start.4 = (f32[56,1152]{1,0:T(8,128)S(1)}, f32[56,1152]{1,0:T(8,128)S(1)}, u32[]{:S(2)}, u32[]{:S(2)}) collective-permute-start(f32[56,1152]{1,0:T(8,128)S(1)} %get-tuple-element.44.refs_1_), channel_id=1, source_target_pairs={{0,16},{2,6},{4,20},{6,2},{8,24},{10,14},{12,28},{14,10},{16,0},{1... | collective-permute-start | bytes 774152 | tf_op jit(solution)/shard_map/ppermute | solution.py:324
  13.9 5.0 %collective-permute-start.2 = (f32[8,1152]{1,0:T(8,128)S(1)}, f32[8,1152]{1,0:T(8,128)S(1)}, u32[]{:S(2)}, u32[]{:S(2)}) collective-permute-start(f32[8,1152]{1,0:T(8,128)S(1)} %get-tuple-element.43.refs_0_), channel_id=1, source_target_pairs={{0,16},{2,6},{4,20},{6,2},{8,24},{10,14},{12,28},{14,10},{16,0},{1... | collective-permute-start | bytes 110600 | tf_op jit(solution)/shard_map/ppermute | solution.py:324
  19.1 3.7 %collective-permute-start.3 = (f32[16,1280]{1,0:T(8,128)S(1)}, f32[16,1280]{1,0:T(8,128)S(1)}, u32[]{:S(2)}, u32[]{:S(2)}) collective-permute-start(f32[16,1280]{1,0:T(8,128)S(1)} %shard_map.41.refs_1_), channel_id=1, source_target_pairs={{0,2},{2,0},{4,20},{6,10},{8,24},{10,6},{12,14},{14,12},{16,18},{1... | collective-permute-start | bytes 245768 | tf_op jit(solution)/shard_map/ppermute | solution.py:363
  23.1 5.0 %collective-permute-start.5 = (f32[32,1152]{1,0:T(8,128)S(1)}, f32[32,1152]{1,0:T(8,128)S(1)}, u32[]{:S(2)}, u32[]{:S(2)}) collective-permute-start(f32[32,1152]{1,0:T(8,128)S(1)} %get-tuple-element.46.refs_2_), channel_id=1, source_target_pairs={{0,6},{1,7},{2,3},{3,2},{4,68},{5,69},{6,0},{7,1},{8,72},{9,73},{1... | collective-permute-start | bytes 442376 | tf_op jit(solution)/shard_map/ppermute | solution.py:368
  28.6 10.9 %copy-start.1 = (f32[256,1024]{1,0:T(8,128)S(1)}, f32[256,1024]{1,0:T(8,128)}, u32[]{:S(2)}) copy-start(f32[256,1024]{1,0:T(8,128)} %refs_5_.1) | copy-start | bytes 3145732
  28.9 5.3 %collective-permute-start.7 = (f32[56,1024]{1,0:T(8,128)S(1)}, f32[56,1024]{1,0:T(8,128)S(1)}, u32[]{:S(2)}, u32[]{:S(2)}) collective-permute-start(f32[56,1024]{1,0:T(8,128)S(1)} %get-tuple-element.55.refs_2_), channel_id=1, source_target_pairs={{0,16},{2,6},{4,20},{6,2},{8,24},{10,14},{12,28},{14,10},{16,0},{1... | collective-permute-start | bytes 688136 | tf_op jit(solution)/shard_map/ppermute | solution.py:324
  29.0 3.5 %collective-permute-start.6 = (f32[16,1024]{1,0:T(8,128)S(1)}, f32[16,1024]{1,0:T(8,128)S(1)}, u32[]{:S(2)}, u32[]{:S(2)}) collective-permute-start(f32[16,1024]{1,0:T(8,128)S(1)} %get-tuple-element.49.refs_2_), channel_id=1, source_target_pairs={{0,2},{2,0},{4,20},{6,10},{8,24},{10,6},{12,14},{14,12},{16,18},{1... | collective-permute-start | bytes 196616 | tf_op jit(solution)/shard_map/ppermute | solution.py:324
  32.7 2.9 %collective-permute-start.8 = (f32[8,1024]{1,0:T(8,128)S(1)}, f32[8,1024]{1,0:T(8,128)S(1)}, u32[]{:S(2)}, u32[]{:S(2)}) collective-permute-start(f32[8,1024]{1,0:T(8,128)S(1)} %get-tuple-element.59.refs_4_), channel_id=1, source_target_pairs={{0,16},{2,6},{4,20},{6,2},{8,24},{10,14},{12,28},{14,10},{16,0},{1... | collective-permute-start | bytes 98312 | tf_op jit(solution)/shard_map/ppermute | solution.py:378
  35.6 5.0 %collective-permute-start.9 = (f32[64,1024]{1,0:T(8,128)S(1)}, f32[64,1024]{1,0:T(8,128)S(1)}, u32[]{:S(2)}, u32[]{:S(2)}) collective-permute-start(f32[64,1024]{1,0:T(8,128)S(1)} %get-tuple-element.61), channel_id=1, source_target_pairs={{0,2},{2,0},{4,6},{6,4},{8,10},{10,8},{12,14},{14,12},{16,18},{18,... | collective-permute-start | bytes 786440 | tf_op jit(solution)/shard_map/ppermute | solution.py:381

commit v5 on v4

--- a/solution.py
+++ b/solution.py
@@ -120,29 +120,32 @@
     inner_ref[...] = inner
     edge_ref[...] = edge
     solved_ref[...] = solved[0:count]
-    msg_ref[...] = jnp.concatenate([dot3(observe, (high_ref[...], low_ref[...])), coef], axis=1)
+    upper, lower = split(observe)
+    both = jnp.dot(jnp.concatenate([upper, lower], axis=0), high_ref[...], preferred_element_type=jnp.float32)
+    rest = jnp.dot(upper, low_ref[...], preferred_element_type=jnp.float32)
+    msg_ref[...] = jnp.concatenate([both[0:64] + (both[64:128] + rest), coef], axis=1)
 
 
 def to_low(tile):
     return jnp.where(lane_of(tile.shape) < 32, pltpu.roll(tile, LANES - 32, 1), 0.0)
 
 
-def solve(blocks, lower, lane=0):
-    for j in range(SWEEPS):
+def solve(blocks, lower, lane=0, sweeps=SWEEPS):
+    for j in range(sweeps):
         source = blocks[j // 8][j % 8 : j % 8 + 1]
         for q in range((j + 1) // 8, len(blocks)):
             blocks[q] = blocks[q] + lower[8 * q : 8 * q + 8, lane + j : lane + j + 1] * source
     return jnp.concatenate(blocks, axis=0)
 
 
-def spread(rows, tile, at, solved, lane, first=0, reach=1):
+def spread(rows, tile, at, solved, lane, first=0, reach=1, base=0):
     blocks = [rows[8 * q : 8 * q + 8] for q in range(rows.shape[0] // 8)]
     for j in range(solved.shape[0]):
         for q in range(len(blocks)):
             top = at + 8 * q
             if top + 7 >= first + j + reach:
                 column = lane + first + j
-                blocks[q] = blocks[q] + tile[top : top + 8, column : column + 1] * solved[j : j + 1]
+                blocks[q] = blocks[q] + tile[top - base : top - base + 8, column : column + 1] * solved[j : j + 1]
     return blocks[0] if len(blocks) == 1 else jnp.concatenate(blocks, axis=0)
 
 
@@ -194,24 +197,41 @@
     msg_ref[...] = jnp.concatenate([p, tile[0:16], tile[16:32]], axis=1)
 
 
-def edges_kernel(first_ref, rest_ref, got_first_ref, got_rest_ref, pair_ref, p_ref, w_ref):
-    cols = first_ref.shape[1] - LANES
-    own = jnp.concatenate([first_ref[...], rest_ref[0:24]], axis=0)
-    got = jnp.concatenate([got_first_ref[...], got_rest_ref[0:24]], axis=0)
+def joined(own, got):
+    cols = own.shape[1] - LANES
     mine, theirs = own[:, cols:], got[:, cols:]
     tau = 2.0 / (mine[:, 64:65] + theirs[:, 64:65])
     lane = lane_of(mine.shape)
-    upper = (lane >= 32) & (lane < 64)
-    outer = to_low(theirs) + jnp.where(upper, mine, 0.0)
-    pair = jnp.concatenate([own[:, 0:cols] + got[:, 0:cols], outer], axis=1) * tau
-    pair = solve([pair[8 * q : 8 * q + 8] for q in range(4)], tau * (mine + theirs))
+    outer = to_low(theirs) + jnp.where((lane >= 32) & (lane < 64), mine, 0.0)
+    return jnp.concatenate([own[:, 0:cols] + got[:, 0:cols], outer], axis=1) * tau, tau * (mine + theirs)
+
+
+def edges_kernel(first_ref, rest_ref, got_first_ref, got_rest_ref, pair_ref, w_ref):
+    cols = first_ref.shape[1] - LANES
+    pair, lower = joined(
+        jnp.concatenate([first_ref[...], rest_ref[0:16]], axis=0),
+        jnp.concatenate([got_first_ref[...], got_rest_ref[0:16]], axis=0),
+    )
+    pair = solve([pair[8 * q : 8 * q + 8] for q in range(3)], lower, sweeps=24)
     pair_ref[...] = pair
+    tile = got_rest_ref[24:56, cols:]
+    kept = to_low(tile) + jnp.where(lane_of(tile.shape) == 64, tile, 0.0)
+    w = jnp.concatenate([got_rest_ref[24:56, 0:cols], kept], axis=1)
+    w_ref[...] = spread(w, tile, 0, pair, 0, reach=8)
+
+
+def late_kernel(rest_ref, got_rest_ref, pair_ref, last_ref, p_ref):
+    cols = rest_ref.shape[1] - LANES
+    pair = pair_ref[...]
+    last, lower = joined(rest_ref[16:24], got_rest_ref[16:24])
+    last = spread(last, lower, 24, pair, 0, base=24)
+    for j in range(7):
+        last = last + lower[:, 24 + j : 25 + j] * last[j : j + 1]
+    last_ref[...] = last
     tile = rest_ref[40:56, cols:]
-    p = jnp.concatenate([rest_ref[40:56, 0:cols], jnp.where((lane_of(tile.shape) >= 32) & (lane_of(tile.shape) < 64), tile, 0.0)], axis=1)
-    p_ref[...] = spread(p, rest_ref[24:56, cols:], 16, pair[0:24], 0, reach=8)
-    tile = got_rest_ref[24:56, cols:]
-    w = jnp.concatenate([got_rest_ref[24:56, 0:cols], to_low(tile) + jnp.where(lane == 64, tile, 0.0)], axis=1)
-    w_ref[...] = spread(w, tile, 0, pair[0:24], 0, reach=8)
+    lane = lane_of(tile.shape)
+    p = jnp.concatenate([rest_ref[40:56, 0:cols], jnp.where((lane >= 32) & (lane < 64), tile, 0.0)], axis=1)
+    p_ref[...] = spread(p, tile, 16, pair, 0, reach=8, base=16)
 
 
 def p0_kernel(msg_ref, own_ref, w_ref, p0_ref, scaled_ref, out_ref):
@@ -241,27 +261,26 @@
     w = both[:, 0:cols] * tau
     w = solve([w[8 * q : 8 * q + 8] for q in range(4)], tau * both[:, cols:])
     out_w_ref[...] = w
-    tile = jnp.concatenate([p_ref[:, cols:], p_ref[:, cols:]], axis=0)
-    rest = spread(p_ref[:, 0:cols], tile, 16, p0_ref[...], 32)
-    out_ref[...] = spread(rest, tile, 16, w[0:16], 0, reach=16)
-
-
-def e0_kernel(pair_ref, w_ref, p0_ref, out_ref, tail_ref):
+    tile = p_ref[:, cols:]
+    rest = spread(p_ref[:, 0:cols], tile, 16, p0_ref[...], 32, base=16)
+    out_ref[...] = spread(rest, tile, 16, w[0:16], 0, reach=16, base=16)
+
+
+def e0_kernel(pair_ref, last_ref, w_ref, p0_ref, out_ref, tail_ref):
     cols = w_ref.shape[1]
-    tile = pair_ref[:, cols:]
-    w = w_ref[...]
-    e = spread(pair_ref[:, 0:cols], tile, 0, w[0:24], 0, reach=8)
-    e = spread(e, tile, 0, p0_ref[...], 32, reach=8)
-    out_ref[...] = jnp.concatenate([w, e[0:24]], axis=0)
-    tail_ref[...] = e[24:32]
-
-
-def p1_kernel(msg_ref, scaled_ref, rest_ref, pair_ref, tail_ref, p0_ref, p_ref, out_ref):
+    w, p0 = w_ref[0:24], p0_ref[...]
+    e = spread(pair_ref[:, 0:cols], pair_ref[:, cols:], 0, w[0:16], 0, reach=8)
+    out_ref[...] = jnp.concatenate([w_ref[...], spread(e, pair_ref[:, cols:], 0, p0, 32, reach=8)], axis=0)
+    tail = spread(last_ref[:, 0:cols], last_ref[:, cols:], 24, w, 0, reach=8, base=24)
+    tail_ref[...] = spread(tail, last_ref[:, cols:], 24, p0, 32, reach=8, base=24)
+
+
+def p1_kernel(msg_ref, scaled_ref, rest_ref, last_ref, tail_ref, p0_ref, p_ref, out_ref):
     cols = msg_ref.shape[1]
     scaled = scaled_ref[...]
     p1 = substitute((rest_ref[...] + msg_ref[...]) * scaled[16:32, 64:65], scaled, 16, 32)
     p_ref[...] = jnp.concatenate([p0_ref[...], p1], axis=0)
-    out_ref[...] = spread(tail_ref[...], pair_ref[:, cols:], 24, p1[0:8], 32, first=16, reach=8)
+    out_ref[...] = spread(tail_ref[...], last_ref[:, cols:], 24, p1[0:8], 32, first=16, reach=8, base=24)
 
 
 def mid_kernel(mid_ref, p_ref, own_ref, got_ref, part_ref, o_ref, e_ref):
@@ -345,7 +364,7 @@
 
     on_chip = swap(lambda i, chip, north, inside: i ^ 1)
     in_pair = swap(lambda i, chip, north, inside: i ^ 2 if north else i ^ 8)
-    p_pairs = swap(lambda i, chip, north, inside: (i ^ 6 if north else i ^ 8) if inside else i ^ 1)
+    p_pairs = swap(lambda i, chip, north, inside: (i ^ 6 if north else i ^ far) if inside else i ^ 1)
     w_pairs = [
         (2 * i + c, 2 * i + 1 - c if j is None else 2 * j + c) for i, j in swap(next_quad) for c in range(2)
     ]
@@ -360,21 +379,20 @@
     got_first = trade(first, in_pair)
     got_rest = trade(rest, in_pair)
     (msg,) = call(pair_kernel, [(16, wide + LANES)], first, rest, got_first, where=is_inside)
-    got = lax.ppermute(msg, "rows", p_pairs)
-    pair, p, w = call(
-        edges_kernel, [(32, wide), (16, wide), (32, wide)], first, rest, got_first, got_rest, where=is_inside
-    )
+    got = trade(msg, p_pairs)
+    pair, w = call(edges_kernel, [(24, wide), (32, wide)], first, rest, got_first, got_rest, where=is_inside)
     p0, scaled, w = call(p0_kernel, [(16, cols), (32, LANES), (32, wide)], got, msg, w, where=is_inside)
     got = lax.ppermute(w, ("rows", "cols"), w_pairs)
+    last, p = call(late_kernel, [(8, wide), (16, wide)], rest, got_rest, pair, where=is_inside)
     partial, lhs = call(
         inner_kernel, [(rows, cols), jax.ShapeDtypeStruct((rows, 256), jnp.bfloat16)],
         inner, edge, solved, high, low, eigvecs, flops=20_000_000,
     )
     w, rest = call(w_kernel, [(32, cols), (16, cols)], got, start, w, p, p0, where=is_inside)
+    most, tail = call(e0_kernel, [(56, cols), (8, cols)], pair, last, w, p0, where=is_inside)
+    got_most = trade(most, in_pair)
     got = trade(rest, p_pairs)
-    most, tail = call(e0_kernel, [(56, cols), (8, cols)], pair, w, p0, where=is_inside)
-    got_most = trade(most, in_pair)
-    p, tail = call(p1_kernel, [(32, cols), (8, cols)], got, scaled, rest, pair, tail, p0, where=is_inside)
+    p, tail = call(p1_kernel, [(32, cols), (8, cols)], got, scaled, rest, last, tail, p0, where=is_inside)
     got = lax.ppermute(tail, "rows", in_pair)
     part, o, e = call(mid_kernel, [(32, cols), (32, cols), (24, cols)], mid, p, most, got_most, where=is_north)
     keep, msg = call(back_kernel, [(64, cols), (64, cols)], mid, part, o, e, tail, got, where=is_north)

time: 42.1 us -> 41 us (0.974)
  the two profiles are of different devices: /device:TPU:37 before, /device:TPU:41 now
where the time goes in v5:
time: 41 us; the launch traced here: 40.8 us
  waiting for transfers between devices  16.6 us (40%)
  starting transfers between devices  14.4 us (35%)
  Pallas kernels  8.05 us (20%)
  local copies, waits for them, and re-layouts  1.66 us (4%)
    ppermute x5, waiting for transfers between devices, trade(): return lax.ppermute(array, 'rows', pairs)  10.5 us
    pallas_call x13, Pallas kernels, call(): pl.pallas_call(body, out_shape=[jax.ShapeDtypeStruct(s, jnp.float32) if i...  6.82 us
    ppermute x1, starting transfers between devices, per_device(): other = lax.ppermute(reflectors, 'cols', [(0, 1), (1, 0)])  6.01 us
    ppermute x1, starting transfers between devices, per_device(): got = lax.ppermute(w, ('rows', 'cols'), w_pairs)  3.48 us
    ppermute x1, waiting for transfers between devices, per_device(): got = lax.ppermute(w, ('rows', 'cols'), w_pairs)  3.27 us
    ppermute x5, starting transfers between devices, trade(): return lax.ppermute(array, 'rows', pairs)  3.14 us
    ppermute x2, starting transfers between devices, per_device(): got = lax.ppermute(msg, 'rows', on_chip)  1.66 us
    unnamed x8, local copies, waits for them, and re-layouts  1.66 us
  transfers between devices with their start and end apart: 10, of which 8 were waited for; matrix products, arithmetic and copies ran while one was open for 0% of the time, Pallas kernels for 7%

profile of v5, /device:TPU:41, one launch (start us, length us, event | category | flops | bytes accessed | tf_op | source)
XLA Modules:
  0.0 40.8 jit_solution(5982664089127185821)
XLA Ops:
  0.0 0.0 copy-start.3
  0.0 6.0 %collective-permute-start = (f32[16,256]{1,0:T(8,128)}, f32[16,256]{1,0:T(8,128)S(1)}, u32[]{:S(2)}, u32[]{:S(2)}) collective-permute-start(f32[16,256]{1,0:T(8,128)} %refs_0_.3), channel_id=1, source_target_pairs={{0,1},{1,0},{2,3},{3,2},{4,5},{5,4},{6,7},{7,6},{8,9},{9,8},{10,11... | collective-permute-start | bytes 49160 | tf_op jit(solution)/shard_map/ppermute | solution.py:371
  6.0 0.0 copy-done.3
  6.0 0.0 copy-start
  6.0 1.2 %copy-done = f32[256,1024]{1,0:T(8,128)S(1)} copy-done((f32[256,1024]{1,0:T(8,128)S(1)}, f32[256,1024]{1,0:T(8,128)}, u32[]{:S(2)}) %copy-start) | copy-done | bytes 1048600
  7.2 0.0 copy-start.2
  7.2 0.3 shard_map.37
  7.5 0.0 collective-permute-done.refs_1_
  7.5 0.4 %copy-done.2 = f32[16,256]{1,0:T(8,128)S(1)} copy-done((f32[16,256]{1,0:T(8,128)S(1)}, f32[16,256]{1,0:T(8,128)}, u32[]{:S(2)}) %copy-start.2) | copy-done | bytes 16408
  8.0 1.9 %shard_map.38 = (f32[64,1152]{1,0:T(8,128)S(1)}, f32[96,256]{1,0:T(8,128)S(1)}, f32[64,256]{1,0:T(8,128)S(1)}, f32[96,384]{1,0:T(8,128)S(1)}) custom-call(f32[16,256]{1,0:T(8,128)S(1)} %copy-done.2, f32[16,256]{1,0:T(8,128)S(1)} %collective-permute-done.refs_1_, f32[32,128]{1,0:T(8,128)S(1)} %get-tuple-element.35.refs_2_.refs_1_, ...), custom_call_target="tpu_custom_call" | custom-call | flops 1000000 | bytes 2146304 | tf_op jit(solution)/shard_map/pallas_call | solution.py:36
  9.8 1.0 %collective-permute-start.1 = (f32[64,1152]{1,0:T(8,128)S(1)}, f32[64,1152]{1,0:T(8,128)S(1)}, u32[]{:S(2)}, u32[]{:S(2)}) collective-permute-start(f32[64,1152]{1,0:T(8,128)S(1)} %get-tuple-element.42.refs_0_), channel_id=1, source_target_pairs={{0,2},{2,0},{4,6},{6,4},{8,10},{10,8},{12,14},{14,12},{16,18},{18,... | collective-permute-start | bytes 884744 | tf_op jit(solution)/shard_map/ppermute | solution.py:377
  10.9 1.2 %collective-permute-done.1.refs_1_ = f32[64,1152]{1,0:T(8,128)S(1)} collective-permute-done((f32[64,1152]{1,0:T(8,128)S(1)}, f32[64,1152]{1,0:T(8,128)S(1)}, u32[]{:S(2)}, u32[]{:S(2)}) %collective-permute-start.1) | collective-permute-done | bytes 294944 | tf_op jit(solution)/shard_map/ppermute | solution.py:377
  12.1 0.9 %shard_map.40 = (f32[32,1152]{1,0:T(8,128)S(1)}, f32[8,1152]{1,0:T(8,128)S(1)}, f32[56,1152]{1,0:T(8,128)S(1)}) custom-call(f32[64,1152]{1,0:T(8,128)S(1)} %get-tuple-element.42.refs_0_, f32[64,1152]{1,0:T(8,128)S(1)} %collective-permute-done.1.refs_1_), custom_call_target="tpu_custom_call" | custom-call | flops 1000000 | bytes 589824 | tf_op jit(solution)/shard_map/pallas_call | solution.py:36
  13.0 0.8 %collective-permute-start.4 = (f32[56,1152]{1,0:T(8,128)S(1)}, f32[56,1152]{1,0:T(8,128)S(1)}, u32[]{:S(2)}, u32[]{:S(2)}) collective-permute-start(f32[56,1152]{1,0:T(8,128)S(1)} %get-tuple-element.45.refs_1_.refs_0_), channel_id=1, source_target_pairs={{0,16},{2,6},{4,20},{6,2},{8,24},{10,14},{12,28},{14,10},{16,0},{1... | collective-permute-start | bytes 774152 | tf_op jit(solution)/shard_map/ppermute | solution.py:343
  13.8 0.7 %collective-permute-start.2 = (f32[8,1152]{1,0:T(8,128)S(1)}, f32[8,1152]{1,0:T(8,128)S(1)}, u32[]{:S(2)}, u32[]{:S(2)}) collective-permute-start(f32[8,1152]{1,0:T(8,128)S(1)} %get-tuple-element.44.refs_0_), channel_id=1, source_target_pairs={{0,16},{2,6},{4,20},{6,2},{8,24},{10,14},{12,28},{14,10},{16,0},{1... | collective-permute-start | bytes 110600 | tf_op jit(solution)/shard_map/ppermute | solution.py:343
  14.6 4.2 %collective-permute-done.2.refs_2_ = f32[8,1152]{1,0:T(8,128)S(1)} collective-permute-done((f32[8,1152]{1,0:T(8,128)S(1)}, f32[8,1152]{1,0:T(8,128)S(1)}, u32[]{:S(2)}, u32[]{:S(2)}) %collective-permute-start.2) | collective-permute-done | bytes 36896 | tf_op jit(solution)/shard_map/ppermute | solution.py:343
  18.8 0.2 shard_map.41.refs_1_
  19.0 1.4 %collective-permute-start.3 = (f32[16,1280]{1,0:T(8,128)S(1)}, f32[16,1280]{1,0:T(8,128)S(1)}, u32[]{:S(2)}, u32[]{:S(2)}) collective-permute-start(f32[16,1280]{1,0:T(8,128)S(1)} %shard_map.41.refs_1_), channel_id=1, source_target_pairs={{0,2},{2,0},{4,68},{6,10},{8,72},{10,6},{12,14},{14,12},{16,18},{1... | collective-permute-start | bytes 245768 | tf_op jit(solution)/shard_map/ppermute | solution.py:343
  20.4 0.0 collective-permute-done.4.refs_3_.refs_1_
  20.4 0.4 %shard_map.42 = (f32[24,1152]{1,0:T(8,128)S(1)}, f32[32,1152]{1,0:T(8,128)S(1)}) custom-call(f32[8,1152]{1,0:T(8,128)S(1)} %get-tuple-element.44.refs_0_, f32[56,1152]{1,0:T(8,128)S(1)} %get-tuple-element.45.refs_1_.refs_0_, f32[8,1152]{1,0:T(8,128)S(1)} %collective-permute-done.2.refs_2_, f32[56,1152]{1,0:T(8,128)S(1)} %collective-permute-done.4.refs_3_.refs_1_), custom_call_target="tpu_custom_call" | custom-call | flops 1000000 | bytes 589824 | tf_op jit(solution)/shard_map/pallas_call | solution.py:36
  20.8 1.8 %collective-permute-done.3.refs_0_ = f32[16,1280]{1,0:T(8,128)S(1)} collective-permute-done((f32[16,1280]{1,0:T(8,128)S(1)}, f32[16,1280]{1,0:T(8,128)S(1)}, u32[]{:S(2)}, u32[]{:S(2)}) %collective-permute-start.3) | collective-permute-done | bytes 81952 | tf_op jit(solution)/shard_map/ppermute | solution.py:343
  22.7 0.3 shard_map.43
  23.0 3.5 %collective-permute-start.5 = (f32[32,1152]{1,0:T(8,128)S(1)}, f32[32,1152]{1,0:T(8,128)S(1)}, u32[]{:S(2)}, u32[]{:S(2)}) collective-permute-start(f32[32,1152]{1,0:T(8,128)S(1)} %get-tuple-element.47.refs_2_), channel_id=1, source_target_pairs={{0,6},{1,7},{2,3},{3,2},{4,68},{5,69},{6,0},{7,1},{8,72},{9,73},{1... | collective-permute-start | bytes 442376 | tf_op jit(solution)/shard_map/ppermute | solution.py:385
  26.4 0.3 shard_map.44
  26.8 3.3 %collective-permute-done.5.refs_0_ = f32[32,1152]{1,0:T(8,128)S(1)} collective-permute-done((f32[32,1152]{1,0:T(8,128)S(1)}, f32[32,1152]{1,0:T(8,128)S(1)}, u32[]{:S(2)}, u32[]{:S(2)}) %collective-permute-start.5) | collective-permute-done | bytes 147488 | tf_op jit(solution)/shard_map/ppermute | solution.py:385
  30.0 0.5 %shard_map.45 = (f32[32,1024]{1,0:T(8,128)S(1)}, f32[16,1024]{1,0:T(8,128)S(1)}) custom-call(f32[32,1152]{1,0:T(8,128)S(1)} %collective-permute-done.5.refs_0_, f32[32,128]{1,0:T(8,128)S(1)} %get-tuple-element.35.refs_2_.refs_1_, f32[32,1152]{1,0:T(8,128)S(1)} %get-tuple-element.47.refs_2_, f32[16,1152]{1,0:T(8,128)S(1)} %get-tuple-element.49.refs_3_, ...), custom_call_target="tpu_custom_call" | custom-call | flops 1000000 | bytes 450560 | tf_op jit(solution)/shard_map/pallas_call | solution.py:36
  30.6 0.0 copy-start.1
  30.6 0.3 shard_map.46
  30.9 0.1 collective-permute-start.7
  31.0 0.1 collective-permute-start.6
  31.1 3.3 %collective-permute-done.6.refs_0_ = f32[16,1024]{1,0:T(8,128)S(1)} collective-permute-done((f32[16,1024]{1,0:T(8,128)S(1)}, f32[16,1024]{1,0:T(8,128)S(1)}, u32[]{:S(2)}, u32[]{:S(2)}) %collective-permute-start.6) | collective-permute-done | bytes 65568 | tf_op jit(solution)/shard_map/ppermute | solution.py:343
  34.4 0.2 shard_map.47
  34.6 0.1 collective-permute-start.8
  34.7 1.1 %collective-permute-done.7.refs_3_ = f32[56,1024]{1,0:T(8,128)S(1)} collective-permute-done((f32[56,1024]{1,0:T(8,128)S(1)}, f32[56,1024]{1,0:T(8,128)S(1)}, u32[]{:S(2)}, u32[]{:S(2)}) %collective-permute-start.7) | collective-permute-done | bytes 229408 | tf_op jit(solution)/shard_map/ppermute | solution.py:343
  35.8 0.4 shard_map.48
  36.2 1.5 %collective-permute-done.8.refs_5_ = f32[8,1024]{1,0:T(8,128)S(1)} collective-permute-done((f32[8,1024]{1,0:T(8,128)S(1)}, f32[8,1024]{1,0:T(8,128)S(1)}, u32[]{:S(2)}, u32[]{:S(2)}) %collective-permute-start.8) | collective-permute-done | bytes 32800 | tf_op jit(solution)/shard_map/ppermute | solution.py:396
  37.7 0.1 shard_map.49
  37.8 0.6 %collective-permute-start.9 = (f32[64,1024]{1,0:T(8,128)S(1)}, f32[64,1024]{1,0:T(8,128)S(1)}, u32[]{:S(2)}, u32[]{:S(2)}) collective-permute-start(f32[64,1024]{1,0:T(8,128)S(1)} %get-tuple-element.63), channel_id=1, source_target_pairs={{0,2},{2,0},{4,6},{6,4},{8,10},{10,8},{12,14},{14,12},{16,18},{18,... | collective-permute-start | bytes 786440 | tf_op jit(solution)/shard_map/ppermute | solution.py:399
  38.4 0.0 copy-done.1
  38.4 1.0 %shard_map.39 = (f32[256,1024]{1,0:T(8,128)S(1)}, bf16[256,256]{1,0:T(8,128)(2,1)S(1)}) custom-call(f32[96,256]{1,0:T(8,128)S(1)} %get-tuple-element.38.refs_0_, f32[64,256]{1,0:T(8,128)S(1)} %get-tuple-element.39.refs_1_, f32[96,384]{1,0:T(8,128)S(1)} %get-tuple-element.40.refs_2_, bf16[256,1024]{1,0:T(8,128)(2,1)S(1)} %get-tuple-element.36.refs_3_, ...), custom_call_target="tpu_custom_call" | custom-call | flops 20000000 | bytes 3457024 | tf_op jit(solution)/shard_map/pallas_call | solution.py:36
  39.5 0.1 collective-permute-done.9.msg_ref
  39.6 1.2 %shard_map.50 = f32[256,1024]{1,0:T(8,128)} custom-call(bf16[256,256]{1,0:T(8,128)(2,1)S(1)} %get-tuple-element.41.lhs_ref, f32[64,1024]{1,0:T(8,128)S(1)} %get-tuple-element.62.keep_ref, f32[64,1024]{1,0:T(8,128)S(1)} %collective-permute-done.9.msg_ref, f32[256,1024]{1,0:T(8,128)S(1)} %get-tuple-element.64.y_ref), custom_call_target="tpu_custom_call" | custom-call | tf_op jit(solution)/shard_map/pallas_call | solution.py:400
Async XLA Ops:
  0.0 6.0 %copy-start.3 = (s32[32]{0:T(128)S(1)}, s32[32]{0:T(128)}, u32[]{:S(2)}) copy-start(s32[32]{0:T(128)} %param.5) | copy-start | bytes 388
  0.0 7.5 %collective-permute-start = (f32[16,256]{1,0:T(8,128)}, f32[16,256]{1,0:T(8,128)S(1)}, u32[]{:S(2)}, u32[]{:S(2)}) collective-permute-start(f32[16,256]{1,0:T(8,128)} %refs_0_.3), channel_id=1, source_target_pairs={{0,1},{1,0},{2,3},{3,2},{4,5},{5,4},{6,7},{7,6},{8,9},{9,8},{10,11... | collective-permute-start | bytes 49160 | tf_op jit(solution)/shard_map/ppermute | solution.py:371
  6.0 1.2 %copy-start = (f32[256,1024]{1,0:T(8,128)S(1)}, f32[256,1024]{1,0:T(8,128)}, u32[]{:S(2)}) copy-start(f32[256,1024]{1,0:T(8,128)} %refs_5_.1) | copy-start | bytes 3145732
  7.2 0.7 %copy-start.2 = (f32[16,256]{1,0:T(8,128)S(1)}, f32[16,256]{1,0:T(8,128)}, u32[]{:S(2)}) copy-start(f32[16,256]{1,0:T(8,128)} %refs_0_.3) | copy-start | bytes 49156
  9.8 2.3 %collective-permute-start.1 = (f32[64,1152]{1,0:T(8,128)S(1)}, f32[64,1152]{1,0:T(8,128)S(1)}, u32[]{:S(2)}, u32[]{:S(2)}) collective-permute-start(f32[64,1152]{1,0:T(8,128)S(1)} %get-tuple-element.42.refs_0_), channel_id=1, source_target_pairs={{0,2},{2,0},{4,6},{6,4},{8,10},{10,8},{12,14},{14,12},{16,18},{18,... | collective-permute-start | bytes 884744 | tf_op jit(solution)/shard_map/ppermute | solution.py:377
  13.0 7.4 %collective-permute-start.4 = (f32[56,1152]{1,0:T(8,128)S(1)}, f32[56,1152]{1,0:T(8,128)S(1)}, u32[]{:S(2)}, u32[]{:S(2)}) collective-permute-start(f32[56,1152]{1,0:T(8,128)S(1)} %get-tuple-element.45.refs_1_.refs_0_), channel_id=1, source_target_pairs={{0,16},{2,6},{4,20},{6,2},{8,24},{10,14},{12,28},{14,10},{16,0},{1... | collective-permute-start | bytes 774152 | tf_op jit(solution)/shard_map/ppermute | solution.py:343
  13.8 5.0 %collective-permute-start.2 = (f32[8,1152]{1,0:T(8,128)S(1)}, f32[8,1152]{1,0:T(8,128)S(1)}, u32[]{:S(2)}, u32[]{:S(2)}) collective-permute-start(f32[8,1152]{1,0:T(8,128)S(1)} %get-tuple-element.44.refs_0_), channel_id=1, source_target_pairs={{0,16},{2,6},{4,20},{6,2},{8,24},{10,14},{12,28},{14,10},{16,0},{1... | collective-permute-start | bytes 110600 | tf_op jit(solution)/shard_map/ppermute | solution.py:343
  19.0 3.7 %collective-permute-start.3 = (f32[16,1280]{1,0:T(8,128)S(1)}, f32[16,1280]{1,0:T(8,128)S(1)}, u32[]{:S(2)}, u32[]{:S(2)}) collective-permute-start(f32[16,1280]{1,0:T(8,128)S(1)} %shard_map.41.refs_1_), channel_id=1, source_target_pairs={{0,2},{2,0},{4,68},{6,10},{8,72},{10,6},{12,14},{14,12},{16,18},{1... | collective-permute-start | bytes 245768 | tf_op jit(solution)/shard_map/ppermute | solution.py:343
  23.0 7.1 %collective-permute-start.5 = (f32[32,1152]{1,0:T(8,128)S(1)}, f32[32,1152]{1,0:T(8,128)S(1)}, u32[]{:S(2)}, u32[]{:S(2)}) collective-permute-start(f32[32,1152]{1,0:T(8,128)S(1)} %get-tuple-element.47.refs_2_), channel_id=1, source_target_pairs={{0,6},{1,7},{2,3},{3,2},{4,68},{5,69},{6,0},{7,1},{8,72},{9,73},{1... | collective-permute-start | bytes 442376 | tf_op jit(solution)/shard_map/ppermute | solution.py:385
  30.6 7.9 %copy-start.1 = (f32[256,1024]{1,0:T(8,128)S(1)}, f32[256,1024]{1,0:T(8,128)}, u32[]{:S(2)}) copy-start(f32[256,1024]{1,0:T(8,128)} %refs_5_.1) | copy-start | bytes 3145732
  30.9 5.0 %collective-permute-start.7 = (f32[56,1024]{1,0:T(8,128)S(1)}, f32[56,1024]{1,0:T(8,128)S(1)}, u32[]{:S(2)}, u32[]{:S(2)}) collective-permute-start(f32[56,1024]{1,0:T(8,128)S(1)} %get-tuple-element.57.refs_2_), channel_id=1, source_target_pairs={{0,16},{2,6},{4,20},{6,2},{8,24},{10,14},{12,28},{14,10},{16,0},{1... | collective-permute-start | bytes 688136 | tf_op jit(solution)/shard_map/ppermute | solution.py:343
  31.0 3.4 %collective-permute-start.6 = (f32[16,1024]{1,0:T(8,128)S(1)}, f32[16,1024]{1,0:T(8,128)S(1)}, u32[]{:S(2)}, u32[]{:S(2)}) collective-permute-start(f32[16,1024]{1,0:T(8,128)S(1)} %get-tuple-element.51.refs_2_), channel_id=1, source_target_pairs={{0,2},{2,0},{4,68},{6,10},{8,72},{10,6},{12,14},{14,12},{16,18},{1... | collective-permute-start | bytes 196616 | tf_op jit(solution)/shard_map/ppermute | solution.py:343
  34.6 3.1 %collective-permute-start.8 = (f32[8,1024]{1,0:T(8,128)S(1)}, f32[8,1024]{1,0:T(8,128)S(1)}, u32[]{:S(2)}, u32[]{:S(2)}) collective-permute-start(f32[8,1024]{1,0:T(8,128)S(1)} %get-tuple-element.61.refs_4_), channel_id=1, source_target_pairs={{0,16},{2,6},{4,20},{6,2},{8,24},{10,14},{12,28},{14,10},{16,0},{1... | collective-permute-start | bytes 98312 | tf_op jit(solution)/shard_map/ppermute | solution.py:396
  37.8 1.8 %collective-permute-start.9 = (f32[64,1024]{1,0:T(8,128)S(1)}, f32[64,1024]{1,0:T(8,128)S(1)}, u32[]{:S(2)}, u32[]{:S(2)}) collective-permute-start(f32[64,1024]{1,0:T(8,128)S(1)} %get-tuple-element.63), channel_id=1, source_target_pairs={{0,2},{2,0},{4,6},{6,4},{8,10},{10,8},{12,14},{14,12},{16,18},{18,... | collective-permute-start | bytes 786440 | tf_op jit(solution)/shard_map/ppermute | solution.py:399

commit v6 on v5

--- a/solution.py
+++ b/solution.py
@@ -71,15 +71,14 @@
     return one(ah, bh) + (one(ah, bl) + one(al, bh))
 
 
-def ready_kernel(x_ref, start_ref, high_ref, low_ref, column_ref):
-    high_ref[...], low_ref[...] = split(x_ref[...])
+def ready_kernel(start_ref, column_ref):
     square = (SWEEPS, SWEEPS)
     row = start_ref[...].astype(jnp.float32)
     column = jnp.sum(jnp.where(lane_of(square) == row_of(square), row, 0.0), axis=1, keepdims=True)
     column_ref[...] = jnp.broadcast_to(column, (SWEEPS, LANES))
 
 
-def factor_kernel(own_ref, other_ref, start_ref, high_ref, low_ref, msg_ref, inner_ref, edge_ref, solved_ref):
+def factor_kernel(own_ref, other_ref, start_ref, observe_ref, coef_ref, inner_ref, edge_ref, solved_ref):
     first = lax.axis_index("cols") == 0
     own, other = own_ref[...], other_ref[...]
     r = jnp.concatenate([jnp.where(first, own, other), jnp.where(first, other, own)], axis=0)
@@ -90,7 +89,7 @@
     zero = jnp.zeros_like(r)
     inner = jnp.concatenate(parts[1:4], axis=0)
     edge = jnp.concatenate([parts[0], parts[4]], axis=0)
-    left = jnp.concatenate([inner, zero, edge], axis=0)
+    left = jnp.concatenate([inner, edge], axis=0)
     right = jnp.concatenate([inner, zero, edge, zero, zero], axis=0)
     gram = dot3(left, right, ((1,), (1,)))
     earlier = (lane_of(gram.shape) & (SWEEPS - 1)) < (row_of(gram.shape) & (SWEEPS - 1))
@@ -112,18 +111,24 @@
                         total = total - lower[at : at + 8, column : column + 1] * source[m]
                 blocks[k][q] = total
     solved = jnp.concatenate([blocks[k][q] for k in range(3) for q in range(4)] + [jnp.zeros((32, rhs.shape[1]), jnp.float32)], axis=0)
-    back = dot3(gram[LANES : LANES + 64, 0:LANES], solved)
+    back = dot3(gram[count : count + 64, 0:LANES], solved)
     observe = edge - back[:, 0:rows]
-    couple = back[:, rows:] - gram[LANES : LANES + 64, LANES : 2 * LANES]
+    couple = back[:, rows:] - gram[count : count + 64, LANES : 2 * LANES]
     squares = jnp.sum(edge * edge, axis=1, keepdims=True)
     coef = jnp.where(lane_of(couple.shape) == 64, squares, couple)
     inner_ref[...] = inner
     edge_ref[...] = edge
     solved_ref[...] = solved[0:count]
-    upper, lower = split(observe)
-    both = jnp.dot(jnp.concatenate([upper, lower], axis=0), high_ref[...], preferred_element_type=jnp.float32)
-    rest = jnp.dot(upper, low_ref[...], preferred_element_type=jnp.float32)
-    msg_ref[...] = jnp.concatenate([both[0:64] + (both[64:128] + rest), coef], axis=1)
+    observe_ref[...] = observe
+    coef_ref[...] = coef
+
+
+def project_kernel(observe_ref, coef_ref, x_ref, msg_ref):
+    upper, lower = split(observe_ref[...])
+    high, low = split(x_ref[...])
+    both = jnp.dot(jnp.concatenate([upper, lower], axis=0), high, preferred_element_type=jnp.float32)
+    rest = jnp.dot(upper, low, preferred_element_type=jnp.float32)
+    msg_ref[...] = jnp.concatenate([both[0:64] + (both[64:128] + rest), coef_ref[...]], axis=1)
 
 
 def to_low(tile):
@@ -311,10 +316,10 @@
         keep_ref[below] = jnp.where(even, e, o)
 
 
-def inner_kernel(inner_ref, edge_ref, solved_ref, high_ref, low_ref, x_ref, y_ref, lhs_ref):
+def inner_kernel(inner_ref, edge_ref, solved_ref, x_ref, y_ref, lhs_ref):
     rows = x_ref.shape[0]
     inner = inner_ref[...]
-    part = dot3(solved_ref[:, 0:rows], (high_ref[...], low_ref[...]))
+    part = dot3(solved_ref[:, 0:rows], x_ref[...])
     y_ref[...] = x_ref[...] - dot3(inner, part, ((0,), (0,)))
     edge = edge_ref[...] - dot(solved_ref[:, rows : rows + 64], inner, ((0,), (0,)))
     high = edge.astype(jnp.bfloat16).astype(jnp.float32)
@@ -369,11 +374,14 @@
         (2 * i + c, 2 * i + 1 - c if j is None else 2 * j + c) for i, j in swap(next_quad) for c in range(2)
     ]
     other = lax.ppermute(reflectors, "cols", [(0, 1), (1, 0)])
-    half = jax.ShapeDtypeStruct(eigvecs.shape, jnp.bfloat16)
-    high, low, start = call(ready_kernel, [half, half, (SWEEPS, LANES)], eigvecs, starts[None, :], flops=20_000_000)
-    msg, inner, edge, solved = call(
-        factor_kernel, [(64, wide), (96, rows), (64, rows), (96, rows + LANES)], reflectors, other, start, high, low
+    (start,) = call(ready_kernel, [(SWEEPS, LANES)], starts[None, :], flops=20_000_000)
+    observe, coef, inner, edge, solved = call(
+        factor_kernel,
+        [(64, rows), (64, LANES), (96, rows), (64, rows), (96, rows + LANES)],
+        reflectors, other, start,
+        flops=2_000_000_000,
     )
+    (msg,) = call(project_kernel, [(64, wide)], observe, coef, eigvecs)
     got = lax.ppermute(msg, "rows", on_chip)
     mid, first, rest = call(merge_kernel, [(32, wide), (8, wide), (56, wide)], msg, got, where=is_north)
     got_first = trade(first, in_pair)
@@ -386,7 +394,7 @@
     last, p = call(late_kernel, [(8, wide), (16, wide)], rest, got_rest, pair, where=is_inside)
     partial, lhs = call(
         inner_kernel, [(rows, cols), jax.ShapeDtypeStruct((rows, 256), jnp.bfloat16)],
-        inner, edge, solved, high, low, eigvecs, flops=20_000_000,
+        inner, edge, solved, eigvecs, flops=20_000_000,
     )
     w, rest = call(w_kernel, [(32, cols), (16, cols)], got, start, w, p, p0, where=is_inside)
     most, tail = call(e0_kernel, [(56, cols), (8, cols)], pair, last, w, p0, where=is_inside)
@@ -402,7 +410,7 @@
         out_shape=jax.ShapeDtypeStruct((rows, cols), jnp.float32),
         in_specs=[pl.BlockSpec(memory_space=pltpu.VMEM)] * 4,
         out_specs=pl.BlockSpec(memory_space=pl.ANY),
-        scratch_shapes=[pltpu.VMEM((4, rows, cols // 4), jnp.float32), pltpu.SemaphoreType.DMA((4,))],
+        scratch_shapes=[pltpu.VMEM((2, rows, cols // 2), jnp.float32), pltpu.SemaphoreType.DMA((2,))],
         compiler_params=pltpu.CompilerParams(vmem_limit_bytes=16 * 1024 * 1024),
     )(lhs, keep, got, partial)
 

time: 41 us -> 40.9 us (level)
  local copies, waits for them, and re-layouts: 1.66 us -> 0.01 us
  waiting for transfers between devices: 16.6 us -> 17.8 us
  starting transfers between devices: 14.4 us -> 15 us
    unnamed x8 -> x6, local copies, waits for them, and re-layouts: 1.66 us -> 0.01 us
    ppermute x1, waiting for transfers between devices: 0.01 us -> 1.25 us  [per_device(): other = lax.ppermute(reflectors, 'cols', [(0, 1), (1, 0)])]
    ppermute x2, starting transfers between devices: 1.66 us -> 2.25 us  [per_device(): got = lax.ppermute(msg, 'rows', on_chip)]
    pallas_call x13 -> x14, Pallas kernels: 6.82 us -> 6.67 us  [call(): pl.pallas_call(body, out_shape=[jax.ShapeDtypeStruct(s, jnp.float32) if i...]
  transfers between devices with their start and end apart: 10 -> 10, of which waited for: 8 -> 9; matrix products, arithmetic and copies ran while one was open for 0% -> 0% of each run, Pallas kernels for 7% -> 7%
where the time goes in v6:
time: 40.9 us; the launch traced here: 40.8 us
  waiting for transfers between devices  17.8 us (44%)
  starting transfers between devices  15 us (37%)
  Pallas kernels  7.89 us (19%)
    ppermute x5, waiting for transfers between devices, trade(): return lax.ppermute(array, 'rows', pairs)  10.5 us
    pallas_call x14, Pallas kernels, call(): pl.pallas_call(body, out_shape=[jax.ShapeDtypeStruct(s, jnp.float32) if i...  6.67 us
    ppermute x1, starting transfers between devices, per_device(): other = lax.ppermute(reflectors, 'cols', [(0, 1), (1, 0)])  6.01 us
    ppermute x1, starting transfers between devices, per_device(): got = lax.ppermute(w, ('rows', 'cols'), w_pairs)  3.51 us
    ppermute x1, waiting for transfers between devices, per_device(): got = lax.ppermute(w, ('rows', 'cols'), w_pairs)  3.25 us
    ppermute x5, starting transfers between devices, trade(): return lax.ppermute(array, 'rows', pairs)  3.16 us
    ppermute x2, starting transfers between devices, per_device(): got = lax.ppermute(msg, 'rows', on_chip)  2.25 us
    ppermute x1, waiting for transfers between devices, per_device(): got = lax.ppermute(tail, 'rows', in_pair)  1.5 us
  transfers between devices with their start and end apart: 10, of which 9 were waited for; matrix products, arithmetic and copies ran while one was open for 0% of the time, Pallas kernels for 7%

profile of v6, /device:TPU:41, one launch (start us, length us, event | category | flops | bytes accessed | tf_op | source)
XLA Modules:
  0.0 40.8 jit_solution(16612485526727278246)
XLA Ops:
  0.0 0.0 copy-start.2
  0.0 6.0 %collective-permute-start = (f32[16,256]{1,0:T(8,128)}, f32[16,256]{1,0:T(8,128)S(1)}, u32[]{:S(2)}, u32[]{:S(2)}) collective-permute-start(f32[16,256]{1,0:T(8,128)} %refs_0_.1), channel_id=1, source_target_pairs={{0,1},{1,0},{2,3},{3,2},{4,5},{5,4},{6,7},{7,6},{8,9},{9,8},{10,11... | collective-permute-start | bytes 49160 | tf_op jit(solution)/shard_map/ppermute | solution.py:376
  6.0 0.0 copy-done.2
  6.0 0.0 copy-start.1
  6.0 0.1 shard_map.37.refs_2_.refs_1_
  6.1 0.0 copy-start
  6.1 1.2 %collective-permute-done.refs_1_ = f32[16,256]{1,0:T(8,128)S(1)} collective-permute-done((f32[16,256]{1,0:T(8,128)}, f32[16,256]{1,0:T(8,128)S(1)}, u32[]{:S(2)}, u32[]{:S(2)}) %collective-permute-start) | collective-permute-done | bytes 16416 | tf_op jit(solution)/shard_map/ppermute | solution.py:376
  7.3 0.0 copy-done.1
  7.4 1.6 %shard_map.38 = (f32[64,256]{1,0:T(8,128)S(1)}, f32[64,128]{1,0:T(8,128)S(1)}, f32[96,256]{1,0:T(8,128)S(1)}, f32[64,256]{1,0:T(8,128)S(1)}, f32[96,384]{1,0:T(8,128)S(1)}) custom-call(f32[16,256]{1,0:T(8,128)S(1)} %copy-done.1, f32[16,256]{1,0:T(8,128)S(1)} %collective-permute-done.refs_1_, f32[32,128]{1,0:T(8,128)S(1)} %shard_map.37.refs_2_.refs_1_), custom_call_target="tpu_custom_call" | custom-call | flops 2000000000 | bytes 49152 | tf_op jit(solution)/shard_map/pallas_call | solution.py:36
  8.9 0.0 copy-done
  8.9 0.3 shard_map.40.refs_0_
  9.2 1.6 %collective-permute-start.1 = (f32[64,1152]{1,0:T(8,128)S(1)}, f32[64,1152]{1,0:T(8,128)S(1)}, u32[]{:S(2)}, u32[]{:S(2)}) collective-permute-start(f32[64,1152]{1,0:T(8,128)S(1)} %shard_map.40.refs_0_), channel_id=1, source_target_pairs={{0,2},{2,0},{4,6},{6,4},{8,10},{10,8},{12,14},{14,12},{16,18},{18,... | collective-permute-start | bytes 884744 | tf_op jit(solution)/shard_map/ppermute | solution.py:385
  10.9 1.2 %collective-permute-done.1.refs_1_ = f32[64,1152]{1,0:T(8,128)S(1)} collective-permute-done((f32[64,1152]{1,0:T(8,128)S(1)}, f32[64,1152]{1,0:T(8,128)S(1)}, u32[]{:S(2)}, u32[]{:S(2)}) %collective-permute-start.1) | collective-permute-done | bytes 294944 | tf_op jit(solution)/shard_map/ppermute | solution.py:385
  12.1 0.9 %shard_map.41 = (f32[32,1152]{1,0:T(8,128)S(1)}, f32[8,1152]{1,0:T(8,128)S(1)}, f32[56,1152]{1,0:T(8,128)S(1)}) custom-call(f32[64,1152]{1,0:T(8,128)S(1)} %shard_map.40.refs_0_, f32[64,1152]{1,0:T(8,128)S(1)} %collective-permute-done.1.refs_1_), custom_call_target="tpu_custom_call" | custom-call | flops 1000000 | bytes 589824 | tf_op jit(solution)/shard_map/pallas_call | solution.py:36
  13.0 0.8 %collective-permute-start.4 = (f32[56,1152]{1,0:T(8,128)S(1)}, f32[56,1152]{1,0:T(8,128)S(1)}, u32[]{:S(2)}, u32[]{:S(2)}) collective-permute-start(f32[56,1152]{1,0:T(8,128)S(1)} %get-tuple-element.41.refs_1_.refs_0_), channel_id=1, source_target_pairs={{0,16},{2,6},{4,20},{6,2},{8,24},{10,14},{12,28},{14,10},{16,0},{1... | collective-permute-start | bytes 774152 | tf_op jit(solution)/shard_map/ppermute | solution.py:348
  13.8 0.7 %collective-permute-start.2 = (f32[8,1152]{1,0:T(8,128)S(1)}, f32[8,1152]{1,0:T(8,128)S(1)}, u32[]{:S(2)}, u32[]{:S(2)}) collective-permute-start(f32[8,1152]{1,0:T(8,128)S(1)} %get-tuple-element.40.refs_0_), channel_id=1, source_target_pairs={{0,16},{2,6},{4,20},{6,2},{8,24},{10,14},{12,28},{14,10},{16,0},{1... | collective-permute-start | bytes 110600 | tf_op jit(solution)/shard_map/ppermute | solution.py:348
  14.6 4.2 %collective-permute-done.2.refs_2_ = f32[8,1152]{1,0:T(8,128)S(1)} collective-permute-done((f32[8,1152]{1,0:T(8,128)S(1)}, f32[8,1152]{1,0:T(8,128)S(1)}, u32[]{:S(2)}, u32[]{:S(2)}) %collective-permute-start.2) | collective-permute-done | bytes 36896 | tf_op jit(solution)/shard_map/ppermute | solution.py:348
  18.8 0.2 shard_map.42.refs_1_
  19.0 1.4 %collective-permute-start.3 = (f32[16,1280]{1,0:T(8,128)S(1)}, f32[16,1280]{1,0:T(8,128)S(1)}, u32[]{:S(2)}, u32[]{:S(2)}) collective-permute-start(f32[16,1280]{1,0:T(8,128)S(1)} %shard_map.42.refs_1_), channel_id=1, source_target_pairs={{0,2},{2,0},{4,68},{6,10},{8,72},{10,6},{12,14},{14,12},{16,18},{1... | collective-permute-start | bytes 245768 | tf_op jit(solution)/shard_map/ppermute | solution.py:348
  20.4 0.0 collective-permute-done.4.refs_3_.refs_1_
  20.4 0.4 %shard_map.43 = (f32[24,1152]{1,0:T(8,128)S(1)}, f32[32,1152]{1,0:T(8,128)S(1)}) custom-call(f32[8,1152]{1,0:T(8,128)S(1)} %get-tuple-element.40.refs_0_, f32[56,1152]{1,0:T(8,128)S(1)} %get-tuple-element.41.refs_1_.refs_0_, f32[8,1152]{1,0:T(8,128)S(1)} %collective-permute-done.2.refs_2_, f32[56,1152]{1,0:T(8,128)S(1)} %collective-permute-done.4.refs_3_.refs_1_), custom_call_target="tpu_custom_call" | custom-call | flops 1000000 | bytes 589824 | tf_op jit(solution)/shard_map/pallas_call | solution.py:36
  20.9 1.8 %collective-permute-done.3.refs_0_ = f32[16,1280]{1,0:T(8,128)S(1)} collective-permute-done((f32[16,1280]{1,0:T(8,128)S(1)}, f32[16,1280]{1,0:T(8,128)S(1)}, u32[]{:S(2)}, u32[]{:S(2)}) %collective-permute-start.3) | collective-permute-done | bytes 81952 | tf_op jit(solution)/shard_map/ppermute | solution.py:348
  22.7 0.3 shard_map.44
  23.0 3.5 %collective-permute-start.5 = (f32[32,1152]{1,0:T(8,128)S(1)}, f32[32,1152]{1,0:T(8,128)S(1)}, u32[]{:S(2)}, u32[]{:S(2)}) collective-permute-start(f32[32,1152]{1,0:T(8,128)S(1)} %get-tuple-element.43.refs_2_), channel_id=1, source_target_pairs={{0,6},{1,7},{2,3},{3,2},{4,68},{5,69},{6,0},{7,1},{8,72},{9,73},{1... | collective-permute-start | bytes 442376 | tf_op jit(solution)/shard_map/ppermute | solution.py:393
  26.5 0.3 shard_map.45
  26.8 3.2 %collective-permute-done.5.refs_0_ = f32[32,1152]{1,0:T(8,128)S(1)} collective-permute-done((f32[32,1152]{1,0:T(8,128)S(1)}, f32[32,1152]{1,0:T(8,128)S(1)}, u32[]{:S(2)}, u32[]{:S(2)}) %collective-permute-start.5) | collective-permute-done | bytes 147488 | tf_op jit(solution)/shard_map/ppermute | solution.py:393
  30.1 0.5 %shard_map.46 = (f32[32,1024]{1,0:T(8,128)S(1)}, f32[16,1024]{1,0:T(8,128)S(1)}) custom-call(f32[32,1152]{1,0:T(8,128)S(1)} %collective-permute-done.5.refs_0_, f32[32,128]{1,0:T(8,128)S(1)} %shard_map.37.refs_2_.refs_1_, f32[32,1152]{1,0:T(8,128)S(1)} %get-tuple-element.43.refs_2_, f32[16,1152]{1,0:T(8,128)S(1)} %get-tuple-element.45.refs_3_, ...), custom_call_target="tpu_custom_call" | custom-call | flops 1000000 | bytes 450560 | tf_op jit(solution)/shard_map/pallas_call | solution.py:36
  30.6 0.3 shard_map.47
  30.9 0.1 collective-permute-start.7
  31.0 0.1 collective-permute-start.6
  31.1 3.3 %collective-permute-done.6.refs_0_ = f32[16,1024]{1,0:T(8,128)S(1)} collective-permute-done((f32[16,1024]{1,0:T(8,128)S(1)}, f32[16,1024]{1,0:T(8,128)S(1)}, u32[]{:S(2)}, u32[]{:S(2)}) %collective-permute-start.6) | collective-permute-done | bytes 65568 | tf_op jit(solution)/shard_map/ppermute | solution.py:348
  34.4 0.2 shard_map.48
  34.6 0.1 collective-permute-start.8
  34.7 1.1 %collective-permute-done.7.refs_3_ = f32[56,1024]{1,0:T(8,128)S(1)} collective-permute-done((f32[56,1024]{1,0:T(8,128)S(1)}, f32[56,1024]{1,0:T(8,128)S(1)}, u32[]{:S(2)}, u32[]{:S(2)}) %collective-permute-start.7) | collective-permute-done | bytes 229408 | tf_op jit(solution)/shard_map/ppermute | solution.py:348
  35.8 0.4 shard_map.49
  36.3 1.5 %collective-permute-done.8.refs_5_ = f32[8,1024]{1,0:T(8,128)S(1)} collective-permute-done((f32[8,1024]{1,0:T(8,128)S(1)}, f32[8,1024]{1,0:T(8,128)S(1)}, u32[]{:S(2)}, u32[]{:S(2)}) %collective-permute-start.8) | collective-permute-done | bytes 32800 | tf_op jit(solution)/shard_map/ppermute | solution.py:404
  37.7 0.1 shard_map.50
  37.8 0.6 %collective-permute-start.9 = (f32[64,1024]{1,0:T(8,128)S(1)}, f32[64,1024]{1,0:T(8,128)S(1)}, u32[]{:S(2)}, u32[]{:S(2)}) collective-permute-start(f32[64,1024]{1,0:T(8,128)S(1)} %get-tuple-element.59), channel_id=1, source_target_pairs={{0,2},{2,0},{4,6},{6,4},{8,10},{10,8},{12,14},{14,12},{16,18},{18,... | collective-permute-start | bytes 786440 | tf_op jit(solution)/shard_map/ppermute | solution.py:407
  38.5 1.1 %shard_map.39 = (f32[256,1024]{1,0:T(8,128)S(1)}, bf16[256,256]{1,0:T(8,128)(2,1)S(1)}) custom-call(f32[96,256]{1,0:T(8,128)S(1)} %get-tuple-element.33.refs_0_, f32[64,256]{1,0:T(8,128)S(1)} %get-tuple-element.34.refs_1_, f32[96,384]{1,0:T(8,128)S(1)} %get-tuple-element.35.refs_2_, f32[256,1024]{1,0:T(8,128)S(1)} %copy-done), custom_call_target="tpu_custom_call" | custom-call | flops 20000000 | bytes 1359872 | tf_op jit(solution)/shard_map/pallas_call | solution.py:36
  39.5 0.1 collective-permute-done.9.msg_ref
  39.6 1.2 %shard_map.51 = f32[256,1024]{1,0:T(8,128)} custom-call(bf16[256,256]{1,0:T(8,128)(2,1)S(1)} %get-tuple-element.36.lhs_ref, f32[64,1024]{1,0:T(8,128)S(1)} %get-tuple-element.58.keep_ref, f32[64,1024]{1,0:T(8,128)S(1)} %collective-permute-done.9.msg_ref, f32[256,1024]{1,0:T(8,128)S(1)} %get-tuple-element.60.y_ref), custom_call_target="tpu_custom_call" | custom-call | tf_op jit(solution)/shard_map/pallas_call | solution.py:408
Async XLA Ops:
  0.0 6.0 %copy-start.2 = (s32[32]{0:T(128)S(1)}, s32[32]{0:T(128)}, u32[]{:S(2)}) copy-start(s32[32]{0:T(128)} %param.5) | copy-start | bytes 388
  0.0 7.3 %collective-permute-start = (f32[16,256]{1,0:T(8,128)}, f32[16,256]{1,0:T(8,128)S(1)}, u32[]{:S(2)}, u32[]{:S(2)}) collective-permute-start(f32[16,256]{1,0:T(8,128)} %refs_0_.1), channel_id=1, source_target_pairs={{0,1},{1,0},{2,3},{3,2},{4,5},{5,4},{6,7},{7,6},{8,9},{9,8},{10,11... | collective-permute-start | bytes 49160 | tf_op jit(solution)/shard_map/ppermute | solution.py:376
  6.0 1.3 %copy-start.1 = (f32[16,256]{1,0:T(8,128)S(1)}, f32[16,256]{1,0:T(8,128)}, u32[]{:S(2)}) copy-start(f32[16,256]{1,0:T(8,128)} %refs_0_.1) | copy-start | bytes 49156
  6.1 2.8 %copy-start = (f32[256,1024]{1,0:T(8,128)S(1)}, f32[256,1024]{1,0:T(8,128)}, u32[]{:S(2)}) copy-start(f32[256,1024]{1,0:T(8,128)} %refs_2_.1) | copy-start | bytes 3145732
  9.2 2.8 %collective-permute-start.1 = (f32[64,1152]{1,0:T(8,128)S(1)}, f32[64,1152]{1,0:T(8,128)S(1)}, u32[]{:S(2)}, u32[]{:S(2)}) collective-permute-start(f32[64,1152]{1,0:T(8,128)S(1)} %shard_map.40.refs_0_), channel_id=1, source_target_pairs={{0,2},{2,0},{4,6},{6,4},{8,10},{10,8},{12,14},{14,12},{16,18},{18,... | collective-permute-start | bytes 884744 | tf_op jit(solution)/shard_map/ppermute | solution.py:385
  13.0 7.4 %collective-permute-start.4 = (f32[56,1152]{1,0:T(8,128)S(1)}, f32[56,1152]{1,0:T(8,128)S(1)}, u32[]{:S(2)}, u32[]{:S(2)}) collective-permute-start(f32[56,1152]{1,0:T(8,128)S(1)} %get-tuple-element.41.refs_1_.refs_0_), channel_id=1, source_target_pairs={{0,16},{2,6},{4,20},{6,2},{8,24},{10,14},{12,28},{14,10},{16,0},{1... | collective-permute-start | bytes 774152 | tf_op jit(solution)/shard_map/ppermute | solution.py:348
  13.8 5.0 %collective-permute-start.2 = (f32[8,1152]{1,0:T(8,128)S(1)}, f32[8,1152]{1,0:T(8,128)S(1)}, u32[]{:S(2)}, u32[]{:S(2)}) collective-permute-start(f32[8,1152]{1,0:T(8,128)S(1)} %get-tuple-element.40.refs_0_), channel_id=1, source_target_pairs={{0,16},{2,6},{4,20},{6,2},{8,24},{10,14},{12,28},{14,10},{16,0},{1... | collective-permute-start | bytes 110600 | tf_op jit(solution)/shard_map/ppermute | solution.py:348
  19.0 3.7 %collective-permute-start.3 = (f32[16,1280]{1,0:T(8,128)S(1)}, f32[16,1280]{1,0:T(8,128)S(1)}, u32[]{:S(2)}, u32[]{:S(2)}) collective-permute-start(f32[16,1280]{1,0:T(8,128)S(1)} %shard_map.42.refs_1_), channel_id=1, source_target_pairs={{0,2},{2,0},{4,68},{6,10},{8,72},{10,6},{12,14},{14,12},{16,18},{1... | collective-permute-start | bytes 245768 | tf_op jit(solution)/shard_map/ppermute | solution.py:348
  23.0 7.1 %collective-permute-start.5 = (f32[32,1152]{1,0:T(8,128)S(1)}, f32[32,1152]{1,0:T(8,128)S(1)}, u32[]{:S(2)}, u32[]{:S(2)}) collective-permute-start(f32[32,1152]{1,0:T(8,128)S(1)} %get-tuple-element.43.refs_2_), channel_id=1, source_target_pairs={{0,6},{1,7},{2,3},{3,2},{4,68},{5,69},{6,0},{7,1},{8,72},{9,73},{1... | collective-permute-start | bytes 442376 | tf_op jit(solution)/shard_map/ppermute | solution.py:393
  30.9 5.0 %collective-permute-start.7 = (f32[56,1024]{1,0:T(8,128)S(1)}, f32[56,1024]{1,0:T(8,128)S(1)}, u32[]{:S(2)}, u32[]{:S(2)}) collective-permute-start(f32[56,1024]{1,0:T(8,128)S(1)} %get-tuple-element.53.refs_2_), channel_id=1, source_target_pairs={{0,16},{2,6},{4,20},{6,2},{8,24},{10,14},{12,28},{14,10},{16,0},{1... | collective-permute-start | bytes 688136 | tf_op jit(solution)/shard_map/ppermute | solution.py:348
  31.0 3.4 %collective-permute-start.6 = (f32[16,1024]{1,0:T(8,128)S(1)}, f32[16,1024]{1,0:T(8,128)S(1)}, u32[]{:S(2)}, u32[]{:S(2)}) collective-permute-start(f32[16,1024]{1,0:T(8,128)S(1)} %get-tuple-element.47.refs_2_), channel_id=1, source_target_pairs={{0,2},{2,0},{4,68},{6,10},{8,72},{10,6},{12,14},{14,12},{16,18},{1... | collective-permute-start | bytes 196616 | tf_op jit(solution)/shard_map/ppermute | solution.py:348
  34.6 3.1 %collective-permute-start.8 = (f32[8,1024]{1,0:T(8,128)S(1)}, f32[8,1024]{1,0:T(8,128)S(1)}, u32[]{:S(2)}, u32[]{:S(2)}) collective-permute-start(f32[8,1024]{1,0:T(8,128)S(1)} %get-tuple-element.57.refs_4_), channel_id=1, source_target_pairs={{0,16},{2,6},{4,20},{6,2},{8,24},{10,14},{12,28},{14,10},{16,0},{1... | collective-permute-start | bytes 98312 | tf_op jit(solution)/shard_map/ppermute | solution.py:404
  37.8 1.8 %collective-permute-start.9 = (f32[64,1024]{1,0:T(8,128)S(1)}, f32[64,1024]{1,0:T(8,128)S(1)}, u32[]{:S(2)}, u32[]{:S(2)}) collective-permute-start(f32[64,1024]{1,0:T(8,128)S(1)} %get-tuple-element.59), channel_id=1, source_target_pairs={{0,2},{2,0},{4,6},{6,4},{8,10},{10,8},{12,14},{14,12},{16,18},{18,... | collective-permute-start | bytes 786440 | tf_op jit(solution)/shard_map/ppermute | solution.py:407
